TPU v7x, 32 devices: a whole 2x2x4 slice. The times are simulated.
32 devices in a mesh: img: 8 (over z, y), sp: 4 (over x, core).
Axes of the slice: x: 2, y: 2, z: 4, core: 2. Of those that a mesh axis runs over, the one named last changes fastest.
Arguments:
- patches: bfloat16 [4096, 1280], P(('img', 'sp')), parts along dimension 0, may hold values from -6 to 6
- pos_ids: int32 [2, 4096], P(None, 'img'), parts along dimension 1, may hold values from 0 to 31, as said below
- norm_gain: float32 [1280], replicated, may hold values from 0.5 to 1.5
- norm_bias: float32 [1280], replicated, may hold values from -3 to 3
- qkv_weight: bfloat16 [1280, 3, 1280], P(None, None, 'sp')
- qkv_bias: float32 [3, 1280], replicated, may hold values from -3 to 3
- proj_weight: bfloat16 [1280, 1280], P('sp'), may hold values from -0.15625 to 0.15625
- proj_bias: float32 [1280], replicated, may hold values from -3 to 3
- merge_gain: float32 [1280], replicated, may hold values from 0.5 to 1.5
- merge_bias: float32 [1280], replicated, may hold values from -3 to 3
- fc1_weight: bfloat16 [5120, 5120], P(None, 'sp'), may hold values from -0.078125 to 0.078125
- fc1_bias: float32 [5120], P('sp'), may hold values from -3 to 3
Outputs:
- vit_out: bfloat16 [4096, 1280], P(('img', 'sp')), parts along dimension 0
- merged_hidden: bfloat16 [1024, 5120], P('img', 'sp'), parts along dimension 0
There are 8 independent parts, one for each index of `img`. A program takes and returns all parts, laid end to end along the dimension named above; an argument that names none is the same for every part. Nothing has to cross between parts.
Inputs may be any that keep to these rules, and one draw needn't show every extreme that they name: pos_ids[0] and pos_ids[1] are the row and column of each patch on a grid of 2 R by 2 C patches, where the grid of 2x2 blocks has R rows and C columns, R C = 128, and one of R and C equals min(8, 128); each aligned run of 4 patches is one 2x2 block in row-major order inside it; every block of the grid appears once, in the order that the argument gives.
All inputs are finite; a program needn't handle non-finite values.
Results may differ from a plain program's by a relative error of at most 0.006.
Values may be sent and summed in bfloat16 or wider, within the bound.
No kernel may reach another device: no remote copies, remote signals or barrier semaphores. Data moves between devices by JAX's collectives and lax.ppermute only.
A program may use at most 64 MiB of HBM per device.

v0:
```python
import jax
import jax.numpy as jnp
from jax import lax
from jax.sharding import PartitionSpec as P

HEADS = 16


def layer_norm(values, gain, bias):
    mean = jnp.mean(values, axis=-1, keepdims=True)
    centered = values - mean
    var = jnp.mean(centered * centered, axis=-1, keepdims=True)
    return centered * lax.rsqrt(var + 1e-06) * gain + bias


def rotate(values, positions, nheads):
    count = values.shape[0]
    hdim = values.shape[1] // nheads
    quarter = hdim // 4
    inv = 1.0 / 10000.0 ** (jnp.arange(quarter, dtype=jnp.float32) * 2.0 / (hdim // 2))
    rows = positions[0].astype(jnp.float32)[:, None] * inv
    cols = positions[1].astype(jnp.float32)[:, None] * inv
    angle = jnp.concatenate([rows, cols, rows, cols], axis=1)
    cosine = jnp.cos(angle)[:, None, :]
    sine = jnp.sin(angle)[:, None, :]
    shaped = values.reshape(count, nheads, hdim)
    half = hdim // 2
    turned = jnp.concatenate([-shaped[..., half:], shaped[..., :half]], axis=-1)
    return (shaped * cosine + turned * sine).reshape(count, nheads * hdim)


def attend(query, keys, value, nheads, hdim):
    count = query.shape[0]
    block = min(512, count)
    qblocks = query.reshape(count // block, block, nheads, hdim)
    kshaped = keys.reshape(count, nheads, hdim)
    vshaped = value.reshape(count, nheads, hdim)
    scale = 1.0 / jnp.sqrt(jnp.float32(hdim))

    def one_block(qpart):
        scores = (
            jnp.einsum("bhd,khd->hbk", qpart, kshaped, preferred_element_type=jnp.float32) * scale
        )
        top = jnp.max(scores, axis=-1, keepdims=True)
        expo = jnp.exp(scores - top)
        weights = (expo / jnp.sum(expo, axis=-1, keepdims=True)).astype(jnp.bfloat16)
        result = jnp.einsum("hbk,khd->bhd", weights, vshaped, preferred_element_type=jnp.float32)
        return result.astype(jnp.bfloat16).reshape(block, nheads * hdim)

    return lax.map(one_block, qblocks).reshape(count, nheads * hdim)


def per_device(
    patches,
    pos_ids,
    norm_gain,
    norm_bias,
    qkv_weight,
    qkv_bias,
    proj_weight,
    proj_bias,
    merge_gain,
    merge_bias,
    fc1_weight,
    fc1_bias,
):
    groups = lax.axis_size("sp")
    where = lax.axis_index("sp")
    prow = patches.shape[0]
    width = patches.shape[1]
    heads_local = HEADS // groups
    hdim = width // HEADS
    local_width = width // groups
    xfloat = patches.astype(jnp.float32)
    normed = layer_norm(xfloat, norm_gain, norm_bias).astype(jnp.bfloat16)
    bias_local = lax.dynamic_slice_in_dim(qkv_bias, where * local_width, local_width, 1)
    qkv = (
        jnp.einsum(
            "pd,dcn->pcn",
            lax.all_gather(normed, "sp", axis=0, tiled=True),
            qkv_weight,
            preferred_element_type=jnp.float32,
        )
        + bias_local[None]
    )
    query = rotate(qkv[:, 0], pos_ids, heads_local).astype(jnp.bfloat16)
    keys = rotate(qkv[:, 1], pos_ids, heads_local).astype(jnp.bfloat16)
    value = qkv[:, 2].astype(jnp.bfloat16)
    spread = jnp.stack([query, keys, value])
    attended = attend(spread[0], spread[1], spread[2], heads_local, hdim)
    returned = lax.all_to_all(attended, "sp", split_axis=0, concat_axis=1, tiled=True)
    projected = jnp.dot(
        returned,
        lax.all_gather(proj_weight, "sp", axis=0, tiled=True),
        preferred_element_type=jnp.float32,
    )
    vit_out = (xfloat + projected + proj_bias).astype(jnp.bfloat16)
    zn = layer_norm(vit_out.astype(jnp.float32), merge_gain, merge_bias).astype(jnp.bfloat16)
    blocks = zn.reshape(prow // 4, 4 * width)
    hidden = (
        jnp.dot(
            lax.all_gather(blocks, "sp", axis=0, tiled=True),
            fc1_weight,
            preferred_element_type=jnp.float32,
        )
        + fc1_bias
    )
    merged_hidden = jax.nn.gelu(hidden, approximate=False).astype(jnp.bfloat16)
    return (vit_out, merged_hidden)


def solution(mesh):
    return jax.shard_map(
        per_device,
        mesh=mesh,
        in_specs=(
            P(("img", "sp"), None),
            P(None, "img"),
            P(),
            P(),
            P(None, None, "sp"),
            P(),
            P("sp", None),
            P(),
            P(),
            P(),
            P(None, "sp"),
            P("sp"),
        ),
        out_specs=(P(("img", "sp"), None), P("img", "sp")),
        check_vma=False,
    )
```

profile of v0, /device:TPU:0, one launch (start us, length us, event | category | flops | bytes accessed | tf_op | source)
XLA Modules:
  0.0 105.2 jit_solution(13298240738997939612)
XLA Ops:
  7.2 0.0 copy-start
  7.2 0.0 all-gather.4.cloned.1.call-start
  7.2 1.2 %convert_reduce_fusion = f32[128]{0:T(128)S(1)} fusion(bf16[128,1280]{1,0:T(8,128)(2,1)} %param.12), kind=kLoop, calls=%fused_computation.17 | loop fusion | flops 327552 | bytes 328192 | tf_op jit(solution)/shard_map/reduce_sum | solution.py:10
  8.5 1.2 %fusion.15 = f32[128]{0:T(128)S(1)} fusion(bf16[128,1280]{1,0:T(8,128)(2,1)} %param.12, f32[128]{0:T(128)S(1)} %broadcast_multiply_fusion.3), kind=kLoop, calls=%fused_computation.24 | loop fusion | flops 655232 | bytes 328704 | tf_op jit(solution)/shard_map/reduce_sum | solution.py:12
  9.7 2.0 %fusion.18 = bf16[128,1280]{1,0:T(8,128)(2,1)} fusion(bf16[128,1280]{1,0:T(8,128)(2,1)} %param.12, f32[1280]{0:T(1024)} %param.15, f32[1280]{0:T(1024)} %param.14, f32[128]{0:T(128)S(1)} %add_rsqrt_fusion.1, f32[128]{0:T(128)S(1)} %broadcast_multiply_fusion.3), kind=kLoop, calls=%fused_computation.27 | loop fusion | flops 983040 | bytes 666624 | tf_op jit(solution)/shard_map/convert_element_type | solution.py:75
  11.7 0.0 all-gather.4.cloned.1.call-update
  11.7 0.0 all-gather.6.cloned.1.call-start
  11.8 0.7 all-gather.6.cloned.1.call-update
  12.5 0.0 all-gather.8.cloned.1.call-start
  12.5 0.8 constant_dynamic-slice_fusion
  13.3 0.8 slice_convert_fusion.2
  14.1 0.1 broadcast_multiply_fusion.1
  14.2 0.6 fusion.40
  14.7 18.0 %all-gather.4.cloned.1.call-done = bf16[512,1280]{1,0:T(8,128)(2,1)} async-done(((bf16[128,1280]{1,0:T(8,128)(2,1)}), bf16[512,1280]{1,0:T(8,128)(2,1)}) %all-gather.4.cloned.1.call-update) | async-done | bytes 1310736 | tf_op jit(solution)/shard_map/all_gather | solution.py:80
  32.8 0.0 copy-done
  32.8 2.8 %convolution_add_fusion.2 = f32[512,3,320]{0,2,1:T(8,128)S(1)} fusion(bf16[1280,3,320]{0,2,1:T(8,128)(2,1)S(1)} %copy-done, bf16[512,1280]{1,0:T(8,128)(2,1)} %all-gather.4.cloned.1.call-done, f32[3,320]{1,0:T(4,128)S(1)} %constant_dynamic-slice_fusion), kind=kOutput, calls=%fused_computation.11 | convolution fusion | flops 1258782720 | bytes 5738240 | tf_op jit(solution)/shard_map/pd,dcn->pcn/dot_general | solution.py:78
  35.5 0.8 slice.51
  36.3 0.1 fusion.42
  36.4 0.1 slice_negate_fusion
  36.6 0.4 fusion.29
  36.9 0.0 copy-start.3
  37.0 3.4 %fusion.43 = (f32[4,512]{1,0:T(4,128)S(1)}, f32[4,512,512]{1,2,0:T(8,128)}) fusion(bf16[512,4,80]{0,2,1:T(8,128)(2,1)S(1)} %get-tuple-element.24, bf16[512,4,80]{0,2,1:T(8,128)(2,1)S(1)} %get-tuple-element.23), kind=kOutput, calls=%fused_computation.75 | convolution fusion | flops 170918400 | bytes 4857856 | tf_op jit(solution)/shard_map/while/body/eval_jaxpr/sub | solution.py:45
  40.4 0.0 copy-done.3
  40.4 0.0 copy-start.1
  40.4 0.0 copy-start.4
  40.4 3.1 %fusion.10 = bf16[512,4,80]{0,2,1:T(8,128)(2,1)S(1)} fusion(bf16[512,4,80]{0,2,1:T(8,128)(2,1)S(1)} %bitcast.30, f32[4,512,512]{1,2,0:T(8,128)} %get-tuple-element.32, f32[4,512]{1,0:T(4,128)S(1)} %get-tuple-element.31), kind=kOutput, calls=%fused_computation.14 | convolution fusion | flops 170033152 | bytes 4857856 | tf_op jit(solution)/shard_map/while/body/eval_jaxpr/hbk,khd->bhd/dot_general | solution.py:47
  43.5 0.0 copy-start.5
  43.5 0.0 copy-start.6
  43.5 0.1 all_to_all.14
  43.6 13.0 %all_to_all.19 = bf16[4,128,320]{1,2,0:T(8,128)(2,1)S(1)} all-to-all(bf16[4,128,320]{1,2,0:T(8,128)(2,1)S(1)} %copy.16), channel_id=1, replica_groups=mesh['img'=8,'sp'=4] {'sp'}, dimensions={0} | all-to-all | bytes 655360 | tf_op jit(solution)/shard_map/all_to_all | solution.py:91
  56.6 0.0 copy-start.7
  56.6 10.5 %all-gather.6.cloned.1.call-done = bf16[1280,1280]{1,0:T(8,128)(2,1)} async-done(((bf16[320,1280]{1,0:T(8,128)(2,1)}), bf16[1280,1280]{1,0:T(8,128)(2,1)}) %all-gather.6.cloned.1.call-update) | async-done | bytes 3276816 | tf_op jit(solution)/shard_map/all_gather | solution.py:94
  67.1 0.0 copy-done.1
  67.1 0.0 copy-done.4
  67.1 2.7 %convert_reduce_fusion.1 = (f32[128]{0:T(128)S(1)}, bf16[128,1280]{1,0:T(8,128)(2,1)S(1)}) fusion(f32[1280]{0:T(1024)S(1)} %copy-done.4, bf16[128,1280]{0,1:T(8,128)(2,1)S(1)} %bitcast.29, bf16[1280,1280]{1,0:T(8,128)(2,1)} %all-gather.6.cloned.1.call-done, bf16[128,1280]{1,0:T(8,128)(2,1)S(1)} %copy-done.1), kind=kOutput, calls=%fused_computation.19 | convolution fusion | flops 420413312 | bytes 4265472 | tf_op jit(solution)/shard_map/dot_general | solution.py:92
  69.8 0.0 copy-start.2
  69.8 0.2 fusion.19
  70.1 0.0 copy-done.5
  70.1 0.0 copy-done.6
  70.1 0.3 fusion.22
  70.4 0.9 reshape.180
  71.3 0.0 all-gather.8.cloned.1.call-update
  71.3 18.3 %all-gather.8.cloned.1.call-done = bf16[128,5120]{1,0:T(8,128)(2,1)} async-done(((bf16[32,5120]{1,0:T(8,128)(2,1)}), bf16[128,5120]{1,0:T(8,128)(2,1)}) %all-gather.8.cloned.1.call-update) | async-done | bytes 1310736 | tf_op jit(solution)/shard_map/all_gather | solution.py:102
  89.6 0.0 copy-done.7
  89.6 9.1 %fusion.25 = bf16[128,1280]{1,0:T(8,128)(2,1)} fusion(bf16[128,5120]{1,0:T(8,128)(2,1)} %all-gather.8.cloned.1.call-done, bf16[5120,1280]{1,0:T(8,128)(2,1)} %param.22, f32[1280]{0:T(1024)S(1)} %copy-done.7), kind=kOutput, calls=%fused_computation.34 | convolution fusion | flops 1688535040 | bytes 14750720 | tf_op jit(solution)/shard_map/dot_general | solution.py:101
  98.7 0.0 copy-done.2
  (6 shorter events, 0.1 us)
Async XLA Ops:
  7.2 25.6 %copy-start = (bf16[1280,3,320]{0,2,1:T(8,128)(2,1)S(1)}, bf16[1280,3,320]{0,2,1:T(8,128)(2,1)}, u32[]{:S(2)}) copy-start(bf16[1280,3,320]{0,2,1:T(8,128)(2,1)} %param.16) | copy-start | bytes 7372804
  7.2 25.6 %all-gather.4.cloned.1.call-start = ((), (), s32[]{:S(2)}) async-start(), calls=%async_computation.1 | async-start | bytes 1638400 | tf_op jit(solution)/shard_map/all_gather | solution.py:80
  11.7 55.4 %all-gather.6.cloned.1.call-start = ((), (), s32[]{:S(2)}) async-start(), calls=%async_computation.2 | async-start | bytes 4096000 | tf_op jit(solution)/shard_map/all_gather | solution.py:94
  12.5 77.2 %all-gather.8.cloned.1.call-start = ((), (), s32[]{:S(2)}) async-start(), calls=%async_computation.3 | async-start | bytes 1638400 | tf_op jit(solution)/shard_map/all_gather | solution.py:102
  36.9 3.5 %copy-start.3 = (bf16[512,1,320]{0,2,1:T(8,128)(2,1)S(1)}, bf16[512,1,320]{0,2,1:T(8,128)(2,1)}, u32[]{:S(2)}) copy-start(bf16[512,1,320]{0,2,1:T(8,128)(2,1)} %slice.51) | copy-start | bytes 983044
  40.4 26.7 %copy-start.1 = (bf16[128,1280]{1,0:T(8,128)(2,1)S(1)}, bf16[128,1280]{1,0:T(8,128)(2,1)}, u32[]{:S(2)}) copy-start(bf16[128,1280]{1,0:T(8,128)(2,1)} %param.12) | copy-start | bytes 983044
  40.4 26.7 %copy-start.4 = (f32[1280]{0:T(1024)S(1)}, f32[1280]{0:T(1024)}, u32[]{:S(2)}) copy-start(f32[1280]{0:T(1024)} %param.19) | copy-start | bytes 15364
  43.5 26.6 %copy-start.5 = (f32[1280]{0:T(1024)S(1)}, f32[1280]{0:T(1024)}, u32[]{:S(2)}) copy-start(f32[1280]{0:T(1024)} %param.21) | copy-start | bytes 15364
  43.5 26.6 %copy-start.6 = (f32[1280]{0:T(1024)S(1)}, f32[1280]{0:T(1024)}, u32[]{:S(2)}) copy-start(f32[1280]{0:T(1024)} %param.20) | copy-start | bytes 15364
  56.6 33.0 %copy-start.7 = (f32[1280]{0:T(1024)S(1)}, f32[1280]{0:T(1024)}, u32[]{:S(2)}) copy-start(f32[1280]{0:T(1024)} %param.23) | copy-start | bytes 15364
  69.8 28.9 %copy-start.2 = (bf16[128,1280]{1,0:T(8,128)(2,1)}, bf16[128,1280]{1,0:T(8,128)(2,1)S(1)}, u32[]{:S(2)}) copy-start(bf16[128,1280]{1,0:T(8,128)(2,1)S(1)} %get-tuple-element.34) | copy-start | bytes 983044
Sparse Core Ops, SparseCore 0:
  11.8 20.8 all-gather.3
  34.3 32.7 all-gather.5
  71.4 18.1 all-gather.7
where the time goes:
time: 106 us; the launch traced here: 105 us
  waiting for transfers between devices  47.5 us (45%)
  matrix products  21 us (20%)
  between operations  13.9 us (13%)
  blocking collectives  13 us (12%)
  other arithmetic  6.95 us (7%)
  local copies, waits for them, and re-layouts  2.74 us (3%)
    all_gather x1, waiting for transfers between devices, per_device(): lax.all_gather(blocks, 'sp', axis=0, tiled=True)  18.3 us
    all_gather x1, waiting for transfers between devices, per_device(): lax.all_gather(normed, 'sp', axis=0, tiled=True)  18 us
    all_to_all x1, blocking collectives, per_device(): lax.all_to_all(attended, 'sp', split_axis=0, concat_axis=1, tiled=True)  13 us
    all_gather x1, waiting for transfers between devices, per_device(): lax.all_gather(proj_weight, 'sp', axis=0, tiled=True)  10.5 us
    dot_general x1, matrix products, per_device(): jnp.dot(lax.all_gather(blocks, 'sp', axis=0, tiled=True), fc1_weight, pre...  9.06 us
    sub x1, matrix products, one_block(): expo = jnp.exp(scores - top)  3.44 us
    dot_general x1, matrix products, one_block(): jnp.einsum('hbk,khd->bhd', weights, vshaped, preferred_element_type=jnp.f...  3.07 us
    dot_general x1, matrix products, per_device(): jnp.einsum('pd,dcn->pcn', lax.all_gather(normed, 'sp', axis=0, tiled=True...  2.77 us
  transfers between devices with their start and end apart: 3, of which 3 were waited for; matrix products, arithmetic and copies ran while one was open for 12% of the time, Pallas kernels for 0%

commit v1 on v0

--- a/solution.py
+++ b/solution.py
@@ -1,16 +1,228 @@
+import functools
+import math
+
 import jax
 import jax.numpy as jnp
 from jax import lax
+from jax.experimental import pallas as pl
+from jax.experimental.pallas import tpu as pltpu
 from jax.sharding import PartitionSpec as P
 
 HEADS = 16
+EPS = 1e-06
+MIB = 1 << 20
+VMEM = pl.BlockSpec(memory_space=pltpu.VMEM)
+NT = (((1,), (1,)), ((), ()))
+TN = (((0,), (0,)), ((), ()))
+NN = (((1,), (0,)), ((), ()))
 
 
 def layer_norm(values, gain, bias):
     mean = jnp.mean(values, axis=-1, keepdims=True)
     centered = values - mean
     var = jnp.mean(centered * centered, axis=-1, keepdims=True)
-    return centered * lax.rsqrt(var + 1e-06) * gain + bias
+    return centered * lax.rsqrt(var + EPS) * gain + bias
+
+
+def dot(a, b, dims):
+    return lax.dot_general(a, b, dims, preferred_element_type=jnp.float32)
+
+
+def call(kernel, outs, nbytes, flops, name):
+    return pl.pallas_call(
+        kernel,
+        out_shape=outs,
+        compiler_params=pltpu.CompilerParams(vmem_limit_bytes=nbytes),
+        cost_estimate=pl.CostEstimate(flops=flops, bytes_accessed=1 << 20, transcendentals=0),
+        name=name,
+    )
+
+
+def project_kernel(hdim, xa, xb, wown, wpair, gain, nbias, qbias, cosine, sine, qout, kout, vout):
+    rows = xa.shape[0]
+    local = wown.shape[0] // 3
+    half = hdim // 2
+    me = lax.axis_index("sp")
+    normed = jnp.concatenate(
+        [
+            layer_norm(x[...].astype(jnp.float32), gain[...], nbias[...]).astype(jnp.bfloat16)
+            for x in (xa, xb)
+        ],
+        axis=0,
+    )
+    cos, sin = cosine[...], sine[...]
+    for side, weight in enumerate((wown, wpair)):
+        owner = me if side == 0 else me ^ 1
+        for c, out in enumerate((qout, kout, vout)):
+            raw = dot(weight[c * local : (c + 1) * local, :], normed, NT)
+            raw = raw + qbias[pl.ds(pl.multiple_of(owner * local, 8), local), c : c + 1]
+            base = side * local
+            if c == 2:
+                out[base : base + local, :] = raw.astype(jnp.bfloat16)
+                continue
+            for h in range(local // hdim):
+                top = raw[h * hdim : h * hdim + half]
+                low = raw[h * hdim + half : (h + 1) * hdim]
+                turned = jnp.concatenate([top * cos - low * sin, low * cos + top * sin], axis=0)
+                out[base + h * hdim : base + (h + 1) * hdim, :] = turned.astype(jnp.bfloat16)
+
+
+def attend_kernel(hdim, rows, q, kl, kr, vl, vr, pown, ppair, part, send):
+    scale = math.log2(math.e) / math.sqrt(hdim)
+    local = pown.shape[0]
+    pieces = []
+    for h in range(q.shape[0] // hdim):
+        f = slice(h * hdim, (h + 1) * hdim)
+        qh = q[f, 0:rows]
+        sl = dot(kl[f, :], qh, TN)
+        sr = dot(kr[f, :], qh, TN)
+        top = jnp.maximum(jnp.max(sl, axis=0, keepdims=True), jnp.max(sr, axis=0, keepdims=True))
+        el = jnp.exp2((sl - top) * scale)
+        er = jnp.exp2((sr - top) * scale)
+        inv = 1.0 / (jnp.sum(el, axis=0, keepdims=True) + jnp.sum(er, axis=0, keepdims=True))
+        wl = (el * inv).astype(jnp.bfloat16)
+        wr = (er * inv).astype(jnp.bfloat16)
+        pieces.append((dot(vl[f, :], wl, NN) + dot(vr[f, :], wr, NN)).astype(jnp.bfloat16))
+    per = local // hdim
+    mine = jnp.concatenate(pieces[:per], axis=0)
+    other = jnp.concatenate(pieces[per:], axis=0)
+    total = dot(mine, pown[...], TN) + dot(other, ppair[...], TN)
+    part[...] = total
+    send[...] = total.astype(jnp.bfloat16)
+
+
+def merge_kernel(x, part, got, pbias, gain, bias, blocks, *rest):
+    scratch = rest[-1]
+    width = x.shape[1]
+    value = x[...].astype(jnp.float32) + (part[...] + got[...].astype(jnp.float32)) + pbias[...]
+    vit = value.astype(jnp.bfloat16)
+    if len(rest) == 2:
+        rest[0][...] = vit
+    normed = layer_norm(vit.astype(jnp.float32), gain[...], bias[...])
+    count = x.shape[0] // 4
+    lanes = scratch.shape[2]
+    for t in range(width // lanes):
+        scratch[t] = normed[:, t * lanes : (t + 1) * lanes]
+        for j in range(4):
+            at = j * width + t * lanes
+            blocks[:, at : at + lanes] = scratch[t, pl.ds(j, count, stride=4), :].astype(jnp.bfloat16)
+
+
+def gelu(v):
+    return 0.5 * v * (1.0 + lax.erf(v * math.sqrt(0.5)))
+
+
+def hidden_kernel(own, pair, weight, bias, *rest):
+    out = rest[-1]
+    me = lax.axis_index("sp")
+    count = own.shape[0]
+    both = jnp.concatenate([own[...], pair[...]], axis=0)
+    hid = gelu(dot(both, weight[...], NN) + bias[...]).astype(jnp.bfloat16)
+    if len(rest) == 1:
+        start = 0
+    else:
+        early = rest[0]
+        chip = me // 2
+        out[pl.ds(pl.multiple_of(chip * 2 * count, 2 * count), 2 * count), :] = early[...]
+        start = (1 - chip) * 2 * count
+    core = me % 2
+    out[pl.ds(pl.multiple_of(start + core * count, count), count), :] = hid[:count]
+    out[pl.ds(pl.multiple_of(start + (1 - core) * count, count), count), :] = hid[count:]
+
+
+def shape(dims, dtype=jnp.bfloat16):
+    return jax.ShapeDtypeStruct(dims, dtype)
+
+
+def two_chips(
+    patches,
+    pos_ids,
+    norm_gain,
+    norm_bias,
+    qkv_weight,
+    qkv_bias,
+    proj_weight,
+    proj_bias,
+    merge_gain,
+    merge_bias,
+    fc1_weight,
+    fc1_bias,
+):
+    me = lax.axis_index("sp")
+    prow, width = patches.shape
+    hdim = width // HEADS
+    local = qkv_weight.shape[2]
+    hidden = fc1_weight.shape[1]
+
+    def swap(value, bit):
+        return lax.ppermute(value, "sp", [(i, i ^ bit) for i in range(4)])
+
+    weight = qkv_weight.transpose(1, 2, 0).reshape(3 * local, width)
+    x_pair = swap(patches, 1)
+    x_far = swap(patches, 2)
+    w_pair = swap(weight, 1)
+    p_pair = swap(proj_weight, 1)
+    x_farpair = swap(x_far, 1)
+
+    quarter = hdim // 4
+    inv = 1.0 / 10000.0 ** (jnp.arange(quarter, dtype=jnp.float32) * 2.0 / (hdim // 2))
+
+    def tables(blocks):
+        pos = jnp.concatenate(
+            [lax.dynamic_slice_in_dim(pos_ids, b * prow, prow, 1) for b in blocks], axis=1
+        ).astype(jnp.float32)
+        angle = jnp.concatenate([inv[:, None] * pos[0:1], inv[:, None] * pos[1:2]], axis=0)
+        return jnp.cos(angle), jnp.sin(angle)
+
+    row = lambda v: v.reshape(1, -1)
+    qbias = qkv_bias.T
+    both = 2 * local
+    part_shape = (shape((prow, width), jnp.float32), shape((prow, width)))
+
+    def project(xa, xb, blocks, name):
+        cos, sin = tables(blocks)
+        outs = tuple(shape((both, 2 * prow)) for _ in range(3))
+        return call(
+            functools.partial(project_kernel, hdim), outs, 24 * MIB, 2 * 2 * prow * width * 3 * both, name
+        )(xa, xb, weight, w_pair, row(norm_gain), row(norm_bias), qbias, cos, sin)
+
+    ql, kl, vl = project(patches, x_pair, (me, me ^ 1), "near")
+    qr, kr, vr = project(x_far, x_farpair, (me ^ 2, me ^ 3), "far")
+
+    def attend(q, name):
+        return call(
+            functools.partial(attend_kernel, hdim, prow), part_shape, 24 * MIB, 4 * prow * 4 * prow * both, name
+        )(q, kl, kr, vl, vr, proj_weight, p_pair)
+
+    part1, send1 = attend(qr, "attend1")
+    got0 = swap(send1, 2)
+    part0, send0 = attend(ql, "attend0")
+    got1 = swap(send0, 2)
+
+    def merge(x, part, got, outs, name):
+        return pl.pallas_call(
+            merge_kernel,
+            out_shape=outs,
+            scratch_shapes=[pltpu.VMEM((width // 128, prow, 128), jnp.float32)],
+            compiler_params=pltpu.CompilerParams(vmem_limit_bytes=16 * MIB),
+            cost_estimate=pl.CostEstimate(flops=1 << 27, bytes_accessed=1 << 20, transcendentals=0),
+            name=name,
+        )(x, part, got, row(proj_bias), row(merge_gain), row(merge_bias))
+
+    bshape = shape((prow // 4, 4 * width))
+    blocks0, vit = merge(patches, part0, got0, (bshape, shape((prow, width))), "merge0")
+    pair0 = swap(blocks0, 1)
+    fc1 = pltpu.with_memory_space_constraint(fc1_weight, pltpu.VMEM)
+    flops = 2 * prow // 2 * 4 * width * hidden
+    early = call(hidden_kernel, shape((prow // 2, hidden)), 24 * MIB, flops, "hidden0")(
+        blocks0, pair0, fc1, row(fc1_bias)
+    )
+    (blocks1,) = merge(x_far, part1, got1, (bshape,), "merge1")
+    pair1 = swap(blocks1, 1)
+    out = call(hidden_kernel, shape((prow, hidden)), 24 * MIB, flops, "hidden1")(
+        blocks1, pair1, fc1, row(fc1_bias), early
+    )
+    return vit, out
 
 
 def rotate(values, positions, nheads):
@@ -29,7 +241,7 @@
     return (shaped * cosine + turned * sine).reshape(count, nheads * hdim)
 
 
-def attend(query, keys, value, nheads, hdim):
+def attend_blocks(query, keys, value, nheads, hdim):
     count = query.shape[0]
     block = min(512, count)
     qblocks = query.reshape(count // block, block, nheads, hdim)
@@ -38,9 +250,7 @@
     scale = 1.0 / jnp.sqrt(jnp.float32(hdim))
 
     def one_block(qpart):
-        scores = (
-            jnp.einsum("bhd,khd->hbk", qpart, kshaped, preferred_element_type=jnp.float32) * scale
-        )
+        scores = jnp.einsum("bhd,khd->hbk", qpart, kshaped, preferred_element_type=jnp.float32) * scale
         top = jnp.max(scores, axis=-1, keepdims=True)
         expo = jnp.exp(scores - top)
         weights = (expo / jnp.sum(expo, axis=-1, keepdims=True)).astype(jnp.bfloat16)
@@ -50,7 +260,7 @@
     return lax.map(one_block, qblocks).reshape(count, nheads * hdim)
 
 
-def per_device(
+def any_size(
     patches,
     pos_ids,
     norm_gain,
@@ -66,8 +276,7 @@
 ):
     groups = lax.axis_size("sp")
     where = lax.axis_index("sp")
-    prow = patches.shape[0]
-    width = patches.shape[1]
+    prow, width = patches.shape
     heads_local = HEADS // groups
     hdim = width // HEADS
     local_width = width // groups
@@ -86,8 +295,7 @@
     query = rotate(qkv[:, 0], pos_ids, heads_local).astype(jnp.bfloat16)
     keys = rotate(qkv[:, 1], pos_ids, heads_local).astype(jnp.bfloat16)
     value = qkv[:, 2].astype(jnp.bfloat16)
-    spread = jnp.stack([query, keys, value])
-    attended = attend(spread[0], spread[1], spread[2], heads_local, hdim)
+    attended = attend_blocks(query, keys, value, heads_local, hdim)
     returned = lax.all_to_all(attended, "sp", split_axis=0, concat_axis=1, tiled=True)
     projected = jnp.dot(
         returned,
@@ -109,6 +317,12 @@
     return (vit_out, merged_hidden)
 
 
+def per_device(*args):
+    if lax.axis_size("sp") == 4:
+        return two_chips(*args)
+    return any_size(*args)
+
+
 def solution(mesh):
     return jax.shard_map(
         per_device,

time: 106 us -> 51.3 us (0.48)
  waiting for transfers between devices: 47.5 us -> 17.3 us
  Pallas kernels: 0 us -> 21.7 us
  matrix products: 21 us -> 0 us
  between operations: 13.9 us -> 0.88 us
  blocking collectives: 13 us -> 0 us
  other arithmetic: 6.95 us -> 0.41 us
  starting transfers between devices: 0.12 us -> 5.86 us
  local copies, waits for them, and re-layouts: 2.74 us -> 4.87 us
    all_gather x3 -> x0, waiting for transfers between devices: 46.8 us -> none  [the longest x1 18.3 us: per_device(): lax.all_gather(blocks, 'sp', axis=0, tiled=True)]
    pallas_call x0 -> x8, Pallas kernels: none -> 21.7 us  [the longest x2 8.89 us: attend(): call(functools.partial(attend_kernel, hdim, prow), part_shape, 24 * MIB,...]
    dot_general x4 -> x0, matrix products: 17.6 us -> none  [the longest x1 9.06 us: per_device(): jnp.dot(lax.all_gather(blocks, 'sp', axis=0, tiled=True), fc1_weight, pre...]
    ppermute x0 -> x9, waiting for transfers between devices: none -> 17.3 us  [swap(): return lax.ppermute(value, 'sp', [(i, i ^ bit) for i in range(4)])]
    all_to_all x1 -> x0, blocking collectives: 13 us -> none  [per_device(): lax.all_to_all(attended, 'sp', split_axis=0, concat_axis=1, tiled=True)]
    ppermute x0 -> x9, starting transfers between devices: none -> 5.86 us  [swap(): return lax.ppermute(value, 'sp', [(i, i ^ bit) for i in range(4)])]
    sub x1 -> x0, matrix products: 3.44 us -> none  [one_block(): expo = jnp.exp(scores - top)]
    convert_element_type x4 -> x1, other arithmetic: 3.4 us -> 0.01 us  [tables(): pos = jnp.concatenate([lax.dynamic_slice_in_dim(pos_ids, b * prow, prow,...]
  transfers between devices with their start and end apart: 3 -> 9, of which waited for: 3 -> 3; matrix products, arithmetic and copies ran while one was open for 12% -> 7% of each run, Pallas kernels for 0% -> 27%
where the time goes in v1:
time: 51.3 us; the launch traced here: 50.9 us
  Pallas kernels  21.7 us (42%)
  waiting for transfers between devices  17.3 us (34%)
  starting transfers between devices  5.86 us (11%)
  local copies, waits for them, and re-layouts  4.87 us (9%)
  between operations  0.88 us (2%)
    ppermute x9, waiting for transfers between devices, swap(): return lax.ppermute(value, 'sp', [(i, i ^ bit) for i in range(4)])  17.3 us
    pallas_call x2, Pallas kernels, attend(): call(functools.partial(attend_kernel, hdim, prow), part_shape, 24 * MIB,...  8.89 us
    pallas_call x2, Pallas kernels, project(): call(functools.partial(project_kernel, hdim), outs, 24 * MIB, 2 * 2 * pro...  5.91 us
    ppermute x9, starting transfers between devices, swap(): return lax.ppermute(value, 'sp', [(i, i ^ bit) for i in range(4)])  5.86 us
    pallas_call x1, Pallas kernels, two_chips(): call(hidden_kernel, shape((prow, hidden)), 24 * MIB, flops, 'hidden1')  3.13 us
    unnamed x19, local copies, waits for them, and re-layouts  2.7 us
    pallas_call x1, Pallas kernels, two_chips(): call(hidden_kernel, shape((prow // 2, hidden)), 24 * MIB, flops, 'hidden0')  2.41 us
    reshape x6, local copies, waits for them, and re-layouts, two_chips(): row = lambda v: v.reshape(1, -1)  1.43 us
  transfers between devices with their start and end apart: 9, of which 3 were waited for; matrix products, arithmetic and copies ran while one was open for 7% of the time, Pallas kernels for 27%

profile of v1, /device:TPU:0, one launch (start us, length us, event | category | flops | bytes accessed | tf_op | source)
XLA Modules:
  0.0 50.9 jit_solution(13169277011352990476)
XLA Ops:
  0.6 0.6 %collective-permute-start.1 = (bf16[960,1280]{1,0:T(8,128)(2,1)}, bf16[960,1280]{1,0:T(8,128)(2,1)S(1)}, u32[]{:S(2)}, u32[]{:S(2)}) collective-permute-start(bf16[960,1280]{1,0:T(8,128)(2,1)} %bitcast.8), channel_id=1, source_target_pairs={{0,1},{1,0},{2,3},{3,2},{4,5},{5,4},{6,7},{7,6},{8,9},{9,8},{10,11... | collective-permute-start | bytes 7372808 | tf_op jit(solution)/shard_map/ppermute | solution.py:158
  1.2 2.6 %collective-permute-start.2 = (bf16[128,1280]{1,0:T(8,128)(2,1)}, bf16[128,1280]{1,0:T(8,128)(2,1)S(1)}, u32[]{:S(2)}, u32[]{:S(2)}) collective-permute-start(bf16[128,1280]{1,0:T(8,128)(2,1)} %x.1), channel_id=1, source_target_pairs={{0,2},{1,3},{2,0},{3,1},{4,6},{5,7},{6,4},{7,5},{8,10},{9,11},{10,... | collective-permute-start | bytes 983048 | tf_op jit(solution)/shard_map/ppermute | solution.py:158
  3.7 0.1 collective-permute-start
  3.9 0.4 collective-permute-start.4
  4.3 0.7 %constant_dynamic-slice_fusion.1 = (s32[2,128]{1,0:T(2,128)S(1)}, s32[2,128]{1,0:T(2,128)S(1)}, s32[2,128]{1,0:T(2,128)S(1)}, s32[2,128]{1,0:T(2,128)S(1)}) fusion(s32[2,512]{1,0:T(2,128)} %param.13, s32[]{:T(128)S(6)} %select_n.14, s32[]{:T(128)S(6)} %select_n.13, s32[]{:T(128)S(6)} %select_n.12, s32[]{:T(128)S(6)} %select_n.15), kind=kLoop, calls=%fused_computation.13 | loop fusion | bytes 8208 | tf_op jit(solution)/shard_map/dynamic_slice | solution.py:172
  5.0 7.2 %collective-permute-done.2.xa.x = bf16[128,1280]{1,0:T(8,128)(2,1)S(1)} collective-permute-done((bf16[128,1280]{1,0:T(8,128)(2,1)}, bf16[128,1280]{1,0:T(8,128)(2,1)S(1)}, u32[]{:S(2)}, u32[]{:S(2)}) %collective-permute-start.2) | collective-permute-done | bytes 327712 | tf_op jit(solution)/shard_map/ppermute | solution.py:158
  12.3 0.0 collective-permute-start.3
  12.3 0.1 broadcast_multiply_fusion.1
  12.3 1.0 %copy.14 = f32[3,1280]{0,1:T(8,128)S(1)} copy(f32[3,1280]{1,0:T(4,128)} %param.17) | data formatting | bytes 30720 | tf_op args[5]
  13.3 0.7 %reshape.38.gain = f32[1,1280]{1,0:T(1,128)S(1)} reshape(f32[1280]{0:T(1024)} %param.14) | data formatting | bytes 10240 | tf_op jit(solution)/shard_map/reshape | solution.py:177
  14.0 0.7 %reshape.39.nbias = f32[1,1280]{1,0:T(1,128)S(1)} reshape(f32[1280]{0:T(1024)} %param.15) | data formatting | bytes 10240 | tf_op jit(solution)/shard_map/reshape | solution.py:177
  14.7 0.2 fusion
  14.9 0.2 fusion.2
  15.1 0.0 collective-permute-done.3.xb
  15.1 0.0 collective-permute-done.1.wpair
  15.1 0.0 copy-start.1
  15.1 1.7 %copy-done.1 = bf16[1280,3,320]{0,2,1:T(8,128)(2,1)S(1)} copy-done((bf16[1280,3,320]{0,2,1:T(8,128)(2,1)S(1)}, bf16[1280,3,320]{0,2,1:T(8,128)(2,1)}, u32[]{:S(2)}) %copy-start.1) | copy-done | bytes 2457624
  16.8 0.0 copy-start.2
  16.8 0.0 copy-start.4
  16.8 0.0 copy-start.3
  16.8 0.0 copy-start.5
  16.8 0.0 copy-start.6
  16.8 0.0 copy-start.7
  16.8 3.0 %far.1 = (bf16[640,256]{1,0:T(8,128)(2,1)S(1)}, bf16[640,256]{1,0:T(8,128)(2,1)S(1)}, bf16[640,256]{1,0:T(8,128)(2,1)S(1)}) custom-call(bf16[128,1280]{1,0:T(8,128)(2,1)S(1)} %collective-permute-done.2.xa.x, bf16[128,1280]{1,0:T(8,128)(2,1)} %collective-permute-done.3.xb, bf16[960,1280]{1,0:T(8,128)(2,1)S(1)} %bitcast.9, ...), custom_call_target="tpu_custom_call" | custom-call | flops 1258291200 | bytes 1048576 | tf_op jit(solution)/shard_map/far/pallas_call | solution.py:185
  19.8 0.0 collective-permute-done.xb
  19.8 0.0 copy-done.2
  19.8 0.0 copy-done.4
  19.8 0.0 copy-start
  19.8 3.0 %near.1 = (bf16[640,256]{1,0:T(8,128)(2,1)S(1)}, bf16[640,256]{1,0:T(8,128)(2,1)S(1)}, bf16[640,256]{1,0:T(8,128)(2,1)S(1)}) custom-call(bf16[128,1280]{1,0:T(8,128)(2,1)S(1)} %copy-done.4, bf16[128,1280]{1,0:T(8,128)(2,1)} %collective-permute-done.xb, bf16[960,1280]{1,0:T(8,128)(2,1)S(1)} %bitcast.10, bf16[960,1280]{1,0:T(8,128)(2,1)S(1)} %collective-permute-done.1.wpair, ...), custom_call_target="tpu_custom_call" | custom-call | flops 1258291200 | bytes 1048576 | tf_op jit(solution)/shard_map/near/pallas_call | solution.py:185
  22.8 0.0 collective-permute-done.4.ppair
  22.8 0.0 copy-done.3
  22.8 4.8 %attend1.1 = (f32[128,1280]{1,0:T(8,128)S(1)}, bf16[128,1280]{1,0:T(8,128)(2,1)S(1)}) custom-call(bf16[640,256]{1,0:T(8,128)(2,1)S(1)} %get-tuple-element.20.q, bf16[640,256]{1,0:T(8,128)(2,1)S(1)} %get-tuple-element.15.kl, bf16[640,256]{1,0:T(8,128)(2,1)S(1)} %get-tuple-element.16.kr, bf16[640,256]{1,0:T(8,128)(2,1)S(1)} %get-tuple-element.17.vl, ...), custom_call_target="tpu_custom_call" | custom-call | flops 167772160 | bytes 1048576 | tf_op jit(solution)/shard_map/attend1/pallas_call | solution.py:193
  27.6 1.8 %collective-permute-start.5 = (bf16[128,1280]{1,0:T(8,128)(2,1)S(1)}, bf16[128,1280]{1,0:T(8,128)(2,1)S(1)}, u32[]{:S(2)}, u32[]{:S(2)}) collective-permute-start(bf16[128,1280]{1,0:T(8,128)(2,1)S(1)} %get-tuple-element.21), channel_id=1, source_target_pairs={{0,2},{1,3},{2,0},{3,1},{4,6},{5,7},{6,4},{7,5},{8,10},{9,11},{10,... | collective-permute-start | bytes 983048 | tf_op jit(solution)/shard_map/ppermute | solution.py:158
  29.4 0.0 copy-start.8
  29.4 4.1 %attend0.1 = (f32[128,1280]{1,0:T(8,128)S(1)}, bf16[128,1280]{1,0:T(8,128)(2,1)S(1)}) custom-call(bf16[640,256]{1,0:T(8,128)(2,1)S(1)} %get-tuple-element.14.q, bf16[640,256]{1,0:T(8,128)(2,1)S(1)} %get-tuple-element.15.kl, bf16[640,256]{1,0:T(8,128)(2,1)S(1)} %get-tuple-element.16.kr, bf16[640,256]{1,0:T(8,128)(2,1)S(1)} %get-tuple-element.17.vl, ...), custom_call_target="tpu_custom_call" | custom-call | flops 167772160 | bytes 1048576 | tf_op jit(solution)/shard_map/attend0/pallas_call | solution.py:193
  33.5 0.3 collective-permute-start.6
  33.9 0.0 copy-done.5
  33.9 0.0 copy-done.6
  33.9 0.0 copy-done.7
  33.9 4.4 %collective-permute-done.5.got = bf16[128,1280]{1,0:T(8,128)(2,1)S(1)} collective-permute-done((bf16[128,1280]{1,0:T(8,128)(2,1)S(1)}, bf16[128,1280]{1,0:T(8,128)(2,1)S(1)}, u32[]{:S(2)}, u32[]{:S(2)}) %collective-permute-start.5) | collective-permute-done | bytes 327712 | tf_op jit(solution)/shard_map/ppermute | solution.py:158
  38.3 0.9 %merge0.1 = (bf16[32,5120]{1,0:T(8,128)(2,1)S(1)}, bf16[128,1280]{1,0:T(8,128)(2,1)}) custom-call(bf16[128,1280]{1,0:T(8,128)(2,1)S(1)} %copy-done.4, f32[128,1280]{1,0:T(8,128)S(1)} %get-tuple-element.19.part, bf16[128,1280]{1,0:T(8,128)(2,1)S(1)} %collective-permute-done.5.got, f32[1,1280]{1,0:T(1,128)S(1)} %reshape.40.pbias, f32[1,1280]{1,0:T(1,128)S(1)} %reshape.41.gain, ...), custom_call_target="tpu_custom_call" | custom-call | flops 134217728 | bytes 1048576 | tf_op jit(solution)/shard_map/merge0/pallas_call | solution.py:203
  39.2 0.0 collective-permute-start.8
  39.2 5.7 %collective-permute-done.6.got = bf16[128,1280]{1,0:T(8,128)(2,1)S(1)} collective-permute-done((bf16[128,1280]{1,0:T(8,128)(2,1)S(1)}, bf16[128,1280]{1,0:T(8,128)(2,1)S(1)}, u32[]{:S(2)}, u32[]{:S(2)}) %collective-permute-start.6) | collective-permute-done | bytes 327712 | tf_op jit(solution)/shard_map/ppermute | solution.py:158
  44.8 0.4 merge1.1.own
  45.3 0.1 collective-permute-start.7
  45.3 0.0 copy-done.8
  45.4 0.0 collective-permute-done.8.pair
  45.4 0.0 copy-done
  45.4 2.4 %hidden0.1.rest_0_ = bf16[64,1280]{1,0:T(8,128)(2,1)S(1)} custom-call(bf16[32,5120]{1,0:T(8,128)(2,1)S(1)} %get-tuple-element.25.own, bf16[32,5120]{1,0:T(8,128)(2,1)S(1)} %collective-permute-done.8.pair, bf16[5120,1280]{1,0:T(8,128)(2,1)S(1)} %copy-done, f32[1,1280]{1,0:T(1,128)S(1)} %reshape.43.bias), custom_call_target="tpu_custom_call" | custom-call | flops 838860800 | bytes 1048576 | tf_op jit(solution)/shard_map/hidden0/pallas_call | solution.py:217
  47.8 0.0 collective-permute-done.7.pair
  47.8 3.1 %hidden1.1 = bf16[128,1280]{1,0:T(8,128)(2,1)} custom-call(bf16[32,5120]{1,0:T(8,128)(2,1)S(1)} %merge1.1.own, bf16[32,5120]{1,0:T(8,128)(2,1)S(1)} %collective-permute-done.7.pair, bf16[5120,1280]{1,0:T(8,128)(2,1)S(1)} %copy-done, f32[1,1280]{1,0:T(1,128)S(1)} %reshape.43.bias, bf16[64,1280]{1,0:T(8,128)(2,1)S(1)} %hidden0.1.rest_0_), custom_call_target="tpu_custom_call" | custom-call | flops 838860800 | bytes 1048576 | tf_op jit(solution)/shard_map/hidden1/pallas_call | solution.py:222
  (8 shorter events, 0.0 us)
Async XLA Ops:
  0.6 14.4 %collective-permute-start.1 = (bf16[960,1280]{1,0:T(8,128)(2,1)}, bf16[960,1280]{1,0:T(8,128)(2,1)S(1)}, u32[]{:S(2)}, u32[]{:S(2)}) collective-permute-start(bf16[960,1280]{1,0:T(8,128)(2,1)} %bitcast.8), channel_id=1, source_target_pairs={{0,1},{1,0},{2,3},{3,2},{4,5},{5,4},{6,7},{7,6},{8,9},{9,8},{10,11... | collective-permute-start | bytes 7372808 | tf_op jit(solution)/shard_map/ppermute | solution.py:158
  1.2 11.1 %collective-permute-start.2 = (bf16[128,1280]{1,0:T(8,128)(2,1)}, bf16[128,1280]{1,0:T(8,128)(2,1)S(1)}, u32[]{:S(2)}, u32[]{:S(2)}) collective-permute-start(bf16[128,1280]{1,0:T(8,128)(2,1)} %x.1), channel_id=1, source_target_pairs={{0,2},{1,3},{2,0},{3,1},{4,6},{5,7},{6,4},{7,5},{8,10},{9,11},{10,... | collective-permute-start | bytes 983048 | tf_op jit(solution)/shard_map/ppermute | solution.py:158
  3.7 16.0 %collective-permute-start = (bf16[128,1280]{1,0:T(8,128)(2,1)}, bf16[128,1280]{1,0:T(8,128)(2,1)}, u32[]{:S(2)}, u32[]{:S(2)}) collective-permute-start(bf16[128,1280]{1,0:T(8,128)(2,1)} %x.1), channel_id=1, source_target_pairs={{0,1},{1,0},{2,3},{3,2},{4,5},{5,4},{6,7},{7,6},{8,9},{9,8},{10,11... | collective-permute-start | bytes 983048 | tf_op jit(solution)/shard_map/ppermute | solution.py:158
  3.9 18.9 %collective-permute-start.4 = (bf16[320,1280]{1,0:T(8,128)(2,1)}, bf16[320,1280]{1,0:T(8,128)(2,1)}, u32[]{:S(2)}, u32[]{:S(2)}) collective-permute-start(bf16[320,1280]{1,0:T(8,128)(2,1)} %pown.3), channel_id=1, source_target_pairs={{0,1},{1,0},{2,3},{3,2},{4,5},{5,4},{6,7},{7,6},{8,9},{9,8},{10,11... | collective-permute-start | bytes 2457608 | tf_op jit(solution)/shard_map/ppermute | solution.py:158
  12.3 2.8 %collective-permute-start.3 = (bf16[128,1280]{1,0:T(8,128)(2,1)S(1)}, bf16[128,1280]{1,0:T(8,128)(2,1)}, u32[]{:S(2)}, u32[]{:S(2)}) collective-permute-start(bf16[128,1280]{1,0:T(8,128)(2,1)S(1)} %collective-permute-done.2.xa.x), channel_id=1, source_target_pairs={{0,1},{1,0},{2,3},{3,2},{4,5},{5,4},{6,7},{7,6},{8,9},{9,8},{10,11... | collective-permute-start | bytes 983048 | tf_op jit(solution)/shard_map/ppermute | solution.py:158
  15.1 1.7 %copy-start.1 = (bf16[1280,3,320]{0,2,1:T(8,128)(2,1)S(1)}, bf16[1280,3,320]{0,2,1:T(8,128)(2,1)}, u32[]{:S(2)}) copy-start(bf16[1280,3,320]{0,2,1:T(8,128)(2,1)} %param.16) | copy-start | bytes 7372804
  16.8 3.0 %copy-start.2 = (bf16[1280,3,320]{0,2,1:T(8,128)(2,1)S(1)}, bf16[1280,3,320]{0,2,1:T(8,128)(2,1)}, u32[]{:S(2)}) copy-start(bf16[1280,3,320]{0,2,1:T(8,128)(2,1)} %param.16) | copy-start | bytes 7372804
  16.8 3.0 %copy-start.4 = (bf16[128,1280]{1,0:T(8,128)(2,1)S(1)}, bf16[128,1280]{1,0:T(8,128)(2,1)}, u32[]{:S(2)}) copy-start(bf16[128,1280]{1,0:T(8,128)(2,1)} %x.1) | copy-start | bytes 983044
  16.8 6.0 %copy-start.3 = (bf16[320,1280]{1,0:T(8,128)(2,1)S(1)}, bf16[320,1280]{1,0:T(8,128)(2,1)}, u32[]{:S(2)}) copy-start(bf16[320,1280]{1,0:T(8,128)(2,1)} %pown.3) | copy-start | bytes 2457604
  16.8 17.1 %copy-start.5 = (f32[1280]{0:T(1024)S(1)}, f32[1280]{0:T(1024)}, u32[]{:S(2)}) copy-start(f32[1280]{0:T(1024)} %param.19) | copy-start | bytes 15364
  16.8 17.1 %copy-start.6 = (f32[1280]{0:T(1024)S(1)}, f32[1280]{0:T(1024)}, u32[]{:S(2)}) copy-start(f32[1280]{0:T(1024)} %param.20) | copy-start | bytes 15364
  16.8 17.1 %copy-start.7 = (f32[1280]{0:T(1024)S(1)}, f32[1280]{0:T(1024)}, u32[]{:S(2)}) copy-start(f32[1280]{0:T(1024)} %param.21) | copy-start | bytes 15364
  19.8 25.6 %copy-start = (bf16[5120,1280]{1,0:T(8,128)(2,1)S(1)}, bf16[5120,1280]{1,0:T(8,128)(2,1)}, u32[]{:S(2)}) copy-start(bf16[5120,1280]{1,0:T(8,128)(2,1)} %weight.3) | copy-start | bytes 39321604
  27.6 10.6 %collective-permute-start.5 = (bf16[128,1280]{1,0:T(8,128)(2,1)S(1)}, bf16[128,1280]{1,0:T(8,128)(2,1)S(1)}, u32[]{:S(2)}, u32[]{:S(2)}) collective-permute-start(bf16[128,1280]{1,0:T(8,128)(2,1)S(1)} %get-tuple-element.21), channel_id=1, source_target_pairs={{0,2},{1,3},{2,0},{3,1},{4,6},{5,7},{6,4},{7,5},{8,10},{9,11},{10,... | collective-permute-start | bytes 983048 | tf_op jit(solution)/shard_map/ppermute | solution.py:158
  29.4 15.9 %copy-start.8 = (f32[1280]{0:T(1024)S(1)}, f32[1280]{0:T(1024)}, u32[]{:S(2)}) copy-start(f32[1280]{0:T(1024)} %param.23) | copy-start | bytes 15364
  33.5 11.3 %collective-permute-start.6 = (bf16[128,1280]{1,0:T(8,128)(2,1)S(1)}, bf16[128,1280]{1,0:T(8,128)(2,1)S(1)}, u32[]{:S(2)}, u32[]{:S(2)}) collective-permute-start(bf16[128,1280]{1,0:T(8,128)(2,1)S(1)} %get-tuple-element.24), channel_id=1, source_target_pairs={{0,2},{1,3},{2,0},{3,1},{4,6},{5,7},{6,4},{7,5},{8,10},{9,11},{10,... | collective-permute-start | bytes 983048 | tf_op jit(solution)/shard_map/ppermute | solution.py:158
  39.2 6.2 %collective-permute-start.8 = (bf16[32,5120]{1,0:T(8,128)(2,1)S(1)}, bf16[32,5120]{1,0:T(8,128)(2,1)S(1)}, u32[]{:S(2)}, u32[]{:S(2)}) collective-permute-start(bf16[32,5120]{1,0:T(8,128)(2,1)S(1)} %get-tuple-element.25.own), channel_id=1, source_target_pairs={{0,1},{1,0},{2,3},{3,2},{4,5},{5,4},{6,7},{7,6},{8,9},{9,8},{10,11... | collective-permute-start | bytes 983048 | tf_op jit(solution)/shard_map/ppermute | solution.py:158
  45.3 2.5 %collective-permute-start.7 = (bf16[32,5120]{1,0:T(8,128)(2,1)S(1)}, bf16[32,5120]{1,0:T(8,128)(2,1)S(1)}, u32[]{:S(2)}, u32[]{:S(2)}) collective-permute-start(bf16[32,5120]{1,0:T(8,128)(2,1)S(1)} %merge1.1.own), channel_id=1, source_target_pairs={{0,1},{1,0},{2,3},{3,2},{4,5},{5,4},{6,7},{7,6},{8,9},{9,8},{10,11... | collective-permute-start | bytes 983048 | tf_op jit(solution)/shard_map/ppermute | solution.py:158

commit v2 on v1

--- a/solution.py
+++ b/solution.py
@@ -8,10 +8,12 @@
 from jax.experimental.pallas import tpu as pltpu
 from jax.sharding import PartitionSpec as P
 
+
 HEADS = 16
 EPS = 1e-06
 MIB = 1 << 20
 VMEM = pl.BlockSpec(memory_space=pltpu.VMEM)
+ANY = pl.BlockSpec(memory_space=pl.ANY)
 NT = (((1,), (1,)), ((), ()))
 TN = (((0,), (0,)), ((), ()))
 NN = (((1,), (0,)), ((), ()))
@@ -28,76 +30,148 @@
     return lax.dot_general(a, b, dims, preferred_element_type=jnp.float32)
 
 
-def call(kernel, outs, nbytes, flops, name):
+def call(kernel, outs, nbytes, flops):
     return pl.pallas_call(
         kernel,
         out_shape=outs,
         compiler_params=pltpu.CompilerParams(vmem_limit_bytes=nbytes),
         cost_estimate=pl.CostEstimate(flops=flops, bytes_accessed=1 << 20, transcendentals=0),
-        name=name,
     )
 
 
-def project_kernel(hdim, xa, xb, wown, wpair, gain, nbias, qbias, cosine, sine, qout, kout, vout):
+def norm_kernel(x, gain, bias, *rest):
+    out = rest[-1]
+    out[...] = layer_norm(x[...].astype(jnp.float32), gain[...], bias[...]).astype(jnp.bfloat16)
+
+
+def column(qbias, owner, local, c):
+    return qbias[pl.ds(pl.multiple_of(owner * local, 8), local), c : c + 1]
+
+
+def rotated(raw, cos, sin, hdim):
+    half = hdim // 2
+    pieces = []
+    for at in range(0, raw.shape[0], hdim):
+        top, low = raw[at : at + half], raw[at + half : at + hdim]
+        pieces += [top * cos - low * sin, low * cos + top * sin]
+    return jnp.concatenate(pieces, axis=0).astype(jnp.bfloat16)
+
+
+def paired(query, hdim):
+    zero = jnp.zeros((hdim, query.shape[1]), query.dtype)
+    rows = []
+    for at in range(0, query.shape[0], 2 * hdim):
+        rows.append(jnp.concatenate([query[at : at + hdim], zero], axis=1))
+        rows.append(jnp.concatenate([zero, query[at + hdim : at + 2 * hdim]], axis=1))
+    return jnp.concatenate(rows, axis=0)
+
+
+def near_kernel(hdim, xa, xb, wown, wpair, qbias, cosine, sine, qout, kout, vout):
+    local = wown.shape[0] // 3
     rows = xa.shape[0]
-    local = wown.shape[0] // 3
-    half = hdim // 2
     me = lax.axis_index("sp")
-    normed = jnp.concatenate(
-        [
-            layer_norm(x[...].astype(jnp.float32), gain[...], nbias[...]).astype(jnp.bfloat16)
-            for x in (xa, xb)
-        ],
-        axis=0,
-    )
+    normed = jnp.concatenate([xa[...], xb[...]], axis=0)
     cos, sin = cosine[...], sine[...]
     for side, weight in enumerate((wown, wpair)):
-        owner = me if side == 0 else me ^ 1
-        for c, out in enumerate((qout, kout, vout)):
-            raw = dot(weight[c * local : (c + 1) * local, :], normed, NT)
-            raw = raw + qbias[pl.ds(pl.multiple_of(owner * local, 8), local), c : c + 1]
-            base = side * local
-            if c == 2:
-                out[base : base + local, :] = raw.astype(jnp.bfloat16)
-                continue
-            for h in range(local // hdim):
-                top = raw[h * hdim : h * hdim + half]
-                low = raw[h * hdim + half : (h + 1) * hdim]
-                turned = jnp.concatenate([top * cos - low * sin, low * cos + top * sin], axis=0)
-                out[base + h * hdim : base + (h + 1) * hdim, :] = turned.astype(jnp.bfloat16)
-
-
-def attend_kernel(hdim, rows, q, kl, kr, vl, vr, pown, ppair, part, send):
+        owner = me ^ side
+        base = slice(side * local, (side + 1) * local)
+        part = lambda c: dot(weight[c * local : (c + 1) * local, :], normed, NT) + column(qbias, owner, local, c)
+        query = dot(weight[0:local, :], normed[:rows], NT) + column(qbias, owner, local, 0)
+        qout[base, :] = paired(rotated(query, cos[:, :rows], sin[:, :rows], hdim), hdim)
+        kout[base, :] = rotated(part(1), cos, sin, hdim)
+        vout[base, :] = part(2).astype(jnp.bfloat16)
+
+
+def first_kernel(hdim, q, k, v, tops, sums, outs):
     scale = math.log2(math.e) / math.sqrt(hdim)
-    local = pown.shape[0]
-    pieces = []
-    for h in range(q.shape[0] // hdim):
-        f = slice(h * hdim, (h + 1) * hdim)
-        qh = q[f, 0:rows]
-        sl = dot(kl[f, :], qh, TN)
-        sr = dot(kr[f, :], qh, TN)
-        top = jnp.maximum(jnp.max(sl, axis=0, keepdims=True), jnp.max(sr, axis=0, keepdims=True))
-        el = jnp.exp2((sl - top) * scale)
-        er = jnp.exp2((sr - top) * scale)
-        inv = 1.0 / (jnp.sum(el, axis=0, keepdims=True) + jnp.sum(er, axis=0, keepdims=True))
-        wl = (el * inv).astype(jnp.bfloat16)
-        wr = (er * inv).astype(jnp.bfloat16)
-        pieces.append((dot(vl[f, :], wl, NN) + dot(vr[f, :], wr, NN)).astype(jnp.bfloat16))
-    per = local // hdim
-    mine = jnp.concatenate(pieces[:per], axis=0)
-    other = jnp.concatenate(pieces[per:], axis=0)
-    total = dot(mine, pown[...], TN) + dot(other, ppair[...], TN)
+    rows = q.shape[1] // 2
+    for p in range(q.shape[0] // (2 * hdim)):
+        f = slice(2 * p * hdim, 2 * (p + 1) * hdim)
+        scores = dot(k[f, :], q[f, :], TN)
+        top = jnp.max(scores, axis=0, keepdims=True)
+        expo = jnp.exp2((scores - top) * scale)
+        tops[p : p + 1, :] = top
+        sums[p : p + 1, :] = jnp.sum(expo, axis=0, keepdims=True)
+        total = dot(v[f, :], expo.astype(jnp.bfloat16), NN)
+        outs[2 * p * hdim : (2 * p + 1) * hdim, :] = total[:hdim, :rows]
+        outs[(2 * p + 1) * hdim : 2 * (p + 1) * hdim, :] = total[hdim:, rows:]
+
+
+def far_kernel(hdim, xa, xb, wown, wpair, qbias, cosine, sine, q, tops, sums, outs, pown, ppair, part, send, kout, vout):
+    scale = math.log2(math.e) / math.sqrt(hdim)
+    local = wown.shape[0] // 3
+    rows = xa.shape[0]
+    me = lax.axis_index("sp")
+    normed = jnp.concatenate([xa[...], xb[...]], axis=0)
+    cos, sin = cosine[...], sine[...]
+    total = None
+    for side, weight in enumerate((wown, wpair)):
+        owner = me ^ side
+        base = slice(side * local, (side + 1) * local)
+        key = rotated(
+            dot(weight[local : 2 * local, :], normed, NT) + column(qbias, owner, local, 1), cos, sin, hdim
+        )
+        value = (dot(weight[2 * local :, :], normed, NT) + column(qbias, owner, local, 2)).astype(jnp.bfloat16)
+        kout[base, :] = key
+        vout[base, :] = value
+        pieces = []
+        for at in range(0, local, 2 * hdim):
+            f = slice(side * local + at, side * local + at + 2 * hdim)
+            p = (side * local + at) // (2 * hdim)
+            scores = dot(key[at : at + 2 * hdim], q[f, :], TN)
+            old = tops[p : p + 1, :]
+            top = jnp.maximum(old, jnp.max(scores, axis=0, keepdims=True))
+            expo = jnp.exp2((scores - top) * scale)
+            shrink = jnp.exp2((old - top) * scale)
+            inv = 1.0 / (sums[p : p + 1, :] * shrink + jnp.sum(expo, axis=0, keepdims=True))
+            late = dot(value[at : at + 2 * hdim], expo.astype(jnp.bfloat16), NN)
+            for h in range(2):
+                lanes = slice(h * rows, (h + 1) * rows)
+                feats = slice(h * hdim, (h + 1) * hdim)
+                early = outs[f.start + h * hdim : f.start + (h + 1) * hdim, :]
+                mixed = (early * shrink[:, lanes] + late[feats, lanes]) * inv[:, lanes]
+                pieces.append(mixed.astype(jnp.bfloat16))
+        add = dot(jnp.concatenate(pieces, axis=0), (pown, ppair)[side][...], TN)
+        total = add if total is None else total + add
     part[...] = total
     send[...] = total.astype(jnp.bfloat16)
 
 
-def merge_kernel(x, part, got, pbias, gain, bias, blocks, *rest):
-    scratch = rest[-1]
+def late_kernel(hdim, x, wown, wpair, qbias, cosine, sine, kn, vn, kf, vf, pown, ppair, part, send):
+    scale = math.log2(math.e) / math.sqrt(hdim)
+    local = wown.shape[0] // 3
+    rows = x.shape[0]
+    me = lax.axis_index("sp")
+    total = None
+    for side, weight in enumerate((wown, wpair)):
+        query = dot(weight[:local, :], x[...], NT) + column(qbias, me ^ side, local, 0)
+        query = paired(rotated(query, cosine[:, :rows], sine[:, :rows], hdim), hdim)
+        pieces = []
+        for at in range(0, local, 2 * hdim):
+            f = slice(side * local + at, side * local + at + 2 * hdim)
+            both = query[at : at + 2 * hdim]
+            sn = dot(kn[f, :], both, TN)
+            sf = dot(kf[f, :], both, TN)
+            top = jnp.maximum(jnp.max(sn, axis=0, keepdims=True), jnp.max(sf, axis=0, keepdims=True))
+            en = jnp.exp2((sn - top) * scale)
+            ef = jnp.exp2((sf - top) * scale)
+            inv = 1.0 / (jnp.sum(en, axis=0, keepdims=True) + jnp.sum(ef, axis=0, keepdims=True))
+            mixed = dot(vn[f, :], (en * inv).astype(jnp.bfloat16), NN)
+            mixed = (mixed + dot(vf[f, :], (ef * inv).astype(jnp.bfloat16), NN)).astype(jnp.bfloat16)
+            pieces += [mixed[:hdim, :rows], mixed[hdim:, rows:]]
+        add = dot(jnp.concatenate(pieces, axis=0), (pown, ppair)[side][...], TN)
+        total = add if total is None else total + add
+    part[...] = total
+    send[...] = total.astype(jnp.bfloat16)
+
+
+def merge_kernel(keep, x, part, got, pbias, gain, bias, *rest):
+    blocks, scratch = rest[-2 - keep], rest[-1]
     width = x.shape[1]
     value = x[...].astype(jnp.float32) + (part[...] + got[...].astype(jnp.float32)) + pbias[...]
     vit = value.astype(jnp.bfloat16)
-    if len(rest) == 2:
-        rest[0][...] = vit
+    if keep:
+        rest[-2][...] = vit
     normed = layer_norm(vit.astype(jnp.float32), gain[...], bias[...])
     count = x.shape[0] // 4
     lanes = scratch.shape[2]
@@ -123,8 +197,8 @@
     else:
         early = rest[0]
         chip = me // 2
-        out[pl.ds(pl.multiple_of(chip * 2 * count, 2 * count), 2 * count), :] = early[...]
-        start = (1 - chip) * 2 * count
+        out[pl.ds(pl.multiple_of((1 - chip) * 2 * count, 2 * count), 2 * count), :] = early[...]
+        start = chip * 2 * count
     core = me % 2
     out[pl.ds(pl.multiple_of(start + core * count, count), count), :] = hid[:count]
     out[pl.ds(pl.multiple_of(start + (1 - core) * count, count), count), :] = hid[count:]
@@ -158,70 +232,80 @@
         return lax.ppermute(value, "sp", [(i, i ^ bit) for i in range(4)])
 
     weight = qkv_weight.transpose(1, 2, 0).reshape(3 * local, width)
+    x_far = swap(patches, 2)
     x_pair = swap(patches, 1)
-    x_far = swap(patches, 2)
     w_pair = swap(weight, 1)
     p_pair = swap(proj_weight, 1)
-    x_farpair = swap(x_far, 1)
 
     quarter = hdim // 4
     inv = 1.0 / 10000.0 ** (jnp.arange(quarter, dtype=jnp.float32) * 2.0 / (hdim // 2))
-
-    def tables(blocks):
-        pos = jnp.concatenate(
-            [lax.dynamic_slice_in_dim(pos_ids, b * prow, prow, 1) for b in blocks], axis=1
-        ).astype(jnp.float32)
-        angle = jnp.concatenate([inv[:, None] * pos[0:1], inv[:, None] * pos[1:2]], axis=0)
-        return jnp.cos(angle), jnp.sin(angle)
+    pos = jnp.concatenate(
+        [lax.dynamic_slice_in_dim(pos_ids, (me ^ k) * prow, prow, 1) for k in range(4)], axis=1
+    ).astype(jnp.float32)
+    angle = jnp.concatenate([inv[:, None] * pos[0:1], inv[:, None] * pos[1:2]], axis=0)
+    cos, sin = jnp.cos(angle), jnp.sin(angle)
+    cos_near, cos_far = cos[:, : 2 * prow], cos[:, 2 * prow :]
+    sin_near, sin_far = sin[:, : 2 * prow], sin[:, 2 * prow :]
 
     row = lambda v: v.reshape(1, -1)
     qbias = qkv_bias.T
     both = 2 * local
+    tall = shape((both, 2 * prow))
     part_shape = (shape((prow, width), jnp.float32), shape((prow, width)))
-
-    def project(xa, xb, blocks, name):
-        cos, sin = tables(blocks)
-        outs = tuple(shape((both, 2 * prow)) for _ in range(3))
-        return call(
-            functools.partial(project_kernel, hdim), outs, 24 * MIB, 2 * 2 * prow * width * 3 * both, name
-        )(xa, xb, weight, w_pair, row(norm_gain), row(norm_bias), qbias, cos, sin)
-
-    ql, kl, vl = project(patches, x_pair, (me, me ^ 1), "near")
-    qr, kr, vr = project(x_far, x_farpair, (me ^ 2, me ^ 3), "far")
-
-    def attend(q, name):
-        return call(
-            functools.partial(attend_kernel, hdim, prow), part_shape, 24 * MIB, 4 * prow * 4 * prow * both, name
-        )(q, kl, kr, vl, vr, proj_weight, p_pair)
-
-    part1, send1 = attend(qr, "attend1")
+    mul = 2 * prow * width * local * 2
+    gain, nbias = row(norm_gain), row(norm_bias)
+
+    def norm(x, *after):
+        return pl.pallas_call(
+            norm_kernel,
+            out_shape=shape((prow, width)),
+            in_specs=[VMEM] * 3 + [ANY] * len(after),
+            compiler_params=pltpu.CompilerParams(vmem_limit_bytes=8 * MIB),
+            cost_estimate=pl.CostEstimate(flops=mul // 4, bytes_accessed=1 << 20, transcendentals=0),
+        )(x, gain, nbias, *after)
+
+    n_own = norm(patches)
+    n_pair = norm(x_pair)
+    q_near, k_near, v_near = call(
+        functools.partial(near_kernel, hdim), (tall, tall, tall), 24 * MIB, 6 * mul
+    )(n_own, n_pair, weight, w_pair, qbias, cos_near, sin_near)
+    state = tuple(shape((HEADS // 4, 2 * prow), jnp.float32) for _ in range(2))
+    tops, sums, outs = call(
+        functools.partial(first_kernel, hdim), state + (shape((both, prow), jnp.float32),), 24 * MIB, 2 * mul
+    )(q_near, k_near, v_near)
+
+    n_far = norm(x_far, tops)
+    n_farpair = swap(n_far, 1)
+    part0, send0, k_far, v_far = call(
+        functools.partial(far_kernel, hdim), part_shape + (tall, tall), 24 * MIB, 6 * mul
+    )(n_far, n_farpair, weight, w_pair, qbias, cos_far, sin_far, q_near, tops, sums, outs, proj_weight, p_pair)
+    got1 = swap(send0, 2)
+    part1, send1 = call(
+        functools.partial(late_kernel, hdim), part_shape, 24 * MIB, 6 * mul
+    )(n_far, weight, w_pair, qbias, cos_far, sin_far, k_near, v_near, k_far, v_far, proj_weight, p_pair)
     got0 = swap(send1, 2)
-    part0, send0 = attend(ql, "attend0")
-    got1 = swap(send0, 2)
-
-    def merge(x, part, got, outs, name):
+
+    pbias = row(proj_bias)
+
+    def merge(keep, x, part, got, outs, *after):
         return pl.pallas_call(
-            merge_kernel,
+            functools.partial(merge_kernel, keep),
             out_shape=outs,
+            in_specs=[VMEM] * 6 + [ANY] * len(after),
             scratch_shapes=[pltpu.VMEM((width // 128, prow, 128), jnp.float32)],
             compiler_params=pltpu.CompilerParams(vmem_limit_bytes=16 * MIB),
-            cost_estimate=pl.CostEstimate(flops=1 << 27, bytes_accessed=1 << 20, transcendentals=0),
-            name=name,
-        )(x, part, got, row(proj_bias), row(merge_gain), row(merge_bias))
+            cost_estimate=pl.CostEstimate(flops=mul // 4, bytes_accessed=1 << 20, transcendentals=0),
+        )(x, part, got, pbias, row(merge_gain), row(merge_bias), *after)
 
     bshape = shape((prow // 4, 4 * width))
-    blocks0, vit = merge(patches, part0, got0, (bshape, shape((prow, width))), "merge0")
-    pair0 = swap(blocks0, 1)
+    (blocks1,) = merge(0, x_far, part1, got1, (bshape,))
+    pair1 = swap(blocks1, 1)
     fc1 = pltpu.with_memory_space_constraint(fc1_weight, pltpu.VMEM)
     flops = 2 * prow // 2 * 4 * width * hidden
-    early = call(hidden_kernel, shape((prow // 2, hidden)), 24 * MIB, flops, "hidden0")(
-        blocks0, pair0, fc1, row(fc1_bias)
-    )
-    (blocks1,) = merge(x_far, part1, got1, (bshape,), "merge1")
-    pair1 = swap(blocks1, 1)
-    out = call(hidden_kernel, shape((prow, hidden)), 24 * MIB, flops, "hidden1")(
-        blocks1, pair1, fc1, row(fc1_bias), early
-    )
+    early = call(hidden_kernel, shape((prow // 2, hidden)), 24 * MIB, flops)(blocks1, pair1, fc1, row(fc1_bias))
+    blocks0, vit = merge(1, patches, part0, got0, (bshape, shape((prow, width))), early)
+    pair0 = swap(blocks0, 1)
+    out = call(hidden_kernel, shape((prow, hidden)), 24 * MIB, flops)(blocks0, pair0, fc1, row(fc1_bias), early)
     return vit, out
 
 

time: 51.3 us -> 49 us (0.955)
  waiting for transfers between devices: 17.3 us -> 15 us
  Pallas kernels: 21.7 us -> 23.6 us
  starting transfers between devices: 5.86 us -> 4.62 us
  local copies, waits for them, and re-layouts: 4.87 us -> 4.19 us
    ppermute x9, waiting for transfers between devices: 17.3 us -> 15 us  [swap(): return lax.ppermute(value, 'sp', [(i, i ^ bit) for i in range(4)])]
    pallas_call x8 -> x11, Pallas kernels: 21.7 us -> 23.6 us  [the longest x1 5.05 us: two_chips(): call(functools.partial(late_kernel, hdim), part_shape, 24 * MIB, 6 * mul)]
    ppermute x9, starting transfers between devices: 5.86 us -> 4.62 us  [swap(): return lax.ppermute(value, 'sp', [(i, i ^ bit) for i in range(4)])]
    unnamed x19 -> x25, local copies, waits for them, and re-layouts: 2.7 us -> 2.01 us
  transfers between devices with their start and end apart: 9 -> 9, of which waited for: 3 -> 5; matrix products, arithmetic and copies ran while one was open for 7% -> 7% of each run, Pallas kernels for 27% -> 29%
where the time goes in v2:
time: 49 us; the launch traced here: 48.7 us
  Pallas kernels  23.6 us (48%)
  waiting for transfers between devices  15 us (31%)
  starting transfers between devices  4.62 us (9%)
  local copies, waits for them, and re-layouts  4.19 us (9%)
  between operations  0.93 us (2%)
    ppermute x9, waiting for transfers between devices, swap(): return lax.ppermute(value, 'sp', [(i, i ^ bit) for i in range(4)])  15 us
    pallas_call x1, Pallas kernels, two_chips(): call(functools.partial(late_kernel, hdim), part_shape, 24 * MIB, 6 * mul)  5.05 us
    pallas_call x1, Pallas kernels, two_chips(): call(functools.partial(far_kernel, hdim), part_shape + (tall, tall), 24 *...  4.91 us
    ppermute x9, starting transfers between devices, swap(): return lax.ppermute(value, 'sp', [(i, i ^ bit) for i in range(4)])  4.62 us
    pallas_call x1, Pallas kernels, two_chips(): call(functools.partial(near_kernel, hdim), (tall, tall, tall), 24 * MIB,...  3.28 us
    pallas_call x1, Pallas kernels, two_chips(): call(hidden_kernel, shape((prow, hidden)), 24 * MIB, flops)  3.16 us
    pallas_call x1, Pallas kernels, two_chips(): call(hidden_kernel, shape((prow // 2, hidden)), 24 * MIB, flops)  2.45 us
    pallas_call x3, Pallas kernels, norm(): pl.pallas_call(norm_kernel, out_shape=shape((prow, width)), in_specs=[VME...  2.01 us
  transfers between devices with their start and end apart: 9, of which 5 were waited for; matrix products, arithmetic and copies ran while one was open for 7% of the time, Pallas kernels for 29%

profile of v2, /device:TPU:0, one launch (start us, length us, event | category | flops | bytes accessed | tf_op | source)
XLA Modules:
  0.0 48.7 jit_solution(11624793475012937978)
XLA Ops:
  0.6 0.0 copy-start
  0.6 0.6 %collective-permute-start.2 = (bf16[960,1280]{1,0:T(8,128)(2,1)}, bf16[960,1280]{1,0:T(8,128)(2,1)}, u32[]{:S(2)}, u32[]{:S(2)}) collective-permute-start(bf16[960,1280]{1,0:T(8,128)(2,1)} %bitcast.8), channel_id=1, source_target_pairs={{0,1},{1,0},{2,3},{3,2},{4,5},{5,4},{6,7},{7,6},{8,9},{9,8},{10,11... | collective-permute-start | bytes 7372808 | tf_op jit(solution)/shard_map/ppermute | solution.py:232
  1.2 0.1 collective-permute-start.1
  1.3 2.9 %collective-permute-start = (bf16[128,1280]{1,0:T(8,128)(2,1)}, bf16[128,1280]{1,0:T(8,128)(2,1)S(1)}, u32[]{:S(2)}, u32[]{:S(2)}) collective-permute-start(bf16[128,1280]{1,0:T(8,128)(2,1)} %x.3), channel_id=1, source_target_pairs={{0,2},{1,3},{2,0},{3,1},{4,6},{5,7},{6,4},{7,5},{8,10},{9,11},{10,... | collective-permute-start | bytes 983048 | tf_op jit(solution)/shard_map/ppermute | solution.py:232
  4.2 0.0 collective-permute-start.4
  4.2 0.7 %reshape.34.gain = f32[1,1280]{1,0:T(1,128)S(1)} reshape(f32[1280]{0:T(1024)} %param.14) | data formatting | bytes 10240 | tf_op jit(solution)/shard_map/reshape | solution.py:250
  4.9 0.7 %reshape.35.bias = f32[1,1280]{1,0:T(1,128)S(1)} reshape(f32[1280]{0:T(1024)} %param.15) | data formatting | bytes 10240 | tf_op jit(solution)/shard_map/reshape | solution.py:250
  5.6 1.0 %copy.14 = f32[3,1280]{0,1:T(8,128)S(1)} copy(f32[3,1280]{1,0:T(4,128)} %param.17) | data formatting | bytes 30720 | tf_op args[5]
  6.6 0.0 copy-start.2
  6.6 1.0 %copy-done.2 = bf16[128,1280]{1,0:T(8,128)(2,1)S(1)} copy-done((bf16[128,1280]{1,0:T(8,128)(2,1)S(1)}, bf16[128,1280]{1,0:T(8,128)(2,1)}, u32[]{:S(2)}) %copy-start.2) | copy-done | bytes 327704
  7.6 0.3 shard_map.131.xa
  7.9 0.7 %constant_dynamic-slice_fusion.3 = (s32[2,128]{1,0:T(2,128)S(1)}, s32[2,128]{1,0:T(2,128)S(1)}, s32[2,128]{1,0:T(2,128)S(1)}, s32[2,128]{1,0:T(2,128)S(1)}) fusion(s32[2,512]{1,0:T(2,128)} %param.13, s32[]{:T(128)S(6)} %select_n.12, s32[]{:T(128)S(6)} %select_n.13, s32[]{:T(128)S(6)} %select_n.15, s32[]{:T(128)S(6)} %select_n.14), kind=kLoop, calls=%fused_computation.9 | loop fusion | bytes 8208 | tf_op jit(solution)/shard_map/dynamic_slice | solution.py:243
  8.6 0.1 broadcast_multiply_fusion.1
  8.7 0.3 fusion
  9.0 0.0 slice-start
  9.1 0.0 collective-permute-done.1.x
  9.1 1.4 %shard_map.132.xb = bf16[128,1280]{1,0:T(8,128)(2,1)S(1)} custom-call(bf16[128,1280]{1,0:T(8,128)(2,1)} %collective-permute-done.1.x, f32[1,1280]{1,0:T(1,128)S(1)} %reshape.34.gain, f32[1,1280]{1,0:T(1,128)S(1)} %reshape.35.bias), custom_call_target="tpu_custom_call" | custom-call | flops 52428800 | bytes 1048576 | tf_op jit(solution)/shard_map/pallas_call | solution.py:259
  10.5 0.0 collective-permute-done.2.wpair
  10.5 0.0 copy-start.1
  10.5 0.0 copy-done
  10.5 0.0 slice-start.1
  10.5 3.3 %shard_map.133 = (bf16[640,256]{1,0:T(8,128)(2,1)S(1)}, bf16[640,256]{1,0:T(8,128)(2,1)S(1)}, bf16[640,256]{1,0:T(8,128)(2,1)S(1)}) custom-call(bf16[128,1280]{1,0:T(8,128)(2,1)S(1)} %shard_map.131.xa, bf16[128,1280]{1,0:T(8,128)(2,1)S(1)} %shard_map.132.xb, bf16[960,1280]{1,0:T(8,128)(2,1)S(1)} %bitcast.9, bf16[960,1280]{1,0:T(8,128)(2,1)} %collective-permute-done.2.wpair, ...), custom_call_target="tpu_custom_call" | custom-call | flops 1258291200 | bytes 1048576 | tf_op jit(solution)/shard_map/pallas_call | solution.py:269
  13.8 1.4 %shard_map.134 = (f32[4,256]{1,0:T(4,128)S(1)}, f32[4,256]{1,0:T(4,128)S(1)}, f32[640,128]{1,0:T(8,128)S(1)}) custom-call(bf16[640,256]{1,0:T(8,128)(2,1)S(1)} %get-tuple-element.16.q, bf16[640,256]{1,0:T(8,128)(2,1)S(1)} %get-tuple-element.17.k.kn, bf16[640,256]{1,0:T(8,128)(2,1)S(1)} %get-tuple-element.18.v.vn), custom_call_target="tpu_custom_call" | custom-call | flops 419430400 | bytes 1048576 | tf_op jit(solution)/shard_map/pallas_call | solution.py:273
  15.2 0.0 collective-permute-done.x
  15.2 0.3 shard_map.135.xa.x
  15.5 0.6 %collective-permute-start.3 = (bf16[128,1280]{1,0:T(8,128)(2,1)S(1)}, bf16[128,1280]{1,0:T(8,128)(2,1)S(1)}, u32[]{:S(2)}, u32[]{:S(2)}) collective-permute-start(bf16[128,1280]{1,0:T(8,128)(2,1)S(1)} %shard_map.135.xa.x), channel_id=1, source_target_pairs={{0,1},{1,0},{2,3},{3,2},{4,5},{5,4},{6,7},{7,6},{8,9},{9,8},{10,11... | collective-permute-start | bytes 983048 | tf_op jit(solution)/shard_map/ppermute | solution.py:232
  16.1 0.0 collective-permute-done.4.ppair
  16.1 1.3 %collective-permute-done.3.xb = bf16[128,1280]{1,0:T(8,128)(2,1)S(1)} collective-permute-done((bf16[128,1280]{1,0:T(8,128)(2,1)S(1)}, bf16[128,1280]{1,0:T(8,128)(2,1)S(1)}, u32[]{:S(2)}, u32[]{:S(2)}) %collective-permute-start.3) | collective-permute-done | bytes 327712 | tf_op jit(solution)/shard_map/ppermute | solution.py:232
  17.3 0.0 copy-done.1
  17.3 0.0 copy-start.4
  17.3 0.0 copy-start.5
  17.3 0.0 copy-start.6
  17.3 0.0 slice-start.2
  17.4 4.9 %shard_map.136 = (f32[128,1280]{1,0:T(8,128)S(1)}, bf16[128,1280]{1,0:T(8,128)(2,1)S(1)}, bf16[640,256]{1,0:T(8,128)(2,1)S(1)}, bf16[640,256]{1,0:T(8,128)(2,1)S(1)}) custom-call(bf16[128,1280]{1,0:T(8,128)(2,1)S(1)} %shard_map.135.xa.x, bf16[128,1280]{1,0:T(8,128)(2,1)S(1)} %collective-permute-done.3.xb, bf16[960,1280]{1,0:T(8,128)(2,1)S(1)} %bitcast.10, ...), custom_call_target="tpu_custom_call" | custom-call | flops 1258291200 | bytes 1048576 | tf_op jit(solution)/shard_map/pallas_call | solution.py:279
  22.3 0.1 collective-permute-start.6
  22.4 0.0 copy-done.4
  22.4 0.0 copy-done.5
  22.4 0.0 copy-done.6
  22.4 0.0 copy-start.7
  22.4 0.0 slice-start.3
  22.4 5.1 %shard_map.137 = (f32[128,1280]{1,0:T(8,128)S(1)}, bf16[128,1280]{1,0:T(8,128)(2,1)S(1)}) custom-call(bf16[128,1280]{1,0:T(8,128)(2,1)S(1)} %shard_map.135.xa.x, bf16[960,1280]{1,0:T(8,128)(2,1)S(1)} %bitcast.11, bf16[960,1280]{1,0:T(8,128)(2,1)} %collective-permute-done.2.wpair, f32[1280,3]{1,0:T(8,128)S(1)} %bitcast.14, ...), custom_call_target="tpu_custom_call" | custom-call | flops 1258291200 | bytes 1048576 | tf_op jit(solution)/shard_map/pallas_call | solution.py:283
  27.5 4.8 %collective-permute-done.6.got = bf16[128,1280]{1,0:T(8,128)(2,1)S(1)} collective-permute-done((bf16[128,1280]{1,0:T(8,128)(2,1)S(1)}, bf16[128,1280]{1,0:T(8,128)(2,1)S(1)}, u32[]{:S(2)}, u32[]{:S(2)}) %collective-permute-start.6) | collective-permute-done | bytes 327712 | tf_op jit(solution)/shard_map/ppermute | solution.py:232
  32.3 0.4 shard_map.138.own
  32.8 0.1 collective-permute-start.7
  32.8 0.4 collective-permute-start.5
  33.2 0.0 copy-done.7
  33.2 0.0 copy-start.3
  33.2 1.2 %collective-permute-done.7.pair = bf16[32,5120]{1,0:T(8,128)(2,1)S(1)} collective-permute-done((bf16[32,5120]{1,0:T(8,128)(2,1)S(1)}, bf16[32,5120]{1,0:T(8,128)(2,1)S(1)}, u32[]{:S(2)}, u32[]{:S(2)}) %collective-permute-start.7) | collective-permute-done | bytes 327712 | tf_op jit(solution)/shard_map/ppermute | solution.py:232
  34.5 0.0 slice-done
  34.5 0.0 slice-done.1
  34.5 0.0 slice-done.2
  34.5 0.0 slice-done.3
  34.5 2.4 %shard_map.139.rest_0_ = bf16[64,1280]{1,0:T(8,128)(2,1)S(1)} custom-call(bf16[32,5120]{1,0:T(8,128)(2,1)S(1)} %shard_map.138.own, bf16[32,5120]{1,0:T(8,128)(2,1)S(1)} %collective-permute-done.7.pair, bf16[5120,1280]{1,0:T(8,128)(2,1)S(1)} %bitcast.7, f32[1,1280]{1,0:T(1,128)S(1)} %reshape.40.bias), custom_call_target="tpu_custom_call" | custom-call | flops 838860800 | bytes 1048576 | tf_op jit(solution)/shard_map/pallas_call | solution.py:305
  36.9 6.0 %collective-permute-done.5.got = bf16[128,1280]{1,0:T(8,128)(2,1)S(1)} collective-permute-done((bf16[128,1280]{1,0:T(8,128)(2,1)S(1)}, bf16[128,1280]{1,0:T(8,128)(2,1)S(1)}, u32[]{:S(2)}, u32[]{:S(2)}) %collective-permute-start.5) | collective-permute-done | bytes 327712 | tf_op jit(solution)/shard_map/ppermute | solution.py:232
  43.0 0.0 copy-done.3
  43.0 0.9 %shard_map.140 = (bf16[32,5120]{1,0:T(8,128)(2,1)S(1)}, bf16[128,1280]{1,0:T(8,128)(2,1)}) custom-call(bf16[128,1280]{1,0:T(8,128)(2,1)S(1)} %copy-done.3, f32[128,1280]{1,0:T(8,128)S(1)} %get-tuple-element.22.part, bf16[128,1280]{1,0:T(8,128)(2,1)S(1)} %collective-permute-done.5.got, f32[1,1280]{1,0:T(1,128)S(1)} %reshape.37.pbias, ...), custom_call_target="tpu_custom_call" | custom-call | flops 52428800 | bytes 1048576 | tf_op jit(solution)/shard_map/pallas_call | solution.py:291
  43.9 0.0 collective-permute-start.8
  43.9 1.6 %collective-permute-done.8.pair = bf16[32,5120]{1,0:T(8,128)(2,1)S(1)} collective-permute-done((bf16[32,5120]{1,0:T(8,128)(2,1)S(1)}, bf16[32,5120]{1,0:T(8,128)(2,1)S(1)}, u32[]{:S(2)}, u32[]{:S(2)}) %collective-permute-start.8) | collective-permute-done | bytes 327712 | tf_op jit(solution)/shard_map/ppermute | solution.py:232
  45.5 3.2 %shard_map.141 = bf16[128,1280]{1,0:T(8,128)(2,1)} custom-call(bf16[32,5120]{1,0:T(8,128)(2,1)S(1)} %get-tuple-element.29.own, bf16[32,5120]{1,0:T(8,128)(2,1)S(1)} %collective-permute-done.8.pair, bf16[5120,1280]{1,0:T(8,128)(2,1)S(1)} %bitcast.7, f32[1,1280]{1,0:T(1,128)S(1)} %reshape.40.bias, bf16[64,1280]{1,0:T(8,128)(2,1)S(1)} %shard_map.139.rest_0_), custom_call_target="tpu_custom_call" | custom-call | flops 838860800 | bytes 1048576 | tf_op jit(solution)/shard_map/pallas_call | solution.py:308
  (9 shorter events, 0.1 us)
Async XLA Ops:
  0.6 9.9 %copy-start = (bf16[1280,3,320]{0,2,1:T(8,128)(2,1)S(1)}, bf16[1280,3,320]{0,2,1:T(8,128)(2,1)}, u32[]{:S(2)}) copy-start(bf16[1280,3,320]{0,2,1:T(8,128)(2,1)} %param.16) | copy-start | bytes 7372804
  0.6 9.9 %collective-permute-start.2 = (bf16[960,1280]{1,0:T(8,128)(2,1)}, bf16[960,1280]{1,0:T(8,128)(2,1)}, u32[]{:S(2)}, u32[]{:S(2)}) collective-permute-start(bf16[960,1280]{1,0:T(8,128)(2,1)} %bitcast.8), channel_id=1, source_target_pairs={{0,1},{1,0},{2,3},{3,2},{4,5},{5,4},{6,7},{7,6},{8,9},{9,8},{10,11... | collective-permute-start | bytes 7372808 | tf_op jit(solution)/shard_map/ppermute | solution.py:232
  1.2 7.9 %collective-permute-start.1 = (bf16[128,1280]{1,0:T(8,128)(2,1)}, bf16[128,1280]{1,0:T(8,128)(2,1)}, u32[]{:S(2)}, u32[]{:S(2)}) collective-permute-start(bf16[128,1280]{1,0:T(8,128)(2,1)} %x.3), channel_id=1, source_target_pairs={{0,1},{1,0},{2,3},{3,2},{4,5},{5,4},{6,7},{7,6},{8,9},{9,8},{10,11... | collective-permute-start | bytes 983048 | tf_op jit(solution)/shard_map/ppermute | solution.py:232
  1.3 13.9 %collective-permute-start = (bf16[128,1280]{1,0:T(8,128)(2,1)}, bf16[128,1280]{1,0:T(8,128)(2,1)S(1)}, u32[]{:S(2)}, u32[]{:S(2)}) collective-permute-start(bf16[128,1280]{1,0:T(8,128)(2,1)} %x.3), channel_id=1, source_target_pairs={{0,2},{1,3},{2,0},{3,1},{4,6},{5,7},{6,4},{7,5},{8,10},{9,11},{10,... | collective-permute-start | bytes 983048 | tf_op jit(solution)/shard_map/ppermute | solution.py:232
  4.2 11.9 %collective-permute-start.4 = (bf16[320,1280]{1,0:T(8,128)(2,1)}, bf16[320,1280]{1,0:T(8,128)(2,1)}, u32[]{:S(2)}, u32[]{:S(2)}) collective-permute-start(bf16[320,1280]{1,0:T(8,128)(2,1)} %pown.3), channel_id=1, source_target_pairs={{0,1},{1,0},{2,3},{3,2},{4,5},{5,4},{6,7},{7,6},{8,9},{9,8},{10,11... | collective-permute-start | bytes 2457608 | tf_op jit(solution)/shard_map/ppermute | solution.py:232
  6.6 1.0 %copy-start.2 = (bf16[128,1280]{1,0:T(8,128)(2,1)S(1)}, bf16[128,1280]{1,0:T(8,128)(2,1)}, u32[]{:S(2)}) copy-start(bf16[128,1280]{1,0:T(8,128)(2,1)} %x.3) | copy-start | bytes 983044
  9.0 25.4 %slice-start = ((s8[13107200]{0:T(1024)(128)(4,1)}), s8[4194304]{0:T(1024)(128)(4,1)S(1)}, s32[]{:S(2)}) async-start(s8[13107200]{0:T(1024)(128)(4,1)} %bitcast.6), calls=%async_computation | async-start | bytes 8388608
  10.5 6.8 %copy-start.1 = (bf16[320,1280]{1,0:T(8,128)(2,1)S(1)}, bf16[320,1280]{1,0:T(8,128)(2,1)}, u32[]{:S(2)}) copy-start(bf16[320,1280]{1,0:T(8,128)(2,1)} %pown.3) | copy-start | bytes 2457604
  10.5 23.9 %slice-start.1 = ((s8[13107200]{0:T(1024)(128)(4,1)}), s8[4194304]{0:T(1024)(128)(4,1)S(1)}, s32[]{:S(2)}) async-start(s8[13107200]{0:T(1024)(128)(4,1)} %bitcast.6), calls=%async_computation.1 | async-start | bytes 8388608
  15.5 1.8 %collective-permute-start.3 = (bf16[128,1280]{1,0:T(8,128)(2,1)S(1)}, bf16[128,1280]{1,0:T(8,128)(2,1)S(1)}, u32[]{:S(2)}, u32[]{:S(2)}) collective-permute-start(bf16[128,1280]{1,0:T(8,128)(2,1)S(1)} %shard_map.135.xa.x), channel_id=1, source_target_pairs={{0,1},{1,0},{2,3},{3,2},{4,5},{5,4},{6,7},{7,6},{8,9},{9,8},{10,11... | collective-permute-start | bytes 983048 | tf_op jit(solution)/shard_map/ppermute | solution.py:232
  17.3 5.0 %copy-start.4 = (f32[1280]{0:T(1024)S(1)}, f32[1280]{0:T(1024)}, u32[]{:S(2)}) copy-start(f32[1280]{0:T(1024)} %param.19) | copy-start | bytes 15364
  17.3 5.0 %copy-start.5 = (f32[1280]{0:T(1024)S(1)}, f32[1280]{0:T(1024)}, u32[]{:S(2)}) copy-start(f32[1280]{0:T(1024)} %param.20) | copy-start | bytes 15364
  17.3 5.1 %copy-start.6 = (f32[1280]{0:T(1024)S(1)}, f32[1280]{0:T(1024)}, u32[]{:S(2)}) copy-start(f32[1280]{0:T(1024)} %param.21) | copy-start | bytes 15364
  17.3 17.1 %slice-start.2 = ((s8[13107200]{0:T(1024)(128)(4,1)}), s8[4194304]{0:T(1024)(128)(4,1)S(1)}, s32[]{:S(2)}) async-start(s8[13107200]{0:T(1024)(128)(4,1)} %bitcast.6), calls=%async_computation.2 | async-start | bytes 8388608
  22.3 10.1 %collective-permute-start.6 = (bf16[128,1280]{1,0:T(8,128)(2,1)S(1)}, bf16[128,1280]{1,0:T(8,128)(2,1)S(1)}, u32[]{:S(2)}, u32[]{:S(2)}) collective-permute-start(bf16[128,1280]{1,0:T(8,128)(2,1)S(1)} %get-tuple-element.27), channel_id=1, source_target_pairs={{0,2},{1,3},{2,0},{3,1},{4,6},{5,7},{6,4},{7,5},{8,10},{9,11},{10,... | collective-permute-start | bytes 983048 | tf_op jit(solution)/shard_map/ppermute | solution.py:232
  22.4 10.8 %copy-start.7 = (f32[1280]{0:T(1024)S(1)}, f32[1280]{0:T(1024)}, u32[]{:S(2)}) copy-start(f32[1280]{0:T(1024)} %param.23) | copy-start | bytes 15364
  22.4 12.0 %slice-start.3 = ((s8[13107200]{0:T(1024)(128)(4,1)}), s8[524288]{0:T(1024)(128)(4,1)S(1)}, s32[]{:S(2)}) async-start(s8[13107200]{0:T(1024)(128)(4,1)} %bitcast.6), calls=%async_computation.3 | async-start | bytes 1048576
  32.8 1.7 %collective-permute-start.7 = (bf16[32,5120]{1,0:T(8,128)(2,1)S(1)}, bf16[32,5120]{1,0:T(8,128)(2,1)S(1)}, u32[]{:S(2)}, u32[]{:S(2)}) collective-permute-start(bf16[32,5120]{1,0:T(8,128)(2,1)S(1)} %shard_map.138.own), channel_id=1, source_target_pairs={{0,1},{1,0},{2,3},{3,2},{4,5},{5,4},{6,7},{7,6},{8,9},{9,8},{10,11... | collective-permute-start | bytes 983048 | tf_op jit(solution)/shard_map/ppermute | solution.py:232
  32.8 10.1 %collective-permute-start.5 = (bf16[128,1280]{1,0:T(8,128)(2,1)S(1)}, bf16[128,1280]{1,0:T(8,128)(2,1)S(1)}, u32[]{:S(2)}, u32[]{:S(2)}) collective-permute-start(bf16[128,1280]{1,0:T(8,128)(2,1)S(1)} %get-tuple-element.25), channel_id=1, source_target_pairs={{0,2},{1,3},{2,0},{3,1},{4,6},{5,7},{6,4},{7,5},{8,10},{9,11},{10,... | collective-permute-start | bytes 983048 | tf_op jit(solution)/shard_map/ppermute | solution.py:232
  33.2 9.8 %copy-start.3 = (bf16[128,1280]{1,0:T(8,128)(2,1)S(1)}, bf16[128,1280]{1,0:T(8,128)(2,1)}, u32[]{:S(2)}) copy-start(bf16[128,1280]{1,0:T(8,128)(2,1)} %x.3) | copy-start | bytes 983044
  43.9 1.6 %collective-permute-start.8 = (bf16[32,5120]{1,0:T(8,128)(2,1)S(1)}, bf16[32,5120]{1,0:T(8,128)(2,1)S(1)}, u32[]{:S(2)}, u32[]{:S(2)}) collective-permute-start(bf16[32,5120]{1,0:T(8,128)(2,1)S(1)} %get-tuple-element.29.own), channel_id=1, source_target_pairs={{0,1},{1,0},{2,3},{3,2},{4,5},{5,4},{6,7},{7,6},{8,9},{9,8},{10,11... | collective-permute-start | bytes 983048 | tf_op jit(solution)/shard_map/ppermute | solution.py:232

commit v3 on v2

--- a/solution.py
+++ b/solution.py
@@ -39,13 +39,42 @@
     )
 
 
-def norm_kernel(x, gain, bias, *rest):
+def setup_kernel(hdim, x, pos, qkv_bias, *rest):
+    vectors, (normed, rows, qcol, cosine, sine) = rest[:-5], rest[-5:]
+    width = x.shape[1]
+    prow = x.shape[0]
+    me = lax.axis_index("sp")
+    rows[...] = jnp.zeros_like(rows)
+    for at, vector in enumerate(vectors):
+        rows[at : at + 1, :] = vector[...].reshape(1, width)
+    cube = jnp.concatenate([qkv_bias[...], jnp.zeros((5, width), jnp.float32)], axis=0)
+    qcol[...] = cube.T
+    quarter = hdim // 4
+    feature = lax.broadcasted_iota(jnp.int32, (2 * quarter, prow), 0)
+    second = feature >= quarter
+    power = jnp.where(second, feature - quarter, feature).astype(jnp.float32)
+    inv = jnp.exp(power * (-2.0 * math.log(10000.0) / (hdim // 2)))
+    for k in range(4):
+        at = pl.ds(pl.multiple_of((me ^ k) * prow, prow), prow)
+        place = jnp.where(second, pos[1:2, at], pos[0:1, at]).astype(jnp.float32)
+        angle = place * inv
+        cosine[:, k * prow : (k + 1) * prow] = jnp.cos(angle)
+        sine[:, k * prow : (k + 1) * prow] = jnp.sin(angle)
+    value = layer_norm(x[...].astype(jnp.float32), rows[0:1, :], rows[1:2, :])
+    normed[...] = value.astype(jnp.bfloat16)
+
+
+def copy_kernel(x, out):
+    out[...] = x[...]
+
+
+def norm_kernel(x, rows, *rest):
     out = rest[-1]
-    out[...] = layer_norm(x[...].astype(jnp.float32), gain[...], bias[...]).astype(jnp.bfloat16)
-
-
-def column(qbias, owner, local, c):
-    return qbias[pl.ds(pl.multiple_of(owner * local, 8), local), c : c + 1]
+    out[...] = layer_norm(x[...].astype(jnp.float32), rows[0:1, :], rows[1:2, :]).astype(jnp.bfloat16)
+
+
+def column(qcol, owner, local, c):
+    return qcol[pl.ds(pl.multiple_of(owner * local, 8), local), c : c + 1]
 
 
 def rotated(raw, cos, sin, hdim):
@@ -66,20 +95,27 @@
     return jnp.concatenate(rows, axis=0)
 
 
-def near_kernel(hdim, xa, xb, wown, wpair, qbias, cosine, sine, qout, kout, vout):
+def near_kernel(hdim, xa, xb, wown, wfrom, pfrom, qcol, cosine, sine, qout, kout, vout, wpair, ppair, sems):
     local = wown.shape[0] // 3
     rows = xa.shape[0]
     me = lax.axis_index("sp")
+    wcopy = pltpu.make_async_copy(wfrom, wpair, sems.at[0])
+    pcopy = pltpu.make_async_copy(pfrom, ppair, sems.at[1])
+    wcopy.start()
+    pcopy.start()
     normed = jnp.concatenate([xa[...], xb[...]], axis=0)
-    cos, sin = cosine[...], sine[...]
+    cos, sin = cosine[:, : 2 * rows], sine[:, : 2 * rows]
     for side, weight in enumerate((wown, wpair)):
+        if side == 1:
+            wcopy.wait()
         owner = me ^ side
         base = slice(side * local, (side + 1) * local)
-        part = lambda c: dot(weight[c * local : (c + 1) * local, :], normed, NT) + column(qbias, owner, local, c)
-        query = dot(weight[0:local, :], normed[:rows], NT) + column(qbias, owner, local, 0)
+        query = dot(weight[0:local, :], normed[:rows], NT) + column(qcol, owner, local, 0)
         qout[base, :] = paired(rotated(query, cos[:, :rows], sin[:, :rows], hdim), hdim)
-        kout[base, :] = rotated(part(1), cos, sin, hdim)
-        vout[base, :] = part(2).astype(jnp.bfloat16)
+        keyval = dot(weight[local:, :], normed, NT)
+        kout[base, :] = rotated(keyval[:local] + column(qcol, owner, local, 1), cos, sin, hdim)
+        vout[base, :] = (keyval[local:] + column(qcol, owner, local, 2)).astype(jnp.bfloat16)
+    pcopy.wait()
 
 
 def first_kernel(hdim, q, k, v, tops, sums, outs):
@@ -97,21 +133,20 @@
         outs[(2 * p + 1) * hdim : 2 * (p + 1) * hdim, :] = total[hdim:, rows:]
 
 
-def far_kernel(hdim, xa, xb, wown, wpair, qbias, cosine, sine, q, tops, sums, outs, pown, ppair, part, send, kout, vout):
+def far_kernel(hdim, xa, xb, wown, wpair, qcol, cosine, sine, q, tops, sums, outs, pown, ppair, part, send, kout, vout):
     scale = math.log2(math.e) / math.sqrt(hdim)
     local = wown.shape[0] // 3
     rows = xa.shape[0]
     me = lax.axis_index("sp")
     normed = jnp.concatenate([xa[...], xb[...]], axis=0)
-    cos, sin = cosine[...], sine[...]
+    cos, sin = cosine[:, 2 * rows :], sine[:, 2 * rows :]
     total = None
     for side, weight in enumerate((wown, wpair)):
         owner = me ^ side
         base = slice(side * local, (side + 1) * local)
-        key = rotated(
-            dot(weight[local : 2 * local, :], normed, NT) + column(qbias, owner, local, 1), cos, sin, hdim
-        )
-        value = (dot(weight[2 * local :, :], normed, NT) + column(qbias, owner, local, 2)).astype(jnp.bfloat16)
+        keyval = dot(weight[local:, :], normed, NT)
+        key = rotated(keyval[:local] + column(qcol, owner, local, 1), cos, sin, hdim)
+        value = (keyval[local:] + column(qcol, owner, local, 2)).astype(jnp.bfloat16)
         kout[base, :] = key
         vout[base, :] = value
         pieces = []
@@ -137,15 +172,16 @@
     send[...] = total.astype(jnp.bfloat16)
 
 
-def late_kernel(hdim, x, wown, wpair, qbias, cosine, sine, kn, vn, kf, vf, pown, ppair, part, send):
+def late_kernel(hdim, x, wown, wpair, qcol, cosine, sine, kn, vn, kf, vf, pown, ppair, part, send):
     scale = math.log2(math.e) / math.sqrt(hdim)
     local = wown.shape[0] // 3
     rows = x.shape[0]
     me = lax.axis_index("sp")
     total = None
     for side, weight in enumerate((wown, wpair)):
-        query = dot(weight[:local, :], x[...], NT) + column(qbias, me ^ side, local, 0)
-        query = paired(rotated(query, cosine[:, :rows], sine[:, :rows], hdim), hdim)
+        query = dot(weight[:local, :], x[...], NT) + column(qcol, me ^ side, local, 0)
+        far = slice(2 * rows, 3 * rows)
+        query = paired(rotated(query, cosine[:, far], sine[:, far], hdim), hdim)
         pieces = []
         for at in range(0, local, 2 * hdim):
             f = slice(side * local + at, side * local + at + 2 * hdim)
@@ -165,14 +201,13 @@
     send[...] = total.astype(jnp.bfloat16)
 
 
-def merge_kernel(keep, x, part, got, pbias, gain, bias, *rest):
-    blocks, scratch = rest[-2 - keep], rest[-1]
+def merge_kernel(x, part, got, rows, *rest):
+    blocks, vit, scratch = rest[-3:]
     width = x.shape[1]
-    value = x[...].astype(jnp.float32) + (part[...] + got[...].astype(jnp.float32)) + pbias[...]
-    vit = value.astype(jnp.bfloat16)
-    if keep:
-        rest[-2][...] = vit
-    normed = layer_norm(vit.astype(jnp.float32), gain[...], bias[...])
+    value = x[...].astype(jnp.float32) + (part[...] + got[...].astype(jnp.float32)) + rows[2:3, :]
+    rounded = value.astype(jnp.bfloat16)
+    vit[...] = rounded
+    normed = layer_norm(rounded.astype(jnp.float32), rows[3:4, :], rows[4:5, :])
     count = x.shape[0] // 4
     lanes = scratch.shape[2]
     for t in range(width // lanes):
@@ -186,22 +221,36 @@
     return 0.5 * v * (1.0 + lax.erf(v * math.sqrt(0.5)))
 
 
-def hidden_kernel(own, pair, weight, bias, *rest):
-    out = rest[-1]
+def hidden_kernel(last, own, pair, weight, rows, *rest):
     me = lax.axis_index("sp")
+    chip, core = me // 2, me % 2
     count = own.shape[0]
+    if last:
+        vit, _, out, vout, stage, sems = rest
+        start = chip * 2 * count
+        vcopy = pltpu.make_async_copy(vit, vout, sems.at[2 * stage.shape[0]])
+        vcopy.start()
+    else:
+        out, stage, sems = rest
+        start = (1 - chip) * 2 * count
     both = jnp.concatenate([own[...], pair[...]], axis=0)
-    hid = gelu(dot(both, weight[...], NN) + bias[...]).astype(jnp.bfloat16)
-    if len(rest) == 1:
-        start = 0
-    else:
-        early = rest[0]
-        chip = me // 2
-        out[pl.ds(pl.multiple_of((1 - chip) * 2 * count, 2 * count), 2 * count), :] = early[...]
-        start = chip * 2 * count
-    core = me % 2
-    out[pl.ds(pl.multiple_of(start + core * count, count), count), :] = hid[:count]
-    out[pl.ds(pl.multiple_of(start + (1 - core) * count, count), count), :] = hid[count:]
+    step = stage.shape[2]
+    copies = []
+    for n in range(stage.shape[0]):
+        cols = slice(n * step, (n + 1) * step)
+        hid = gelu(dot(both, weight[:, cols], NN) + rows[5:6, cols]).astype(jnp.bfloat16)
+        stage[n] = hid
+        for half, place in enumerate((core, 1 - core)):
+            at = pl.ds(pl.multiple_of(start + place * count, count), count)
+            copy = pltpu.make_async_copy(
+                stage.at[n, pl.ds(half * count, count)], out.at[at, pl.ds(n * step, step)], sems.at[2 * n + half]
+            )
+            copy.start()
+            copies.append(copy)
+    for copy in copies:
+        copy.wait()
+    if last:
+        vcopy.wait()
 
 
 def shape(dims, dtype=jnp.bfloat16):
@@ -222,7 +271,6 @@
     fc1_weight,
     fc1_bias,
 ):
-    me = lax.axis_index("sp")
     prow, width = patches.shape
     hdim = width // HEADS
     local = qkv_weight.shape[2]
@@ -237,76 +285,96 @@
     w_pair = swap(weight, 1)
     p_pair = swap(proj_weight, 1)
 
-    quarter = hdim // 4
-    inv = 1.0 / 10000.0 ** (jnp.arange(quarter, dtype=jnp.float32) * 2.0 / (hdim // 2))
-    pos = jnp.concatenate(
-        [lax.dynamic_slice_in_dim(pos_ids, (me ^ k) * prow, prow, 1) for k in range(4)], axis=1
-    ).astype(jnp.float32)
-    angle = jnp.concatenate([inv[:, None] * pos[0:1], inv[:, None] * pos[1:2]], axis=0)
-    cos, sin = jnp.cos(angle), jnp.sin(angle)
-    cos_near, cos_far = cos[:, : 2 * prow], cos[:, 2 * prow :]
-    sin_near, sin_far = sin[:, : 2 * prow], sin[:, 2 * prow :]
-
-    row = lambda v: v.reshape(1, -1)
-    qbias = qkv_bias.T
     both = 2 * local
     tall = shape((both, 2 * prow))
     part_shape = (shape((prow, width), jnp.float32), shape((prow, width)))
     mul = 2 * prow * width * local * 2
-    gain, nbias = row(norm_gain), row(norm_bias)
+    table = shape((hdim // 2, 4 * prow), jnp.float32)
+
+    n_own, rows, qcol, cos, sin = call(
+        functools.partial(setup_kernel, hdim),
+        (shape((prow, width)), shape((8, width), jnp.float32), shape((width, 8), jnp.float32), table, table),
+        8 * MIB,
+        mul,
+    )(patches, pos_ids, qkv_bias, norm_gain, norm_bias, proj_bias, merge_gain, merge_bias, fc1_bias)
 
     def norm(x, *after):
         return pl.pallas_call(
             norm_kernel,
             out_shape=shape((prow, width)),
-            in_specs=[VMEM] * 3 + [ANY] * len(after),
+            in_specs=[VMEM] * 2 + [ANY] * len(after),
             compiler_params=pltpu.CompilerParams(vmem_limit_bytes=8 * MIB),
             cost_estimate=pl.CostEstimate(flops=mul // 4, bytes_accessed=1 << 20, transcendentals=0),
-        )(x, gain, nbias, *after)
-
-    n_own = norm(patches)
+        )(x, rows, *after)
+
     n_pair = norm(x_pair)
-    q_near, k_near, v_near = call(
-        functools.partial(near_kernel, hdim), (tall, tall, tall), 24 * MIB, 6 * mul
-    )(n_own, n_pair, weight, w_pair, qbias, cos_near, sin_near)
+    q_near, k_near, v_near, w_vmem, p_vmem = pl.pallas_call(
+        functools.partial(near_kernel, hdim),
+        out_shape=(tall, tall, tall, pltpu.VMEM(weight.shape, weight.dtype), pltpu.VMEM(proj_weight.shape, weight.dtype)),
+        in_specs=[VMEM] * 3 + [ANY] * 2 + [VMEM] * 3,
+        out_specs=[VMEM] * 5,
+        scratch_shapes=[pltpu.SemaphoreType.DMA((2,))],
+        compiler_params=pltpu.CompilerParams(vmem_limit_bytes=16 * MIB),
+        cost_estimate=pl.CostEstimate(flops=6 * mul, bytes_accessed=1 << 23, transcendentals=0),
+        name="near",
+    )(n_own, n_pair, weight, w_pair, p_pair, qcol, cos, sin)
     state = tuple(shape((HEADS // 4, 2 * prow), jnp.float32) for _ in range(2))
     tops, sums, outs = call(
-        functools.partial(first_kernel, hdim), state + (shape((both, prow), jnp.float32),), 24 * MIB, 2 * mul
+        functools.partial(first_kernel, hdim), state + (shape((both, prow), jnp.float32),), 16 * MIB, 2 * mul
     )(q_near, k_near, v_near)
 
     n_far = norm(x_far, tops)
     n_farpair = swap(n_far, 1)
     part0, send0, k_far, v_far = call(
-        functools.partial(far_kernel, hdim), part_shape + (tall, tall), 24 * MIB, 6 * mul
-    )(n_far, n_farpair, weight, w_pair, qbias, cos_far, sin_far, q_near, tops, sums, outs, proj_weight, p_pair)
+        functools.partial(far_kernel, hdim), part_shape + (tall, tall), 16 * MIB, 6 * mul
+    )(n_far, n_farpair, weight, w_vmem, qcol, cos, sin, q_near, tops, sums, outs, proj_weight, p_vmem)
     got1 = swap(send0, 2)
     part1, send1 = call(
-        functools.partial(late_kernel, hdim), part_shape, 24 * MIB, 6 * mul
-    )(n_far, weight, w_pair, qbias, cos_far, sin_far, k_near, v_near, k_far, v_far, proj_weight, p_pair)
+        functools.partial(late_kernel, hdim), part_shape, 16 * MIB, 6 * mul
+    )(n_far, weight, w_vmem, qcol, cos, sin, k_near, v_near, k_far, v_far, proj_weight, p_vmem)
     got0 = swap(send1, 2)
 
-    pbias = row(proj_bias)
-
-    def merge(keep, x, part, got, outs, *after):
+    late_rows = call(copy_kernel, shape(rows.shape, rows.dtype), MIB, 1000)(rows)
+
+    def merge(x, part, got, *after):
         return pl.pallas_call(
-            functools.partial(merge_kernel, keep),
+            merge_kernel,
+            out_shape=(shape((prow // 4, 4 * width)), shape((prow, width))),
+            in_specs=[VMEM] * 4 + [ANY] * len(after),
+            scratch_shapes=[pltpu.VMEM((width // 128, prow, 128), jnp.float32)],
+            compiler_params=pltpu.CompilerParams(vmem_limit_bytes=8 * MIB),
+            cost_estimate=pl.CostEstimate(flops=mul // 4, bytes_accessed=1 << 20, transcendentals=0),
+        )(x, part, got, late_rows, *after)
+
+    fc1 = pltpu.with_memory_space_constraint(fc1_weight, pltpu.VMEM)
+    out_shape = shape((prow, hidden))
+
+    def finish(blocks, pair, *more):
+        last = len(more) > 0
+        outs = (out_shape, shape((prow, width))) if last else (out_shape,)
+        return pl.pallas_call(
+            functools.partial(hidden_kernel, last),
             out_shape=outs,
-            in_specs=[VMEM] * 6 + [ANY] * len(after),
-            scratch_shapes=[pltpu.VMEM((width // 128, prow, 128), jnp.float32)],
-            compiler_params=pltpu.CompilerParams(vmem_limit_bytes=16 * MIB),
-            cost_estimate=pl.CostEstimate(flops=mul // 4, bytes_accessed=1 << 20, transcendentals=0),
-        )(x, part, got, pbias, row(merge_gain), row(merge_bias), *after)
-
-    bshape = shape((prow // 4, 4 * width))
-    (blocks1,) = merge(0, x_far, part1, got1, (bshape,))
+            in_specs=[VMEM] * 4 + [VMEM, ANY][: len(more)],
+            out_specs=[ANY] * len(outs),
+            scratch_shapes=[
+                pltpu.VMEM((hidden // 256, prow // 2, 256), jnp.bfloat16),
+                pltpu.SemaphoreType.DMA((2 * (hidden // 256) + 1,)),
+            ],
+            input_output_aliases={5: 0} if last else {},
+            compiler_params=pltpu.CompilerParams(vmem_limit_bytes=8 * MIB),
+            cost_estimate=pl.CostEstimate(
+                flops=prow * 4 * width * hidden, bytes_accessed=1 << 24, transcendentals=0
+            ),
+        )(blocks, pair, fc1, rows, *more)
+
+    blocks1, _ = merge(x_far, part1, got1)
     pair1 = swap(blocks1, 1)
-    fc1 = pltpu.with_memory_space_constraint(fc1_weight, pltpu.VMEM)
-    flops = 2 * prow // 2 * 4 * width * hidden
-    early = call(hidden_kernel, shape((prow // 2, hidden)), 24 * MIB, flops)(blocks1, pair1, fc1, row(fc1_bias))
-    blocks0, vit = merge(1, patches, part0, got0, (bshape, shape((prow, width))), early)
+    (early,) = finish(blocks1, pair1)
+    blocks0, vit = merge(patches, part0, got0, early)
     pair0 = swap(blocks0, 1)
-    out = call(hidden_kernel, shape((prow, hidden)), 24 * MIB, flops)(blocks0, pair0, fc1, row(fc1_bias), early)
-    return vit, out
+    merged, vit_out = finish(blocks0, pair0, vit, early)
+    return vit_out, merged
 
 
 def rotate(values, positions, nheads):

time: 49 us -> 50.8 us (1.037)
  local copies, waits for them, and re-layouts: 4.19 us -> 9.29 us
  Pallas kernels: 23.6 us -> 19.4 us
  waiting for transfers between devices: 15 us -> 16.4 us
    unnamed x25 -> x36, local copies, waits for them, and re-layouts: 2.01 us -> 9.29 us
    pallas_call x7 -> x9, Pallas kernels: 20.2 us -> 17.5 us  [the longest x2 6.23 us: finish(): pl.pallas_call(functools.partial(hidden_kernel, last), out_shape=outs, in...]
    reshape x6 -> x0, local copies, waits for them, and re-layouts: 1.42 us -> none  [two_chips(): row = lambda v: v.reshape(1, -1)]
    pallas_call x3 -> x2, Pallas kernels: 2.01 us -> 0.6 us  [norm(): pl.pallas_call(norm_kernel, out_shape=shape((prow, width)), in_specs=[VME...]
    ppermute x9, waiting for transfers between devices: 15 us -> 16.4 us  [swap(): return lax.ppermute(value, 'sp', [(i, i ^ bit) for i in range(4)])]
    dynamic_slice x1 -> x0, local copies, waits for them, and re-layouts: 0.74 us -> none  [two_chips(): lax.dynamic_slice_in_dim(pos_ids, (me ^ k) * prow, prow, 1)]
  transfers between devices with their start and end apart: 9 -> 9, of which waited for: 5 -> 5; matrix products, arithmetic and copies ran while one was open for 7% -> 0% of each run, Pallas kernels for 29% -> 22%
where the time goes in v3:
time: 50.8 us; the launch traced here: 50.2 us
  Pallas kernels  19.4 us (38%)
  waiting for transfers between devices  16.4 us (32%)
  local copies, waits for them, and re-layouts  9.29 us (18%)
  starting transfers between devices  4.3 us (8%)
  between operations  0.8 us (2%)
    ppermute x9, waiting for transfers between devices, swap(): return lax.ppermute(value, 'sp', [(i, i ^ bit) for i in range(4)])  16.4 us
    unnamed x36, local copies, waits for them, and re-layouts  9.29 us
    pallas_call x2, Pallas kernels, finish(): pl.pallas_call(functools.partial(hidden_kernel, last), out_shape=outs, in...  6.23 us
    ppermute x9, starting transfers between devices, swap(): return lax.ppermute(value, 'sp', [(i, i ^ bit) for i in range(4)])  4.3 us
    pallas_call x1, Pallas kernels, two_chips(): call(functools.partial(far_kernel, hdim), part_shape + (tall, tall), 16 *...  3.48 us
    pallas_call x1, Pallas kernels, two_chips(): call(functools.partial(late_kernel, hdim), part_shape, 16 * MIB, 6 * mul)  3.1 us
    pallas_call x1, Pallas kernels, two_chips(): pl.pallas_call(functools.partial(near_kernel, hdim), out_shape=(tall, tal...  2.59 us
    pallas_call x1, Pallas kernels, two_chips(): call(functools.partial(first_kernel, hdim), state + (shape((both, prow),...  1.36 us
  transfers between devices with their start and end apart: 9, of which 5 were waited for; matrix products, arithmetic and copies ran while one was open for 0% of the time, Pallas kernels for 22%

profile of v3, /device:TPU:0, one launch (start us, length us, event | category | flops | bytes accessed | tf_op | source)
XLA Modules:
  0.0 50.2 jit_solution(1980102760360961934)
XLA Ops:
  0.6 0.6 %collective-permute-start.2 = (bf16[960,1280]{1,0:T(8,128)(2,1)}, bf16[960,1280]{1,0:T(8,128)(2,1)S(1)}, u32[]{:S(2)}, u32[]{:S(2)}) collective-permute-start(bf16[960,1280]{1,0:T(8,128)(2,1)} %bitcast.5), channel_id=1, source_target_pairs={{0,1},{1,0},{2,3},{3,2},{4,5},{5,4},{6,7},{7,6},{8,9},{9,8},{10,11... | collective-permute-start | bytes 7372808 | tf_op jit(solution)/shard_map/ppermute | solution.py:280
  1.2 0.1 collective-permute-start.3
  1.3 0.4 collective-permute-start.1
  1.7 2.6 %collective-permute-start = (bf16[128,1280]{1,0:T(8,128)(2,1)}, bf16[128,1280]{1,0:T(8,128)(2,1)S(1)}, u32[]{:S(2)}, u32[]{:S(2)}) collective-permute-start(bf16[128,1280]{1,0:T(8,128)(2,1)} %x.3), channel_id=1, source_target_pairs={{0,2},{1,3},{2,0},{3,1},{4,6},{5,7},{6,4},{7,5},{8,10},{9,11},{10,... | collective-permute-start | bytes 983048 | tf_op jit(solution)/shard_map/ppermute | solution.py:280
  4.3 0.0 copy-start.4
  4.3 1.0 %copy-done.4 = bf16[128,1280]{1,0:T(8,128)(2,1)S(1)} copy-done((bf16[128,1280]{1,0:T(8,128)(2,1)S(1)}, bf16[128,1280]{1,0:T(8,128)(2,1)}, u32[]{:S(2)}) %copy-start.4) | copy-done | bytes 327704
  5.3 0.0 copy-start.6
  5.3 0.7 %copy-done.6 = f32[3,1280]{1,0:T(4,128)S(1)} copy-done((f32[3,1280]{1,0:T(4,128)S(1)}, f32[3,1280]{1,0:T(4,128)}, u32[]{:S(2)}) %copy-start.6) | copy-done | bytes 15384
  6.0 0.0 copy-start.7
  6.0 0.7 %copy-done.7 = f32[1280]{0:T(1024)S(1)} copy-done((f32[1280]{0:T(1024)S(1)}, f32[1280]{0:T(1024)}, u32[]{:S(2)}) %copy-start.7) | copy-done | bytes 5144
  6.7 0.0 copy-start.8
  6.7 0.7 %copy-done.8 = f32[1280]{0:T(1024)S(1)} copy-done((f32[1280]{0:T(1024)S(1)}, f32[1280]{0:T(1024)}, u32[]{:S(2)}) %copy-start.8) | copy-done | bytes 5144
  7.4 0.0 copy-start.9
  7.4 0.7 %copy-done.9 = f32[1280]{0:T(1024)S(1)} copy-done((f32[1280]{0:T(1024)S(1)}, f32[1280]{0:T(1024)}, u32[]{:S(2)}) %copy-start.9) | copy-done | bytes 5144
  8.1 0.0 copy-start.10
  8.1 0.7 %copy-done.10 = f32[1280]{0:T(1024)S(1)} copy-done((f32[1280]{0:T(1024)S(1)}, f32[1280]{0:T(1024)}, u32[]{:S(2)}) %copy-start.10) | copy-done | bytes 5144
  8.8 0.0 copy-start.11
  8.8 0.7 %copy-done.11 = f32[1280]{0:T(1024)S(1)} copy-done((f32[1280]{0:T(1024)S(1)}, f32[1280]{0:T(1024)}, u32[]{:S(2)}) %copy-start.11) | copy-done | bytes 5144
  9.5 0.0 copy-start.12
  9.5 0.7 %copy-done.12 = f32[1280]{0:T(1024)S(1)} copy-done((f32[1280]{0:T(1024)S(1)}, f32[1280]{0:T(1024)}, u32[]{:S(2)}) %copy-start.12) | copy-done | bytes 5144
  10.2 0.0 copy-start.13
  10.2 0.7 %copy-done.13 = s32[2,512]{1,0:T(2,128)S(1)} copy-done((s32[2,512]{1,0:T(2,128)S(1)}, s32[2,512]{1,0:T(2,128)}, u32[]{:S(2)}) %copy-start.13) | copy-done | bytes 4120
  10.9 0.7 %shard_map.131 = (bf16[128,1280]{1,0:T(8,128)(2,1)S(1)}, f32[8,1280]{1,0:T(8,128)S(1)}, f32[1280,8]{1,0:T(8,128)S(1)}, f32[40,512]{1,0:T(8,128)S(1)}, f32[40,512]{1,0:T(8,128)S(1)}) custom-call(bf16[128,1280]{1,0:T(8,128)(2,1)S(1)} %copy-done.4, s32[2,512]{1,0:T(2,128)S(1)} %copy-done.13, f32[3,1280]{1,0:T(4,128)S(1)} %copy-done.6, f32[1280]{0:T(1024)S(1)} %copy-done.7, ...), custom_call_target="tpu_custom_call" | custom-call | flops 209715200 | bytes 1048576 | tf_op jit(solution)/shard_map/pallas_call | solution.py:294
  11.6 0.0 collective-permute-done.1.x
  11.6 0.3 shard_map.132.xb
  11.9 0.0 collective-permute-done.3.pfrom
  11.9 0.0 collective-permute-done.2.wfrom
  11.9 0.0 copy-start
  11.9 1.7 %copy-done = bf16[1280,3,320]{0,2,1:T(8,128)(2,1)S(1)} copy-done((bf16[1280,3,320]{0,2,1:T(8,128)(2,1)S(1)}, bf16[1280,3,320]{0,2,1:T(8,128)(2,1)}, u32[]{:S(2)}) %copy-start) | copy-done | bytes 2457624
  13.6 0.0 copy-start.1
  13.6 0.0 slice-start
  13.6 0.0 slice-start.1
  13.6 2.6 %near.1 = (bf16[640,256]{1,0:T(8,128)(2,1)S(1)}, bf16[640,256]{1,0:T(8,128)(2,1)S(1)}, bf16[640,256]{1,0:T(8,128)(2,1)S(1)}, bf16[960,1280]{1,0:T(8,128)(2,1)S(1)}, bf16[320,1280]{1,0:T(8,128)(2,1)S(1)}) custom-call(bf16[128,1280]{1,0:T(8,128)(2,1)S(1)} %get-tuple-element.27.xa, bf16[128,1280]{1,0:T(8,128)(2,1)S(1)} %shard_map.132.xb, ...), custom_call_target="tpu_custom_call" | custom-call | flops 1258291200 | bytes 8388608 | tf_op jit(solution)/shard_map/near/pallas_call | solution.py:311
  16.2 0.0 copy-start.2
  16.2 1.4 %shard_map.133 = (f32[4,256]{1,0:T(4,128)S(1)}, f32[4,256]{1,0:T(4,128)S(1)}, f32[640,128]{1,0:T(8,128)S(1)}) custom-call(bf16[640,256]{1,0:T(8,128)(2,1)S(1)} %get-tuple-element.31.q, bf16[640,256]{1,0:T(8,128)(2,1)S(1)} %get-tuple-element.32.k.kn, bf16[640,256]{1,0:T(8,128)(2,1)S(1)} %get-tuple-element.33.v.vn), custom_call_target="tpu_custom_call" | custom-call | flops 419430400 | bytes 1048576 | tf_op jit(solution)/shard_map/pallas_call | solution.py:322
  17.6 0.0 collective-permute-done.x
  17.6 0.3 shard_map.134.xa.x
  17.9 0.2 collective-permute-start.4
  18.1 1.5 %collective-permute-done.4.xb = bf16[128,1280]{1,0:T(8,128)(2,1)S(1)} collective-permute-done((bf16[128,1280]{1,0:T(8,128)(2,1)S(1)}, bf16[128,1280]{1,0:T(8,128)(2,1)S(1)}, u32[]{:S(2)}, u32[]{:S(2)}) %collective-permute-start.4) | collective-permute-done | bytes 327712 | tf_op jit(solution)/shard_map/ppermute | solution.py:280
  19.6 0.0 copy-done.1
  19.6 0.0 copy-done.2
  19.6 0.0 slice-start.2
  19.6 3.5 %shard_map.135 = (f32[128,1280]{1,0:T(8,128)S(1)}, bf16[128,1280]{1,0:T(8,128)(2,1)S(1)}, bf16[640,256]{1,0:T(8,128)(2,1)S(1)}, bf16[640,256]{1,0:T(8,128)(2,1)S(1)}) custom-call(bf16[128,1280]{1,0:T(8,128)(2,1)S(1)} %shard_map.134.xa.x, bf16[128,1280]{1,0:T(8,128)(2,1)S(1)} %collective-permute-done.4.xb, bf16[960,1280]{1,0:T(8,128)(2,1)S(1)} %bitcast.7, ...), custom_call_target="tpu_custom_call" | custom-call | flops 1258291200 | bytes 1048576 | tf_op jit(solution)/shard_map/pallas_call | solution.py:328
  23.1 0.1 collective-permute-start.6
  23.2 0.0 slice-start.3
  23.2 3.1 %shard_map.136 = (f32[128,1280]{1,0:T(8,128)S(1)}, bf16[128,1280]{1,0:T(8,128)(2,1)S(1)}) custom-call(bf16[128,1280]{1,0:T(8,128)(2,1)S(1)} %shard_map.134.xa.x, bf16[960,1280]{1,0:T(8,128)(2,1)S(1)} %bitcast.8, bf16[960,1280]{1,0:T(8,128)(2,1)S(1)} %get-tuple-element.35.wpair, f32[1280,8]{1,0:T(8,128)S(1)} %get-tuple-element.28.qcol, ...), custom_call_target="tpu_custom_call" | custom-call | flops 1258291200 | bytes 1048576 | tf_op jit(solution)/shard_map/pallas_call | solution.py:332
  26.3 6.6 %collective-permute-done.6.got = bf16[128,1280]{1,0:T(8,128)(2,1)S(1)} collective-permute-done((bf16[128,1280]{1,0:T(8,128)(2,1)S(1)}, bf16[128,1280]{1,0:T(8,128)(2,1)S(1)}, u32[]{:S(2)}, u32[]{:S(2)}) %collective-permute-start.6) | collective-permute-done | bytes 327712 | tf_op jit(solution)/shard_map/ppermute | solution.py:280
  32.9 0.9 %shard_map.138 = (bf16[32,5120]{1,0:T(8,128)(2,1)S(1)}, bf16[128,1280]{1,0:T(8,128)(2,1)}) custom-call(bf16[128,1280]{1,0:T(8,128)(2,1)S(1)} %collective-permute-done.x, f32[128,1280]{1,0:T(8,128)S(1)} %get-tuple-element.43.part, bf16[128,1280]{1,0:T(8,128)(2,1)S(1)} %collective-permute-done.6.got, f32[8,1280]{1,0:T(8,128)S(1)} %shard_map.137.rows), custom_call_target="tpu_custom_call" | custom-call | flops 52428800 | bytes 1048576 | tf_op jit(solution)/shard_map/pallas_call | solution.py:340
  33.8 0.0 collective-permute-start.7
  33.8 0.0 copy-start.5
  33.8 0.3 collective-permute-start.5
  34.1 1.3 %collective-permute-done.7.pair = bf16[32,5120]{1,0:T(8,128)(2,1)S(1)} collective-permute-done((bf16[32,5120]{1,0:T(8,128)(2,1)S(1)}, bf16[32,5120]{1,0:T(8,128)(2,1)S(1)}, u32[]{:S(2)}, u32[]{:S(2)}) %collective-permute-start.7) | collective-permute-done | bytes 327712 | tf_op jit(solution)/shard_map/ppermute | solution.py:280
  35.4 0.0 slice-done
  35.5 0.0 slice-done.1
  35.5 0.0 slice-done.2
  35.5 0.0 slice-done.3
  35.5 3.1 %shard_map.139.rest_0_.rest_1_ = bf16[128,1280]{1,0:T(8,128)(2,1)} custom-call(bf16[32,5120]{1,0:T(8,128)(2,1)S(1)} %get-tuple-element.45.own, bf16[32,5120]{1,0:T(8,128)(2,1)S(1)} %collective-permute-done.7.pair, bf16[5120,1280]{1,0:T(8,128)(2,1)S(1)} %bitcast.4, f32[8,1280]{1,0:T(8,128)S(1)} %get-tuple-element.26.rows.x), custom_call_target="tpu_custom_call" | custom-call | flops 838860800 | bytes 16777216 | tf_op jit(solution)/shard_map/pallas_call | solution.py:355
  38.6 5.3 %collective-permute-done.5.got = bf16[128,1280]{1,0:T(8,128)(2,1)S(1)} collective-permute-done((bf16[128,1280]{1,0:T(8,128)(2,1)S(1)}, bf16[128,1280]{1,0:T(8,128)(2,1)S(1)}, u32[]{:S(2)}, u32[]{:S(2)}) %collective-permute-start.5) | collective-permute-done | bytes 327712 | tf_op jit(solution)/shard_map/ppermute | solution.py:280
  43.9 0.0 copy-done.5
  44.0 1.0 %copy-done.3 = bf16[128,1280]{1,0:T(8,128)(2,1)S(1)} copy-done((bf16[128,1280]{1,0:T(8,128)(2,1)S(1)}, bf16[128,1280]{1,0:T(8,128)(2,1)}, u32[]{:S(2)}) %copy-start.3) | copy-done | bytes 327704
  44.9 0.5 shard_map.140
  45.4 0.1 collective-permute-start.8
  45.5 1.6 %collective-permute-done.8.pair = bf16[32,5120]{1,0:T(8,128)(2,1)S(1)} collective-permute-done((bf16[32,5120]{1,0:T(8,128)(2,1)S(1)}, bf16[32,5120]{1,0:T(8,128)(2,1)S(1)}, u32[]{:S(2)}, u32[]{:S(2)}) %collective-permute-start.8) | collective-permute-done | bytes 327712 | tf_op jit(solution)/shard_map/ppermute | solution.py:280
  47.1 3.1 %shard_map.141 = (bf16[128,1280]{1,0:T(8,128)(2,1)}, bf16[128,1280]{1,0:T(8,128)(2,1)}) custom-call(bf16[32,5120]{1,0:T(8,128)(2,1)S(1)} %get-tuple-element.46.own, bf16[32,5120]{1,0:T(8,128)(2,1)S(1)} %collective-permute-done.8.pair, bf16[5120,1280]{1,0:T(8,128)(2,1)S(1)} %bitcast.4, ...), custom_call_target="tpu_custom_call", output_to_operand_aliasing={{0}: (5, {})} | custom-call | flops 838860800 | bytes 16777216 | tf_op jit(solution)/shard_map/pallas_call | solution.py:355
  (3 shorter events, 0.0 us)
Async XLA Ops:
  0.6 11.3 %collective-permute-start.2 = (bf16[960,1280]{1,0:T(8,128)(2,1)}, bf16[960,1280]{1,0:T(8,128)(2,1)S(1)}, u32[]{:S(2)}, u32[]{:S(2)}) collective-permute-start(bf16[960,1280]{1,0:T(8,128)(2,1)} %bitcast.5), channel_id=1, source_target_pairs={{0,1},{1,0},{2,3},{3,2},{4,5},{5,4},{6,7},{7,6},{8,9},{9,8},{10,11... | collective-permute-start | bytes 7372808 | tf_op jit(solution)/shard_map/ppermute | solution.py:280
  1.2 10.7 %collective-permute-start.3 = (bf16[320,1280]{1,0:T(8,128)(2,1)}, bf16[320,1280]{1,0:T(8,128)(2,1)S(1)}, u32[]{:S(2)}, u32[]{:S(2)}) collective-permute-start(bf16[320,1280]{1,0:T(8,128)(2,1)} %pown.3), channel_id=1, source_target_pairs={{0,1},{1,0},{2,3},{3,2},{4,5},{5,4},{6,7},{7,6},{8,9},{9,8},{10,11... | collective-permute-start | bytes 2457608 | tf_op jit(solution)/shard_map/ppermute | solution.py:280
  1.3 10.3 %collective-permute-start.1 = (bf16[128,1280]{1,0:T(8,128)(2,1)}, bf16[128,1280]{1,0:T(8,128)(2,1)S(1)}, u32[]{:S(2)}, u32[]{:S(2)}) collective-permute-start(bf16[128,1280]{1,0:T(8,128)(2,1)} %x.3), channel_id=1, source_target_pairs={{0,1},{1,0},{2,3},{3,2},{4,5},{5,4},{6,7},{7,6},{8,9},{9,8},{10,11... | collective-permute-start | bytes 983048 | tf_op jit(solution)/shard_map/ppermute | solution.py:280
  1.7 15.9 %collective-permute-start = (bf16[128,1280]{1,0:T(8,128)(2,1)}, bf16[128,1280]{1,0:T(8,128)(2,1)S(1)}, u32[]{:S(2)}, u32[]{:S(2)}) collective-permute-start(bf16[128,1280]{1,0:T(8,128)(2,1)} %x.3), channel_id=1, source_target_pairs={{0,2},{1,3},{2,0},{3,1},{4,6},{5,7},{6,4},{7,5},{8,10},{9,11},{10,... | collective-permute-start | bytes 983048 | tf_op jit(solution)/shard_map/ppermute | solution.py:280
  4.3 1.0 %copy-start.4 = (bf16[128,1280]{1,0:T(8,128)(2,1)S(1)}, bf16[128,1280]{1,0:T(8,128)(2,1)}, u32[]{:S(2)}) copy-start(bf16[128,1280]{1,0:T(8,128)(2,1)} %x.3) | copy-start | bytes 983044
  5.3 0.7 %copy-start.6 = (f32[3,1280]{1,0:T(4,128)S(1)}, f32[3,1280]{1,0:T(4,128)}, u32[]{:S(2)}) copy-start(f32[3,1280]{1,0:T(4,128)} %qkv_bias.1) | copy-start | bytes 46084
  6.0 0.7 %copy-start.7 = (f32[1280]{0:T(1024)S(1)}, f32[1280]{0:T(1024)}, u32[]{:S(2)}) copy-start(f32[1280]{0:T(1024)} %rest_0_.1) | copy-start | bytes 15364
  6.7 0.7 %copy-start.8 = (f32[1280]{0:T(1024)S(1)}, f32[1280]{0:T(1024)}, u32[]{:S(2)}) copy-start(f32[1280]{0:T(1024)} %rest_1_.1) | copy-start | bytes 15364
  7.4 0.7 %copy-start.9 = (f32[1280]{0:T(1024)S(1)}, f32[1280]{0:T(1024)}, u32[]{:S(2)}) copy-start(f32[1280]{0:T(1024)} %rest_2_.1) | copy-start | bytes 15364
  8.1 0.7 %copy-start.10 = (f32[1280]{0:T(1024)S(1)}, f32[1280]{0:T(1024)}, u32[]{:S(2)}) copy-start(f32[1280]{0:T(1024)} %rest_3_.1) | copy-start | bytes 15364
  8.8 0.7 %copy-start.11 = (f32[1280]{0:T(1024)S(1)}, f32[1280]{0:T(1024)}, u32[]{:S(2)}) copy-start(f32[1280]{0:T(1024)} %rest_4_.1) | copy-start | bytes 15364
  9.5 0.7 %copy-start.12 = (f32[1280]{0:T(1024)S(1)}, f32[1280]{0:T(1024)}, u32[]{:S(2)}) copy-start(f32[1280]{0:T(1024)} %rest_5_.1) | copy-start | bytes 15364
  10.2 0.7 %copy-start.13 = (s32[2,512]{1,0:T(2,128)S(1)}, s32[2,512]{1,0:T(2,128)}, u32[]{:S(2)}) copy-start(s32[2,512]{1,0:T(2,128)} %pos.1) | copy-start | bytes 12292
  11.9 1.7 %copy-start = (bf16[1280,3,320]{0,2,1:T(8,128)(2,1)S(1)}, bf16[1280,3,320]{0,2,1:T(8,128)(2,1)}, u32[]{:S(2)}) copy-start(bf16[1280,3,320]{0,2,1:T(8,128)(2,1)} %param.16) | copy-start | bytes 7372804
  13.6 6.0 %copy-start.1 = (bf16[1280,3,320]{0,2,1:T(8,128)(2,1)S(1)}, bf16[1280,3,320]{0,2,1:T(8,128)(2,1)}, u32[]{:S(2)}) copy-start(bf16[1280,3,320]{0,2,1:T(8,128)(2,1)} %param.16) | copy-start | bytes 7372804
  13.6 21.8 %slice-start = ((s8[13107200]{0:T(1024)(128)(4,1)}), s8[524288]{0:T(1024)(128)(4,1)S(1)}, s32[]{:S(2)}) async-start(s8[13107200]{0:T(1024)(128)(4,1)} %bitcast.3), calls=%async_computation | async-start | bytes 1048576
  13.6 21.8 %slice-start.1 = ((s8[13107200]{0:T(1024)(128)(4,1)}), s8[4194304]{0:T(1024)(128)(4,1)S(1)}, s32[]{:S(2)}) async-start(s8[13107200]{0:T(1024)(128)(4,1)} %bitcast.3), calls=%async_computation.1 | async-start | bytes 8388608
  16.2 3.4 %copy-start.2 = (bf16[320,1280]{1,0:T(8,128)(2,1)S(1)}, bf16[320,1280]{1,0:T(8,128)(2,1)}, u32[]{:S(2)}) copy-start(bf16[320,1280]{1,0:T(8,128)(2,1)} %pown.3) | copy-start | bytes 2457604
  17.9 1.7 %collective-permute-start.4 = (bf16[128,1280]{1,0:T(8,128)(2,1)S(1)}, bf16[128,1280]{1,0:T(8,128)(2,1)S(1)}, u32[]{:S(2)}, u32[]{:S(2)}) collective-permute-start(bf16[128,1280]{1,0:T(8,128)(2,1)S(1)} %shard_map.134.xa.x), channel_id=1, source_target_pairs={{0,1},{1,0},{2,3},{3,2},{4,5},{5,4},{6,7},{7,6},{8,9},{9,8},{10,11... | collective-permute-start | bytes 983048 | tf_op jit(solution)/shard_map/ppermute | solution.py:280
  19.6 15.8 %slice-start.2 = ((s8[13107200]{0:T(1024)(128)(4,1)}), s8[4194304]{0:T(1024)(128)(4,1)S(1)}, s32[]{:S(2)}) async-start(s8[13107200]{0:T(1024)(128)(4,1)} %bitcast.3), calls=%async_computation.2 | async-start | bytes 8388608
  23.1 9.8 %collective-permute-start.6 = (bf16[128,1280]{1,0:T(8,128)(2,1)S(1)}, bf16[128,1280]{1,0:T(8,128)(2,1)S(1)}, u32[]{:S(2)}, u32[]{:S(2)}) collective-permute-start(bf16[128,1280]{1,0:T(8,128)(2,1)S(1)} %get-tuple-element.44), channel_id=1, source_target_pairs={{0,2},{1,3},{2,0},{3,1},{4,6},{5,7},{6,4},{7,5},{8,10},{9,11},{10,... | collective-permute-start | bytes 983048 | tf_op jit(solution)/shard_map/ppermute | solution.py:280
  23.2 12.2 %slice-start.3 = ((s8[13107200]{0:T(1024)(128)(4,1)}), s8[4194304]{0:T(1024)(128)(4,1)S(1)}, s32[]{:S(2)}) async-start(s8[13107200]{0:T(1024)(128)(4,1)} %bitcast.3), calls=%async_computation.3 | async-start | bytes 8388608
  33.8 1.6 %collective-permute-start.7 = (bf16[32,5120]{1,0:T(8,128)(2,1)S(1)}, bf16[32,5120]{1,0:T(8,128)(2,1)S(1)}, u32[]{:S(2)}, u32[]{:S(2)}) collective-permute-start(bf16[32,5120]{1,0:T(8,128)(2,1)S(1)} %get-tuple-element.45.own), channel_id=1, source_target_pairs={{0,1},{1,0},{2,3},{3,2},{4,5},{5,4},{6,7},{7,6},{8,9},{9,8},{10,11... | collective-permute-start | bytes 983048 | tf_op jit(solution)/shard_map/ppermute | solution.py:280
  33.8 10.1 %copy-start.5 = (bf16[128,1280]{1,0:T(8,128)(2,1)S(1)}, bf16[128,1280]{1,0:T(8,128)(2,1)}, u32[]{:S(2)}) copy-start(bf16[128,1280]{1,0:T(8,128)(2,1)} %x.3) | copy-start | bytes 983044
  33.8 10.1 %collective-permute-start.5 = (bf16[128,1280]{1,0:T(8,128)(2,1)S(1)}, bf16[128,1280]{1,0:T(8,128)(2,1)S(1)}, u32[]{:S(2)}, u32[]{:S(2)}) collective-permute-start(bf16[128,1280]{1,0:T(8,128)(2,1)S(1)} %get-tuple-element.42), channel_id=1, source_target_pairs={{0,2},{1,3},{2,0},{3,1},{4,6},{5,7},{6,4},{7,5},{8,10},{9,11},{10,... | collective-permute-start | bytes 983048 | tf_op jit(solution)/shard_map/ppermute | solution.py:280
  43.9 1.0 %copy-start.3 = (bf16[128,1280]{1,0:T(8,128)(2,1)S(1)}, bf16[128,1280]{1,0:T(8,128)(2,1)}, u32[]{:S(2)}) copy-start(bf16[128,1280]{1,0:T(8,128)(2,1)} %shard_map.139.rest_0_.rest_1_) | copy-start | bytes 983044
  45.4 1.7 %collective-permute-start.8 = (bf16[32,5120]{1,0:T(8,128)(2,1)S(1)}, bf16[32,5120]{1,0:T(8,128)(2,1)S(1)}, u32[]{:S(2)}, u32[]{:S(2)}) collective-permute-start(bf16[32,5120]{1,0:T(8,128)(2,1)S(1)} %get-tuple-element.46.own), channel_id=1, source_target_pairs={{0,1},{1,0},{2,3},{3,2},{4,5},{5,4},{6,7},{7,6},{8,9},{9,8},{10,11... | collective-permute-start | bytes 983048 | tf_op jit(solution)/shard_map/ppermute | solution.py:280

commit v4 on v3

--- a/solution.py
+++ b/solution.py
@@ -14,6 +14,7 @@
 MIB = 1 << 20
 VMEM = pl.BlockSpec(memory_space=pltpu.VMEM)
 ANY = pl.BlockSpec(memory_space=pl.ANY)
+HBM = pl.BlockSpec(memory_space=pltpu.HBM)
 NT = (((1,), (1,)), ((), ()))
 TN = (((0,), (0,)), ((), ()))
 NN = (((1,), (0,)), ((), ()))
@@ -39,29 +40,38 @@
     )
 
 
-def setup_kernel(hdim, x, pos, qkv_bias, *rest):
-    vectors, (normed, rows, qcol, cosine, sine) = rest[:-5], rest[-5:]
-    width = x.shape[1]
-    prow = x.shape[0]
+def setup_kernel(hdim, count, *refs):
+    sources, rest = refs[:count], refs[count:]
+    x, wown, pown, normed, rows, qcol, cosine, sine, pos, qkv_bias = rest[:10]
+    vectors, sems = rest[10:-1], rest[-1]
+    targets = (x, pos, qkv_bias) + tuple(vectors) + (pown, wown)
+    copies = [pltpu.make_async_copy(a, b, sems.at[n]) for n, (a, b) in enumerate(zip(sources, targets))]
+    for copy in copies:
+        copy.start()
+    prow, width = x.shape
     me = lax.axis_index("sp")
-    rows[...] = jnp.zeros_like(rows)
-    for at, vector in enumerate(vectors):
-        rows[at : at + 1, :] = vector[...].reshape(1, width)
-    cube = jnp.concatenate([qkv_bias[...], jnp.zeros((5, width), jnp.float32)], axis=0)
-    qcol[...] = cube.T
     quarter = hdim // 4
     feature = lax.broadcasted_iota(jnp.int32, (2 * quarter, prow), 0)
     second = feature >= quarter
     power = jnp.where(second, feature - quarter, feature).astype(jnp.float32)
     inv = jnp.exp(power * (-2.0 * math.log(10000.0) / (hdim // 2)))
+    rows[...] = jnp.zeros_like(rows)
+    for copy in copies[:-2]:
+        copy.wait()
     for k in range(4):
         at = pl.ds(pl.multiple_of((me ^ k) * prow, prow), prow)
         place = jnp.where(second, pos[1:2, at], pos[0:1, at]).astype(jnp.float32)
         angle = place * inv
         cosine[:, k * prow : (k + 1) * prow] = jnp.cos(angle)
         sine[:, k * prow : (k + 1) * prow] = jnp.sin(angle)
+    for at, vector in enumerate(vectors):
+        rows[at : at + 1, :] = vector[...].reshape(1, width)
+    cube = jnp.concatenate([qkv_bias[...], jnp.zeros((5, width), jnp.float32)], axis=0)
+    qcol[...] = cube.T
     value = layer_norm(x[...].astype(jnp.float32), rows[0:1, :], rows[1:2, :])
     normed[...] = value.astype(jnp.bfloat16)
+    for copy in copies[-2:]:
+        copy.wait()
 
 
 def copy_kernel(x, out):
@@ -95,46 +105,36 @@
     return jnp.concatenate(rows, axis=0)
 
 
-def near_kernel(hdim, xa, xb, wown, wfrom, pfrom, qcol, cosine, sine, qout, kout, vout, wpair, ppair, sems):
-    local = wown.shape[0] // 3
+def near_kernel(hdim, side, xa, xb, weight, qcol, cosine, sine, qout, kout, vout, tops, sums, outs):
+    scale = math.log2(math.e) / math.sqrt(hdim)
+    local = weight.shape[0] // 3
     rows = xa.shape[0]
-    me = lax.axis_index("sp")
-    wcopy = pltpu.make_async_copy(wfrom, wpair, sems.at[0])
-    pcopy = pltpu.make_async_copy(pfrom, ppair, sems.at[1])
-    wcopy.start()
-    pcopy.start()
+    owner = lax.axis_index("sp") ^ side
     normed = jnp.concatenate([xa[...], xb[...]], axis=0)
     cos, sin = cosine[:, : 2 * rows], sine[:, : 2 * rows]
-    for side, weight in enumerate((wown, wpair)):
-        if side == 1:
-            wcopy.wait()
-        owner = me ^ side
-        base = slice(side * local, (side + 1) * local)
-        query = dot(weight[0:local, :], normed[:rows], NT) + column(qcol, owner, local, 0)
-        qout[base, :] = paired(rotated(query, cos[:, :rows], sin[:, :rows], hdim), hdim)
-        keyval = dot(weight[local:, :], normed, NT)
-        kout[base, :] = rotated(keyval[:local] + column(qcol, owner, local, 1), cos, sin, hdim)
-        vout[base, :] = (keyval[local:] + column(qcol, owner, local, 2)).astype(jnp.bfloat16)
-    pcopy.wait()
-
-
-def first_kernel(hdim, q, k, v, tops, sums, outs):
-    scale = math.log2(math.e) / math.sqrt(hdim)
-    rows = q.shape[1] // 2
-    for p in range(q.shape[0] // (2 * hdim)):
+    query = dot(weight[0:local, :], normed[:rows], NT) + column(qcol, owner, local, 0)
+    query = paired(rotated(query, cos[:, :rows], sin[:, :rows], hdim), hdim)
+    keyval = dot(weight[local:, :], normed, NT)
+    key = rotated(keyval[:local] + column(qcol, owner, local, 1), cos, sin, hdim)
+    value = (keyval[local:] + column(qcol, owner, local, 2)).astype(jnp.bfloat16)
+    qout[...] = query
+    kout[...] = key
+    vout[...] = value
+    for p in range(local // (2 * hdim)):
         f = slice(2 * p * hdim, 2 * (p + 1) * hdim)
-        scores = dot(k[f, :], q[f, :], TN)
+        scores = dot(key[f], query[f], TN)
         top = jnp.max(scores, axis=0, keepdims=True)
         expo = jnp.exp2((scores - top) * scale)
         tops[p : p + 1, :] = top
         sums[p : p + 1, :] = jnp.sum(expo, axis=0, keepdims=True)
-        total = dot(v[f, :], expo.astype(jnp.bfloat16), NN)
-        outs[2 * p * hdim : (2 * p + 1) * hdim, :] = total[:hdim, :rows]
-        outs[(2 * p + 1) * hdim : 2 * (p + 1) * hdim, :] = total[hdim:, rows:]
-
-
-def far_kernel(hdim, xa, xb, wown, wpair, qcol, cosine, sine, q, tops, sums, outs, pown, ppair, part, send, kout, vout):
+        total = dot(value[f], expo.astype(jnp.bfloat16), NN)
+        outs[f.start : f.start + hdim, :] = total[:hdim, :rows]
+        outs[f.start + hdim : f.stop, :] = total[hdim:, rows:]
+
+
+def far_kernel(hdim, xa, xb, wown, wpair, pown, ppair, qcol, cosine, sine, *refs):
     scale = math.log2(math.e) / math.sqrt(hdim)
+    near, (part, send, kout, vout) = (refs[:4], refs[4:8]), refs[8:]
     local = wown.shape[0] // 3
     rows = xa.shape[0]
     me = lax.axis_index("sp")
@@ -142,6 +142,7 @@
     cos, sin = cosine[:, 2 * rows :], sine[:, 2 * rows :]
     total = None
     for side, weight in enumerate((wown, wpair)):
+        q, tops, sums, outs = near[side]
         owner = me ^ side
         base = slice(side * local, (side + 1) * local)
         keyval = dot(weight[local:, :], normed, NT)
@@ -150,16 +151,15 @@
         kout[base, :] = key
         vout[base, :] = value
         pieces = []
-        for at in range(0, local, 2 * hdim):
-            f = slice(side * local + at, side * local + at + 2 * hdim)
-            p = (side * local + at) // (2 * hdim)
-            scores = dot(key[at : at + 2 * hdim], q[f, :], TN)
+        for p in range(local // (2 * hdim)):
+            f = slice(2 * p * hdim, 2 * (p + 1) * hdim)
+            scores = dot(key[f], q[f, :], TN)
             old = tops[p : p + 1, :]
             top = jnp.maximum(old, jnp.max(scores, axis=0, keepdims=True))
             expo = jnp.exp2((scores - top) * scale)
             shrink = jnp.exp2((old - top) * scale)
             inv = 1.0 / (sums[p : p + 1, :] * shrink + jnp.sum(expo, axis=0, keepdims=True))
-            late = dot(value[at : at + 2 * hdim], expo.astype(jnp.bfloat16), NN)
+            late = dot(value[f], expo.astype(jnp.bfloat16), NN)
             for h in range(2):
                 lanes = slice(h * rows, (h + 1) * rows)
                 feats = slice(h * hdim, (h + 1) * hdim)
@@ -172,7 +172,7 @@
     send[...] = total.astype(jnp.bfloat16)
 
 
-def late_kernel(hdim, x, wown, wpair, qcol, cosine, sine, kn, vn, kf, vf, pown, ppair, part, send):
+def late_kernel(hdim, x, wown, wpair, pown, ppair, qcol, cosine, sine, kna, vna, knb, vnb, kf, vf, part, send):
     scale = math.log2(math.e) / math.sqrt(hdim)
     local = wown.shape[0] // 3
     rows = x.shape[0]
@@ -185,14 +185,16 @@
         pieces = []
         for at in range(0, local, 2 * hdim):
             f = slice(side * local + at, side * local + at + 2 * hdim)
-            both = query[at : at + 2 * hdim]
-            sn = dot(kn[f, :], both, TN)
+            g = slice(at, at + 2 * hdim)
+            kn, vn = ((kna, vna), (knb, vnb))[side]
+            both = query[g]
+            sn = dot(kn[g, :], both, TN)
             sf = dot(kf[f, :], both, TN)
             top = jnp.maximum(jnp.max(sn, axis=0, keepdims=True), jnp.max(sf, axis=0, keepdims=True))
             en = jnp.exp2((sn - top) * scale)
             ef = jnp.exp2((sf - top) * scale)
             inv = 1.0 / (jnp.sum(en, axis=0, keepdims=True) + jnp.sum(ef, axis=0, keepdims=True))
-            mixed = dot(vn[f, :], (en * inv).astype(jnp.bfloat16), NN)
+            mixed = dot(vn[g, :], (en * inv).astype(jnp.bfloat16), NN)
             mixed = (mixed + dot(vf[f, :], (ef * inv).astype(jnp.bfloat16), NN)).astype(jnp.bfloat16)
             pieces += [mixed[:hdim, :rows], mixed[hdim:, rows:]]
         add = dot(jnp.concatenate(pieces, axis=0), (pown, ppair)[side][...], TN)
@@ -201,12 +203,13 @@
     send[...] = total.astype(jnp.bfloat16)
 
 
-def merge_kernel(x, part, got, rows, *rest):
-    blocks, vit, scratch = rest[-3:]
+def merge_kernel(keep, x, part, got, rows, *rest):
+    blocks, scratch = rest[-2], rest[-1]
     width = x.shape[1]
     value = x[...].astype(jnp.float32) + (part[...] + got[...].astype(jnp.float32)) + rows[2:3, :]
     rounded = value.astype(jnp.bfloat16)
-    vit[...] = rounded
+    if keep:
+        rest[-3][...] = rounded
     normed = layer_norm(rounded.astype(jnp.float32), rows[3:4, :], rows[4:5, :])
     count = x.shape[0] // 4
     lanes = scratch.shape[2]
@@ -221,36 +224,40 @@
     return 0.5 * v * (1.0 + lax.erf(v * math.sqrt(0.5)))
 
 
-def hidden_kernel(last, own, pair, weight, rows, *rest):
+def hidden_kernel(own, pair, weight, rows, out):
+    core = lax.axis_index("sp") % 2
+    count = own.shape[0]
+    both = jnp.concatenate([own[...], pair[...]], axis=0)
+    hid = gelu(dot(both, weight[...], NN) + rows[5:6, :]).astype(jnp.bfloat16)
+    for half, place in enumerate((core, 1 - core)):
+        out[pl.ds(pl.multiple_of(place * count, count), count), :] = hid[half * count : (half + 1) * count]
+
+
+def last_kernel(own, pair, weight, rows, vit, early, out, vout, stage, sems):
     me = lax.axis_index("sp")
     chip, core = me // 2, me % 2
     count = own.shape[0]
-    if last:
-        vit, _, out, vout, stage, sems = rest
-        start = chip * 2 * count
-        vcopy = pltpu.make_async_copy(vit, vout, sems.at[2 * stage.shape[0]])
-        vcopy.start()
-    else:
-        out, stage, sems = rest
-        start = (1 - chip) * 2 * count
+    at = lambda start: pl.ds(pl.multiple_of(start, count), count)
+    copies = [pltpu.make_async_copy(vit, vout, sems.at[0])]
+    there = out.at[pl.ds(pl.multiple_of((1 - chip) * 2 * count, count), 2 * count)]
+    copies.append(pltpu.make_async_copy(early, there, sems.at[1]))
+    for copy in copies:
+        copy.start()
     both = jnp.concatenate([own[...], pair[...]], axis=0)
     step = stage.shape[2]
-    copies = []
     for n in range(stage.shape[0]):
         cols = slice(n * step, (n + 1) * step)
-        hid = gelu(dot(both, weight[:, cols], NN) + rows[5:6, cols]).astype(jnp.bfloat16)
-        stage[n] = hid
+        stage[n] = gelu(dot(both, weight[:, cols], NN) + rows[5:6, cols]).astype(jnp.bfloat16)
         for half, place in enumerate((core, 1 - core)):
-            at = pl.ds(pl.multiple_of(start + place * count, count), count)
             copy = pltpu.make_async_copy(
-                stage.at[n, pl.ds(half * count, count)], out.at[at, pl.ds(n * step, step)], sems.at[2 * n + half]
+                stage.at[n, pl.ds(half * count, count)],
+                out.at[at(chip * 2 * count + place * count), pl.ds(n * step, step)],
+                sems.at[2 + 2 * n + half],
             )
             copy.start()
             copies.append(copy)
     for copy in copies:
         copy.wait()
-    if last:
-        vcopy.wait()
 
 
 def shape(dims, dtype=jnp.bfloat16):
@@ -286,94 +293,101 @@
     p_pair = swap(proj_weight, 1)
 
     both = 2 * local
-    tall = shape((both, 2 * prow))
     part_shape = (shape((prow, width), jnp.float32), shape((prow, width)))
     mul = 2 * prow * width * local * 2
     table = shape((hdim // 2, 4 * prow), jnp.float32)
 
-    n_own, rows, qcol, cos, sin = call(
-        functools.partial(setup_kernel, hdim),
-        (shape((prow, width)), shape((8, width), jnp.float32), shape((width, 8), jnp.float32), table, table),
-        8 * MIB,
-        mul,
-    )(patches, pos_ids, qkv_bias, norm_gain, norm_bias, proj_bias, merge_gain, merge_bias, fc1_bias)
+    sources = (patches, pos_ids, qkv_bias, norm_gain, norm_bias, proj_bias, merge_gain, merge_bias, fc1_bias)
+    sources += (proj_weight, weight)
+    held = lambda v: pltpu.VMEM(v.shape, v.dtype)
+    x_own, w_own, p_own, n_own, rows, qcol, cos, sin = pl.pallas_call(
+        functools.partial(setup_kernel, hdim, len(sources)),
+        out_shape=(
+            held(patches),
+            held(weight),
+            held(proj_weight),
+            shape((prow, width)),
+            shape((8, width), jnp.float32),
+            shape((width, 8), jnp.float32),
+            table,
+            table,
+        ),
+        in_specs=[HBM] * len(sources),
+        scratch_shapes=[held(v) for v in sources[1:-2]] + [pltpu.SemaphoreType.DMA((len(sources),))],
+        compiler_params=pltpu.CompilerParams(vmem_limit_bytes=4 * MIB),
+        cost_estimate=pl.CostEstimate(flops=mul, bytes_accessed=1 << 22, transcendentals=0),
+        name="setup",
+    )(*(pltpu.with_memory_space_constraint(v, pltpu.HBM) for v in sources))
 
     def norm(x, *after):
         return pl.pallas_call(
             norm_kernel,
             out_shape=shape((prow, width)),
             in_specs=[VMEM] * 2 + [ANY] * len(after),
-            compiler_params=pltpu.CompilerParams(vmem_limit_bytes=8 * MIB),
+            compiler_params=pltpu.CompilerParams(vmem_limit_bytes=4 * MIB),
             cost_estimate=pl.CostEstimate(flops=mul // 4, bytes_accessed=1 << 20, transcendentals=0),
         )(x, rows, *after)
 
     n_pair = norm(x_pair)
-    q_near, k_near, v_near, w_vmem, p_vmem = pl.pallas_call(
-        functools.partial(near_kernel, hdim),
-        out_shape=(tall, tall, tall, pltpu.VMEM(weight.shape, weight.dtype), pltpu.VMEM(proj_weight.shape, weight.dtype)),
-        in_specs=[VMEM] * 3 + [ANY] * 2 + [VMEM] * 3,
-        out_specs=[VMEM] * 5,
-        scratch_shapes=[pltpu.SemaphoreType.DMA((2,))],
-        compiler_params=pltpu.CompilerParams(vmem_limit_bytes=16 * MIB),
-        cost_estimate=pl.CostEstimate(flops=6 * mul, bytes_accessed=1 << 23, transcendentals=0),
-        name="near",
-    )(n_own, n_pair, weight, w_pair, p_pair, qcol, cos, sin)
-    state = tuple(shape((HEADS // 4, 2 * prow), jnp.float32) for _ in range(2))
-    tops, sums, outs = call(
-        functools.partial(first_kernel, hdim), state + (shape((both, prow), jnp.float32),), 16 * MIB, 2 * mul
-    )(q_near, k_near, v_near)
-
-    n_far = norm(x_far, tops)
+    flat = shape((local, 2 * prow))
+    state = shape((local // (2 * hdim), 2 * prow), jnp.float32)
+    near_shape = (flat, flat, flat, state, state, shape((local, prow), jnp.float32))
+
+    def near(side, weight):
+        q, k, v, *rest = call(
+            functools.partial(near_kernel, hdim, side), near_shape, 8 * MIB, 4 * mul
+        )(n_own, n_pair, weight, qcol, cos, sin)
+        return (q, *rest), (k, v)
+
+    early_own, kv_own = near(0, w_own)
+    early_pair, kv_pair = near(1, w_pair)
+
+    n_far = norm(x_far, early_own[1], early_pair[1])
     n_farpair = swap(n_far, 1)
+    tall = shape((both, 2 * prow))
+    shared = (w_own, w_pair, p_own, p_pair, qcol, cos, sin)
     part0, send0, k_far, v_far = call(
-        functools.partial(far_kernel, hdim), part_shape + (tall, tall), 16 * MIB, 6 * mul
-    )(n_far, n_farpair, weight, w_vmem, qcol, cos, sin, q_near, tops, sums, outs, proj_weight, p_vmem)
+        functools.partial(far_kernel, hdim), part_shape + (tall, tall), 8 * MIB, 6 * mul
+    )(n_far, n_farpair, *shared, *early_own, *early_pair)
     got1 = swap(send0, 2)
     part1, send1 = call(
-        functools.partial(late_kernel, hdim), part_shape, 16 * MIB, 6 * mul
-    )(n_far, weight, w_vmem, qcol, cos, sin, k_near, v_near, k_far, v_far, proj_weight, p_vmem)
+        functools.partial(late_kernel, hdim), part_shape, 8 * MIB, 6 * mul
+    )(n_far, *shared, *kv_own, *kv_pair, k_far, v_far)
     got0 = swap(send1, 2)
-
     late_rows = call(copy_kernel, shape(rows.shape, rows.dtype), MIB, 1000)(rows)
 
-    def merge(x, part, got, *after):
+    blocks_shape = shape((prow // 4, 4 * width))
+
+    def merge(x, part, got, outs, *after):
         return pl.pallas_call(
-            merge_kernel,
-            out_shape=(shape((prow // 4, 4 * width)), shape((prow, width))),
+            functools.partial(merge_kernel, len(outs) == 2),
+            out_shape=outs,
             in_specs=[VMEM] * 4 + [ANY] * len(after),
             scratch_shapes=[pltpu.VMEM((width // 128, prow, 128), jnp.float32)],
-            compiler_params=pltpu.CompilerParams(vmem_limit_bytes=8 * MIB),
+            compiler_params=pltpu.CompilerParams(vmem_limit_bytes=4 * MIB),
             cost_estimate=pl.CostEstimate(flops=mul // 4, bytes_accessed=1 << 20, transcendentals=0),
         )(x, part, got, late_rows, *after)
 
     fc1 = pltpu.with_memory_space_constraint(fc1_weight, pltpu.VMEM)
-    out_shape = shape((prow, hidden))
-
-    def finish(blocks, pair, *more):
-        last = len(more) > 0
-        outs = (out_shape, shape((prow, width))) if last else (out_shape,)
-        return pl.pallas_call(
-            functools.partial(hidden_kernel, last),
-            out_shape=outs,
-            in_specs=[VMEM] * 4 + [VMEM, ANY][: len(more)],
-            out_specs=[ANY] * len(outs),
-            scratch_shapes=[
-                pltpu.VMEM((hidden // 256, prow // 2, 256), jnp.bfloat16),
-                pltpu.SemaphoreType.DMA((2 * (hidden // 256) + 1,)),
-            ],
-            input_output_aliases={5: 0} if last else {},
-            compiler_params=pltpu.CompilerParams(vmem_limit_bytes=8 * MIB),
-            cost_estimate=pl.CostEstimate(
-                flops=prow * 4 * width * hidden, bytes_accessed=1 << 24, transcendentals=0
-            ),
-        )(blocks, pair, fc1, rows, *more)
-
-    blocks1, _ = merge(x_far, part1, got1)
+    (blocks1,) = merge(x_far, part1, got1, (blocks_shape,))
     pair1 = swap(blocks1, 1)
-    (early,) = finish(blocks1, pair1)
-    blocks0, vit = merge(patches, part0, got0, early)
+    flops = prow * 4 * width * hidden
+    early = call(hidden_kernel, shape((prow // 2, hidden)), 4 * MIB, flops)(blocks1, pair1, fc1, rows)
+    vit, blocks0 = merge(x_own, part0, got0, (shape((prow, width)), blocks_shape), early)
     pair0 = swap(blocks0, 1)
-    merged, vit_out = finish(blocks0, pair0, vit, early)
+    parts = hidden // 256
+    merged, vit_out = pl.pallas_call(
+        last_kernel,
+        out_shape=(shape((prow, hidden)), shape((prow, width))),
+        out_specs=[HBM] * 2,
+        scratch_shapes=[
+            pltpu.VMEM((parts, prow // 2, 256), jnp.bfloat16),
+            pltpu.SemaphoreType.DMA((2 + 2 * parts,)),
+        ],
+        compiler_params=pltpu.CompilerParams(vmem_limit_bytes=4 * MIB),
+        cost_estimate=pl.CostEstimate(flops=flops, bytes_accessed=1 << 24, transcendentals=0),
+        name="hidden0",
+    )(blocks0, pair0, fc1, rows, vit, early)
     return vit_out, merged
 
 

time: 50.8 us -> 44.2 us (0.87)
  local copies, waits for them, and re-layouts: 9.29 us -> 0.02 us
  starting transfers between devices: 4.3 us -> 7.45 us
    unnamed x36 -> x8, local copies, waits for them, and re-layouts: 9.29 us -> 0.02 us
    ppermute x9, starting transfers between devices: 4.3 us -> 7.45 us  [swap(): return lax.ppermute(value, 'sp', [(i, i ^ bit) for i in range(4)])]
  transfers between devices with their start and end apart: 9 -> 9, of which waited for: 5 -> 5; matrix products, arithmetic and copies ran while one was open for 0% -> 0% of each run, Pallas kernels for 22% -> 26%
where the time goes in v4:
time: 44.2 us; the launch traced here: 44 us
  Pallas kernels  19 us (43%)
  waiting for transfers between devices  16.7 us (38%)
  starting transfers between devices  7.45 us (17%)
  between operations  0.8 us (2%)
    ppermute x9, waiting for transfers between devices, swap(): return lax.ppermute(value, 'sp', [(i, i ^ bit) for i in range(4)])  16.7 us
    ppermute x9, starting transfers between devices, swap(): return lax.ppermute(value, 'sp', [(i, i ^ bit) for i in range(4)])  7.45 us
    pallas_call x1, Pallas kernels, two_chips(): call(functools.partial(far_kernel, hdim), part_shape + (tall, tall), 8 *...  3.48 us
    pallas_call x1, Pallas kernels, two_chips(): pl.pallas_call(last_kernel, out_shape=(shape((prow, hidden)), shape((prow...  3.18 us
    pallas_call x1, Pallas kernels, two_chips(): call(functools.partial(late_kernel, hdim), part_shape, 8 * MIB, 6 * mul)  3.14 us
    pallas_call x2, Pallas kernels, near(): call(functools.partial(near_kernel, hdim, side), near_shape, 8 * MIB, 4 *...  3.05 us
    pallas_call x1, Pallas kernels, two_chips(): call(hidden_kernel, shape((prow // 2, hidden)), 4 * MIB, flops)  2.43 us
    pallas_call x1, Pallas kernels, two_chips(): pl.pallas_call(functools.partial(setup_kernel, hdim, len(sources)), out_s...  2.27 us
  transfers between devices with their start and end apart: 9, of which 5 were waited for; matrix products, arithmetic and copies ran while one was open for 0% of the time, Pallas kernels for 26%

profile of v4, /device:TPU:0, one launch (start us, length us, event | category | flops | bytes accessed | tf_op | source)
XLA Modules:
  0.0 44.0 jit_solution(6482061571808867630)
XLA Ops:
  0.6 0.6 %collective-permute-start.2 = (bf16[960,1280]{1,0:T(8,128)(2,1)}, bf16[960,1280]{1,0:T(8,128)(2,1)S(1)}, u32[]{:S(2)}, u32[]{:S(2)}) collective-permute-start(bf16[960,1280]{1,0:T(8,128)(2,1)} %bitcast.5), channel_id=1, source_target_pairs={{0,1},{1,0},{2,3},{3,2},{4,5},{5,4},{6,7},{7,6},{8,9},{9,8},{10,11... | collective-permute-start | bytes 7372808 | tf_op jit(solution)/shard_map/ppermute | solution.py:287
  1.2 0.1 collective-permute-start.1
  1.3 0.4 collective-permute-start.4
  1.7 2.6 %collective-permute-start = (bf16[128,1280]{1,0:T(8,128)(2,1)}, bf16[128,1280]{1,0:T(8,128)(2,1)S(1)}, u32[]{:S(2)}, u32[]{:S(2)}) collective-permute-start(bf16[128,1280]{1,0:T(8,128)(2,1)} %refs_0_.1), channel_id=1, source_target_pairs={{0,2},{1,3},{2,0},{3,1},{4,6},{5,7},{6,4},{7,5},{8,10},{9,11},{10,... | collective-permute-start | bytes 983048 | tf_op jit(solution)/shard_map/ppermute | solution.py:287
  4.3 2.3 %setup.1 = (bf16[128,1280]{1,0:T(8,128)(2,1)S(1)}, bf16[960,1280]{1,0:T(8,128)(2,1)S(1)}, bf16[320,1280]{1,0:T(8,128)(2,1)S(1)}, bf16[128,1280]{1,0:T(8,128)(2,1...) custom-call(bf16[128,1280]{1,0:T(8,128)(2,1)} %refs_0_.1, ...), custom_call_target="tpu_custom_call" | custom-call | flops 209715200 | bytes 4194304 | tf_op jit(solution)/shard_map/setup/pallas_call | solution.py:303
  6.5 0.0 collective-permute-done.1.x
  6.5 0.3 shard_map.131.xb
  6.8 0.0 slice-start
  6.9 1.5 %shard_map.132 = (bf16[320,256]{1,0:T(8,128)(2,1)S(1)}, bf16[320,256]{1,0:T(8,128)(2,1)S(1)}, bf16[320,256]{1,0:T(8,128)(2,1)S(1)}, f32[2,256]{1,0:T(2,128)S(1)}...) custom-call(bf16[128,1280]{1,0:T(8,128)(2,1)S(1)} %get-tuple-element.34.xa, bf16[128,1280]{1,0:T(8,128)(2,1)S(1)} %shard_map.131.xb, ...), custom_call_target="tpu_custom_call" | custom-call | flops 838860800 | bytes 1048576 | tf_op jit(solution)/shard_map/pallas_call | solution.py:337
  8.4 0.0 slice-start.1
  8.4 0.0 collective-permute-done.2.weight.wpair
  8.4 1.5 %shard_map.133 = (bf16[320,256]{1,0:T(8,128)(2,1)S(1)}, bf16[320,256]{1,0:T(8,128)(2,1)S(1)}, bf16[320,256]{1,0:T(8,128)(2,1)S(1)}, f32[2,256]{1,0:T(2,128)S(1)}...) custom-call(bf16[128,1280]{1,0:T(8,128)(2,1)S(1)} %get-tuple-element.34.xa, bf16[128,1280]{1,0:T(8,128)(2,1)S(1)} %shard_map.131.xb, ...), custom_call_target="tpu_custom_call" | custom-call | flops 838860800 | bytes 1048576 | tf_op jit(solution)/shard_map/pallas_call | solution.py:337
  10.0 2.8 %collective-permute-done.x = bf16[128,1280]{1,0:T(8,128)(2,1)S(1)} collective-permute-done((bf16[128,1280]{1,0:T(8,128)(2,1)}, bf16[128,1280]{1,0:T(8,128)(2,1)S(1)}, u32[]{:S(2)}, u32[]{:S(2)}) %collective-permute-start) | collective-permute-done | bytes 327712 | tf_op jit(solution)/shard_map/ppermute | solution.py:287
  12.8 0.3 shard_map.134.xa.x
  13.1 0.1 collective-permute-start.3
  13.2 0.0 collective-permute-done.4.ppair
  13.2 1.6 %collective-permute-done.3.xb = bf16[128,1280]{1,0:T(8,128)(2,1)S(1)} collective-permute-done((bf16[128,1280]{1,0:T(8,128)(2,1)S(1)}, bf16[128,1280]{1,0:T(8,128)(2,1)S(1)}, u32[]{:S(2)}, u32[]{:S(2)}) %collective-permute-start.3) | collective-permute-done | bytes 327712 | tf_op jit(solution)/shard_map/ppermute | solution.py:287
  14.8 0.0 slice-start.2
  14.8 3.5 %shard_map.135 = (f32[128,1280]{1,0:T(8,128)S(1)}, bf16[128,1280]{1,0:T(8,128)(2,1)S(1)}, bf16[640,256]{1,0:T(8,128)(2,1)S(1)}, bf16[640,256]{1,0:T(8,128)(2,1)S(1)}) custom-call(bf16[128,1280]{1,0:T(8,128)(2,1)S(1)} %shard_map.134.xa.x, bf16[128,1280]{1,0:T(8,128)(2,1)S(1)} %collective-permute-done.3.xb, ...), custom_call_target="tpu_custom_call" | custom-call | flops 1258291200 | bytes 1048576 | tf_op jit(solution)/shard_map/pallas_call | solution.py:349
  18.3 1.8 %collective-permute-start.6 = (bf16[128,1280]{1,0:T(8,128)(2,1)S(1)}, bf16[128,1280]{1,0:T(8,128)(2,1)S(1)}, u32[]{:S(2)}, u32[]{:S(2)}) collective-permute-start(bf16[128,1280]{1,0:T(8,128)(2,1)S(1)} %get-tuple-element.57), channel_id=1, source_target_pairs={{0,2},{1,3},{2,0},{3,1},{4,6},{5,7},{6,4},{7,5},{8,10},{9,11},{10,... | collective-permute-start | bytes 983048 | tf_op jit(solution)/shard_map/ppermute | solution.py:287
  20.1 0.0 slice-start.3
  20.1 3.1 %shard_map.136 = (f32[128,1280]{1,0:T(8,128)S(1)}, bf16[128,1280]{1,0:T(8,128)(2,1)S(1)}) custom-call(bf16[128,1280]{1,0:T(8,128)(2,1)S(1)} %shard_map.134.xa.x, bf16[960,1280]{1,0:T(8,128)(2,1)S(1)} %get-tuple-element.35.weight.wown, bf16[960,1280]{1,0:T(8,128)(2,1)S(1)} %collective-permute-done.2.weight.wpair, ...), custom_call_target="tpu_custom_call" | custom-call | flops 1258291200 | bytes 1048576 | tf_op jit(solution)/shard_map/pallas_call | solution.py:353
  23.2 4.9 %collective-permute-done.6.got = bf16[128,1280]{1,0:T(8,128)(2,1)S(1)} collective-permute-done((bf16[128,1280]{1,0:T(8,128)(2,1)S(1)}, bf16[128,1280]{1,0:T(8,128)(2,1)S(1)}, u32[]{:S(2)}, u32[]{:S(2)}) %collective-permute-start.6) | collective-permute-done | bytes 327712 | tf_op jit(solution)/shard_map/ppermute | solution.py:287
  28.1 0.4 shard_map.138.own
  28.5 0.1 collective-permute-start.7
  28.6 1.8 %collective-permute-start.5 = (bf16[128,1280]{1,0:T(8,128)(2,1)S(1)}, bf16[128,1280]{1,0:T(8,128)(2,1)S(1)}, u32[]{:S(2)}, u32[]{:S(2)}) collective-permute-start(bf16[128,1280]{1,0:T(8,128)(2,1)S(1)} %get-tuple-element.55), channel_id=1, source_target_pairs={{0,2},{1,3},{2,0},{3,1},{4,6},{5,7},{6,4},{7,5},{8,10},{9,11},{10,... | collective-permute-start | bytes 983048 | tf_op jit(solution)/shard_map/ppermute | solution.py:287
  30.4 0.0 collective-permute-done.7.pair
  30.4 0.0 slice-done
  30.4 0.0 slice-done.1
  30.4 0.0 slice-done.2
  30.4 0.0 slice-done.3
  30.4 2.4 %shard_map.139.rest_0_.early = bf16[64,1280]{1,0:T(8,128)(2,1)S(1)} custom-call(bf16[32,5120]{1,0:T(8,128)(2,1)S(1)} %shard_map.138.own, bf16[32,5120]{1,0:T(8,128)(2,1)S(1)} %collective-permute-done.7.pair, bf16[5120,1280]{1,0:T(8,128)(2,1)S(1)} %bitcast.4, f32[8,1280]{1,0:T(8,128)S(1)} %get-tuple-element.33.rows.x), custom_call_target="tpu_custom_call" | custom-call | flops 838860800 | bytes 1048576 | tf_op jit(solution)/shard_map/pallas_call | solution.py:375
  32.9 5.8 %collective-permute-done.5.got = bf16[128,1280]{1,0:T(8,128)(2,1)S(1)} collective-permute-done((bf16[128,1280]{1,0:T(8,128)(2,1)S(1)}, bf16[128,1280]{1,0:T(8,128)(2,1)S(1)}, u32[]{:S(2)}, u32[]{:S(2)}) %collective-permute-start.5) | collective-permute-done | bytes 327712 | tf_op jit(solution)/shard_map/ppermute | solution.py:287
  38.7 0.4 shard_map.140
  39.2 0.1 collective-permute-start.8
  39.2 1.6 %collective-permute-done.8.pair = bf16[32,5120]{1,0:T(8,128)(2,1)S(1)} collective-permute-done((bf16[32,5120]{1,0:T(8,128)(2,1)S(1)}, bf16[32,5120]{1,0:T(8,128)(2,1)S(1)}, u32[]{:S(2)}, u32[]{:S(2)}) %collective-permute-start.8) | collective-permute-done | bytes 327712 | tf_op jit(solution)/shard_map/ppermute | solution.py:287
  40.8 3.2 %hidden0.1 = (bf16[128,1280]{1,0:T(8,128)(2,1)}, bf16[128,1280]{1,0:T(8,128)(2,1)}) custom-call(bf16[32,5120]{1,0:T(8,128)(2,1)S(1)} %get-tuple-element.58.own, bf16[32,5120]{1,0:T(8,128)(2,1)S(1)} %collective-permute-done.8.pair, bf16[5120,1280]{1,0:T(8,128)(2,1)S(1)} %bitcast.4, f32[8,1280]{1,0:T(8,128)S(1)} %get-tuple-element.33.rows.x, ...), custom_call_target="tpu_custom_call" | custom-call | flops 838860800 | bytes 16777216 | tf_op jit(solution)/shard_map/hidden0/pallas_call | solution.py:379
  (2 shorter events, 0.0 us)
Async XLA Ops:
  0.6 7.8 %collective-permute-start.2 = (bf16[960,1280]{1,0:T(8,128)(2,1)}, bf16[960,1280]{1,0:T(8,128)(2,1)S(1)}, u32[]{:S(2)}, u32[]{:S(2)}) collective-permute-start(bf16[960,1280]{1,0:T(8,128)(2,1)} %bitcast.5), channel_id=1, source_target_pairs={{0,1},{1,0},{2,3},{3,2},{4,5},{5,4},{6,7},{7,6},{8,9},{9,8},{10,11... | collective-permute-start | bytes 7372808 | tf_op jit(solution)/shard_map/ppermute | solution.py:287
  1.2 5.3 %collective-permute-start.1 = (bf16[128,1280]{1,0:T(8,128)(2,1)}, bf16[128,1280]{1,0:T(8,128)(2,1)S(1)}, u32[]{:S(2)}, u32[]{:S(2)}) collective-permute-start(bf16[128,1280]{1,0:T(8,128)(2,1)} %refs_0_.1), channel_id=1, source_target_pairs={{0,1},{1,0},{2,3},{3,2},{4,5},{5,4},{6,7},{7,6},{8,9},{9,8},{10,11... | collective-permute-start | bytes 983048 | tf_op jit(solution)/shard_map/ppermute | solution.py:287
  1.3 11.9 %collective-permute-start.4 = (bf16[320,1280]{1,0:T(8,128)(2,1)}, bf16[320,1280]{1,0:T(8,128)(2,1)S(1)}, u32[]{:S(2)}, u32[]{:S(2)}) collective-permute-start(bf16[320,1280]{1,0:T(8,128)(2,1)} %refs_9_.1), channel_id=1, source_target_pairs={{0,1},{1,0},{2,3},{3,2},{4,5},{5,4},{6,7},{7,6},{8,9},{9,8},{10,11... | collective-permute-start | bytes 2457608 | tf_op jit(solution)/shard_map/ppermute | solution.py:287
  1.7 11.1 %collective-permute-start = (bf16[128,1280]{1,0:T(8,128)(2,1)}, bf16[128,1280]{1,0:T(8,128)(2,1)S(1)}, u32[]{:S(2)}, u32[]{:S(2)}) collective-permute-start(bf16[128,1280]{1,0:T(8,128)(2,1)} %refs_0_.1), channel_id=1, source_target_pairs={{0,2},{1,3},{2,0},{3,1},{4,6},{5,7},{6,4},{7,5},{8,10},{9,11},{10,... | collective-permute-start | bytes 983048 | tf_op jit(solution)/shard_map/ppermute | solution.py:287
  6.8 23.6 %slice-start = ((s8[13107200]{0:T(1024)(128)(4,1)}), s8[524288]{0:T(1024)(128)(4,1)S(1)}, s32[]{:S(2)}) async-start(s8[13107200]{0:T(1024)(128)(4,1)} %bitcast.3), calls=%async_computation | async-start | bytes 1048576
  8.4 22.0 %slice-start.1 = ((s8[13107200]{0:T(1024)(128)(4,1)}), s8[4194304]{0:T(1024)(128)(4,1)S(1)}, s32[]{:S(2)}) async-start(s8[13107200]{0:T(1024)(128)(4,1)} %bitcast.3), calls=%async_computation.1 | async-start | bytes 8388608
  13.1 1.7 %collective-permute-start.3 = (bf16[128,1280]{1,0:T(8,128)(2,1)S(1)}, bf16[128,1280]{1,0:T(8,128)(2,1)S(1)}, u32[]{:S(2)}, u32[]{:S(2)}) collective-permute-start(bf16[128,1280]{1,0:T(8,128)(2,1)S(1)} %shard_map.134.xa.x), channel_id=1, source_target_pairs={{0,1},{1,0},{2,3},{3,2},{4,5},{5,4},{6,7},{7,6},{8,9},{9,8},{10,11... | collective-permute-start | bytes 983048 | tf_op jit(solution)/shard_map/ppermute | solution.py:287
  14.8 15.6 %slice-start.2 = ((s8[13107200]{0:T(1024)(128)(4,1)}), s8[4194304]{0:T(1024)(128)(4,1)S(1)}, s32[]{:S(2)}) async-start(s8[13107200]{0:T(1024)(128)(4,1)} %bitcast.3), calls=%async_computation.2 | async-start | bytes 8388608
  18.3 9.8 %collective-permute-start.6 = (bf16[128,1280]{1,0:T(8,128)(2,1)S(1)}, bf16[128,1280]{1,0:T(8,128)(2,1)S(1)}, u32[]{:S(2)}, u32[]{:S(2)}) collective-permute-start(bf16[128,1280]{1,0:T(8,128)(2,1)S(1)} %get-tuple-element.57), channel_id=1, source_target_pairs={{0,2},{1,3},{2,0},{3,1},{4,6},{5,7},{6,4},{7,5},{8,10},{9,11},{10,... | collective-permute-start | bytes 983048 | tf_op jit(solution)/shard_map/ppermute | solution.py:287
  20.1 10.4 %slice-start.3 = ((s8[13107200]{0:T(1024)(128)(4,1)}), s8[4194304]{0:T(1024)(128)(4,1)S(1)}, s32[]{:S(2)}) async-start(s8[13107200]{0:T(1024)(128)(4,1)} %bitcast.3), calls=%async_computation.3 | async-start | bytes 8388608
  28.5 1.9 %collective-permute-start.7 = (bf16[32,5120]{1,0:T(8,128)(2,1)S(1)}, bf16[32,5120]{1,0:T(8,128)(2,1)S(1)}, u32[]{:S(2)}, u32[]{:S(2)}) collective-permute-start(bf16[32,5120]{1,0:T(8,128)(2,1)S(1)} %shard_map.138.own), channel_id=1, source_target_pairs={{0,1},{1,0},{2,3},{3,2},{4,5},{5,4},{6,7},{7,6},{8,9},{9,8},{10,11... | collective-permute-start | bytes 983048 | tf_op jit(solution)/shard_map/ppermute | solution.py:287
  28.6 10.1 %collective-permute-start.5 = (bf16[128,1280]{1,0:T(8,128)(2,1)S(1)}, bf16[128,1280]{1,0:T(8,128)(2,1)S(1)}, u32[]{:S(2)}, u32[]{:S(2)}) collective-permute-start(bf16[128,1280]{1,0:T(8,128)(2,1)S(1)} %get-tuple-element.55), channel_id=1, source_target_pairs={{0,2},{1,3},{2,0},{3,1},{4,6},{5,7},{6,4},{7,5},{8,10},{9,11},{10,... | collective-permute-start | bytes 983048 | tf_op jit(solution)/shard_map/ppermute | solution.py:287
  39.2 1.7 %collective-permute-start.8 = (bf16[32,5120]{1,0:T(8,128)(2,1)S(1)}, bf16[32,5120]{1,0:T(8,128)(2,1)S(1)}, u32[]{:S(2)}, u32[]{:S(2)}) collective-permute-start(bf16[32,5120]{1,0:T(8,128)(2,1)S(1)} %get-tuple-element.58.own), channel_id=1, source_target_pairs={{0,1},{1,0},{2,3},{3,2},{4,5},{5,4},{6,7},{7,6},{8,9},{9,8},{10,11... | collective-permute-start | bytes 983048 | tf_op jit(solution)/shard_map/ppermute | solution.py:287

commit v5 on v4

--- a/solution.py
+++ b/solution.py
@@ -42,9 +42,9 @@
 
 def setup_kernel(hdim, count, *refs):
     sources, rest = refs[:count], refs[count:]
-    x, wown, pown, normed, rows, qcol, cosine, sine, pos, qkv_bias = rest[:10]
+    x, wown, pall, normed, rows, qcol, cosine, sine, pos, qkv_bias = rest[:10]
     vectors, sems = rest[10:-1], rest[-1]
-    targets = (x, pos, qkv_bias) + tuple(vectors) + (pown, wown)
+    targets = (x, pos, qkv_bias) + tuple(vectors) + (pall.at[pl.ds(0, pall.shape[0] // 2)], wown)
     copies = [pltpu.make_async_copy(a, b, sems.at[n]) for n, (a, b) in enumerate(zip(sources, targets))]
     for copy in copies:
         copy.start()
@@ -78,9 +78,10 @@
     out[...] = x[...]
 
 
-def norm_kernel(x, rows, *rest):
+def norm_kernel(start, x, rows, *rest):
     out = rest[-1]
-    out[...] = layer_norm(x[...].astype(jnp.float32), rows[0:1, :], rows[1:2, :]).astype(jnp.bfloat16)
+    value = x[start : start + out.shape[0], :].astype(jnp.float32)
+    out[...] = layer_norm(value, rows[0:1, :], rows[1:2, :]).astype(jnp.bfloat16)
 
 
 def column(qcol, owner, local, c):
@@ -105,7 +106,14 @@
     return jnp.concatenate(rows, axis=0)
 
 
-def near_kernel(hdim, side, xa, xb, weight, qcol, cosine, sine, qout, kout, vout, tops, sums, outs):
+def near_kernel(hdim, side, xa, xb, weight, qcol, cosine, sine, *rest):
+    if side:
+        ppair, _, qout, kout, vout, tops, sums, outs, pall, sem = rest
+        count = ppair.shape[0]
+        copy = pltpu.make_async_copy(ppair, pall.at[pl.ds(count, count)], sem)
+        copy.start()
+    else:
+        qout, kout, vout, tops, sums, outs = rest
     scale = math.log2(math.e) / math.sqrt(hdim)
     local = weight.shape[0] // 3
     rows = xa.shape[0]
@@ -130,59 +138,59 @@
         total = dot(value[f], expo.astype(jnp.bfloat16), NN)
         outs[f.start : f.start + hdim, :] = total[:hdim, :rows]
         outs[f.start + hdim : f.stop, :] = total[hdim:, rows:]
-
-
-def far_kernel(hdim, xa, xb, wown, wpair, pown, ppair, qcol, cosine, sine, *refs):
+    if side:
+        copy.wait()
+
+
+def far_kernel(hdim, xa, xb, xc, xd, wown, wpair, pall, qcol, cosine, sine, *refs):
     scale = math.log2(math.e) / math.sqrt(hdim)
     near, (part, send, kout, vout) = (refs[:4], refs[4:8]), refs[8:]
     local = wown.shape[0] // 3
-    rows = xa.shape[0]
+    rows = 2 * xa.shape[0]
     me = lax.axis_index("sp")
-    normed = jnp.concatenate([xa[...], xb[...]], axis=0)
+    normed = jnp.concatenate([x[...] for x in (xa, xb, xc, xd)], axis=0)
     cos, sin = cosine[:, 2 * rows :], sine[:, 2 * rows :]
-    total = None
     for side, weight in enumerate((wown, wpair)):
-        q, tops, sums, outs = near[side]
         owner = me ^ side
         base = slice(side * local, (side + 1) * local)
         keyval = dot(weight[local:, :], normed, NT)
-        key = rotated(keyval[:local] + column(qcol, owner, local, 1), cos, sin, hdim)
-        value = (keyval[local:] + column(qcol, owner, local, 2)).astype(jnp.bfloat16)
-        kout[base, :] = key
-        vout[base, :] = value
-        pieces = []
+        kout[base, :] = rotated(keyval[:local] + column(qcol, owner, local, 1), cos, sin, hdim)
+        vout[base, :] = (keyval[local:] + column(qcol, owner, local, 2)).astype(jnp.bfloat16)
+    pieces = []
+    for side in range(2):
+        q, tops, sums, outs = near[side]
         for p in range(local // (2 * hdim)):
             f = slice(2 * p * hdim, 2 * (p + 1) * hdim)
-            scores = dot(key[f], q[f, :], TN)
+            g = slice(side * local + f.start, side * local + f.stop)
+            scores = dot(kout[g, :], q[f, :], TN)
             old = tops[p : p + 1, :]
             top = jnp.maximum(old, jnp.max(scores, axis=0, keepdims=True))
             expo = jnp.exp2((scores - top) * scale)
             shrink = jnp.exp2((old - top) * scale)
             inv = 1.0 / (sums[p : p + 1, :] * shrink + jnp.sum(expo, axis=0, keepdims=True))
-            late = dot(value[f], expo.astype(jnp.bfloat16), NN)
+            late = dot(vout[g, :], expo.astype(jnp.bfloat16), NN)
             for h in range(2):
                 lanes = slice(h * rows, (h + 1) * rows)
                 feats = slice(h * hdim, (h + 1) * hdim)
                 early = outs[f.start + h * hdim : f.start + (h + 1) * hdim, :]
                 mixed = (early * shrink[:, lanes] + late[feats, lanes]) * inv[:, lanes]
                 pieces.append(mixed.astype(jnp.bfloat16))
-        add = dot(jnp.concatenate(pieces, axis=0), (pown, ppair)[side][...], TN)
-        total = add if total is None else total + add
+    total = dot(jnp.concatenate(pieces, axis=0), pall[...], TN)
     part[...] = total
     send[...] = total.astype(jnp.bfloat16)
 
 
-def late_kernel(hdim, x, wown, wpair, pown, ppair, qcol, cosine, sine, kna, vna, knb, vnb, kf, vf, part, send):
+def late_kernel(hdim, xa, xb, wown, wpair, pall, qcol, cosine, sine, kna, vna, knb, vnb, kf, vf, part, send0, send1):
     scale = math.log2(math.e) / math.sqrt(hdim)
     local = wown.shape[0] // 3
-    rows = x.shape[0]
+    rows = 2 * xa.shape[0]
     me = lax.axis_index("sp")
-    total = None
+    normed = jnp.concatenate([xa[...], xb[...]], axis=0)
+    pieces = []
     for side, weight in enumerate((wown, wpair)):
-        query = dot(weight[:local, :], x[...], NT) + column(qcol, me ^ side, local, 0)
+        query = dot(weight[:local, :], normed, NT) + column(qcol, me ^ side, local, 0)
         far = slice(2 * rows, 3 * rows)
         query = paired(rotated(query, cosine[:, far], sine[:, far], hdim), hdim)
-        pieces = []
         for at in range(0, local, 2 * hdim):
             f = slice(side * local + at, side * local + at + 2 * hdim)
             g = slice(at, at + 2 * hdim)
@@ -197,21 +205,23 @@
             mixed = dot(vn[g, :], (en * inv).astype(jnp.bfloat16), NN)
             mixed = (mixed + dot(vf[f, :], (ef * inv).astype(jnp.bfloat16), NN)).astype(jnp.bfloat16)
             pieces += [mixed[:hdim, :rows], mixed[hdim:, rows:]]
-        add = dot(jnp.concatenate(pieces, axis=0), (pown, ppair)[side][...], TN)
-        total = add if total is None else total + add
+    total = dot(jnp.concatenate(pieces, axis=0), pall[...], TN)
     part[...] = total
-    send[...] = total.astype(jnp.bfloat16)
-
-
-def merge_kernel(keep, x, part, got, rows, *rest):
+    half = rows // 2
+    send0[...] = total[:half].astype(jnp.bfloat16)
+    send1[...] = total[half:].astype(jnp.bfloat16)
+
+
+def merge_kernel(keep, start, x, part, got, rows, *rest):
     blocks, scratch = rest[-2], rest[-1]
     width = x.shape[1]
-    value = x[...].astype(jnp.float32) + (part[...] + got[...].astype(jnp.float32)) + rows[2:3, :]
+    place = slice(start, start + got.shape[0])
+    value = x[place, :].astype(jnp.float32) + (part[place, :] + got[...].astype(jnp.float32)) + rows[2:3, :]
     rounded = value.astype(jnp.bfloat16)
     if keep:
         rest[-3][...] = rounded
     normed = layer_norm(rounded.astype(jnp.float32), rows[3:4, :], rows[4:5, :])
-    count = x.shape[0] // 4
+    count = got.shape[0] // 4
     lanes = scratch.shape[2]
     for t in range(width // lanes):
         scratch[t] = normed[:, t * lanes : (t + 1) * lanes]
@@ -227,32 +237,37 @@
 def hidden_kernel(own, pair, weight, rows, out):
     core = lax.axis_index("sp") % 2
     count = own.shape[0]
-    both = jnp.concatenate([own[...], pair[...]], axis=0)
-    hid = gelu(dot(both, weight[...], NN) + rows[5:6, :]).astype(jnp.bfloat16)
+    both = jnp.concatenate([own[...], pair[...]] * 2, axis=0)
+    hid = gelu(dot(both, weight[...], NN)[: 2 * count] + rows[5:6, :]).astype(jnp.bfloat16)
     for half, place in enumerate((core, 1 - core)):
         out[pl.ds(pl.multiple_of(place * count, count), count), :] = hid[half * count : (half + 1) * count]
 
 
-def last_kernel(own, pair, weight, rows, vit, early, out, vout, stage, sems):
+def last_kernel(own0, own1, pair0, pair1, weight, rows, vit0, vit1, early, out, vout, stage, sems):
     me = lax.axis_index("sp")
     chip, core = me // 2, me % 2
-    count = own.shape[0]
+    count = 2 * own0.shape[0]
+    half = vit0.shape[0]
     at = lambda start: pl.ds(pl.multiple_of(start, count), count)
-    copies = [pltpu.make_async_copy(vit, vout, sems.at[0])]
     there = out.at[pl.ds(pl.multiple_of((1 - chip) * 2 * count, count), 2 * count)]
-    copies.append(pltpu.make_async_copy(early, there, sems.at[1]))
+    copies = [
+        pltpu.make_async_copy(vit0, vout.at[pl.ds(0, half)], sems.at[0]),
+        pltpu.make_async_copy(vit1, vout.at[pl.ds(half, half)], sems.at[1]),
+        pltpu.make_async_copy(early, there, sems.at[2]),
+    ]
     for copy in copies:
         copy.start()
-    both = jnp.concatenate([own[...], pair[...]], axis=0)
+    both = jnp.concatenate([x[...] for x in (own0, own1, pair0, pair1)] * 2, axis=0)
     step = stage.shape[2]
     for n in range(stage.shape[0]):
         cols = slice(n * step, (n + 1) * step)
-        stage[n] = gelu(dot(both, weight[:, cols], NN) + rows[5:6, cols]).astype(jnp.bfloat16)
-        for half, place in enumerate((core, 1 - core)):
+        value = dot(both, weight[:, cols], NN)[: 2 * count] + rows[5:6, cols]
+        stage[n] = gelu(value).astype(jnp.bfloat16)
+        for side, place in enumerate((core, 1 - core)):
             copy = pltpu.make_async_copy(
-                stage.at[n, pl.ds(half * count, count)],
+                stage.at[n, pl.ds(side * count, count)],
                 out.at[at(chip * 2 * count + place * count), pl.ds(n * step, step)],
-                sems.at[2 + 2 * n + half],
+                sems.at[3 + 2 * n + side],
             )
             copy.start()
             copies.append(copy)
@@ -293,19 +308,18 @@
     p_pair = swap(proj_weight, 1)
 
     both = 2 * local
-    part_shape = (shape((prow, width), jnp.float32), shape((prow, width)))
     mul = 2 * prow * width * local * 2
     table = shape((hdim // 2, 4 * prow), jnp.float32)
 
     sources = (patches, pos_ids, qkv_bias, norm_gain, norm_bias, proj_bias, merge_gain, merge_bias, fc1_bias)
     sources += (proj_weight, weight)
     held = lambda v: pltpu.VMEM(v.shape, v.dtype)
-    x_own, w_own, p_own, n_own, rows, qcol, cos, sin = pl.pallas_call(
+    x_own, w_own, p_half, n_own, rows, qcol, cos, sin = pl.pallas_call(
         functools.partial(setup_kernel, hdim, len(sources)),
         out_shape=(
             held(patches),
             held(weight),
-            held(proj_weight),
+            pltpu.VMEM((both, width), proj_weight.dtype),
             shape((prow, width)),
             shape((8, width), jnp.float32),
             shape((width, 8), jnp.float32),
@@ -319,62 +333,77 @@
         name="setup",
     )(*(pltpu.with_memory_space_constraint(v, pltpu.HBM) for v in sources))
 
-    def norm(x, *after):
+    def norm(x, start, count, *after):
         return pl.pallas_call(
-            norm_kernel,
-            out_shape=shape((prow, width)),
+            functools.partial(norm_kernel, start),
+            out_shape=shape((count, width)),
             in_specs=[VMEM] * 2 + [ANY] * len(after),
             compiler_params=pltpu.CompilerParams(vmem_limit_bytes=4 * MIB),
             cost_estimate=pl.CostEstimate(flops=mul // 4, bytes_accessed=1 << 20, transcendentals=0),
         )(x, rows, *after)
 
-    n_pair = norm(x_pair)
+    n_pair = norm(x_pair, 0, prow)
     flat = shape((local, 2 * prow))
     state = shape((local // (2 * hdim), 2 * prow), jnp.float32)
     near_shape = (flat, flat, flat, state, state, shape((local, prow), jnp.float32))
 
-    def near(side, weight):
-        q, k, v, *rest = call(
-            functools.partial(near_kernel, hdim, side), near_shape, 8 * MIB, 4 * mul
-        )(n_own, n_pair, weight, qcol, cos, sin)
-        return (q, *rest), (k, v)
-
-    early_own, kv_own = near(0, w_own)
-    early_pair, kv_pair = near(1, w_pair)
-
-    n_far = norm(x_far, early_own[1], early_pair[1])
-    n_farpair = swap(n_far, 1)
+    def near(side, weight, *more):
+        return pl.pallas_call(
+            functools.partial(near_kernel, hdim, side),
+            out_shape=near_shape + (pltpu.VMEM((both, width), proj_weight.dtype),) * side,
+            input_output_aliases={7: 6} if side else {},
+            scratch_shapes=[pltpu.SemaphoreType.DMA] * side,
+            compiler_params=pltpu.CompilerParams(vmem_limit_bytes=8 * MIB),
+            cost_estimate=pl.CostEstimate(flops=4 * mul, bytes_accessed=1 << 22, transcendentals=0),
+        )(n_own, n_pair, weight, qcol, cos, sin, *more)
+
+    q, *kv_own, tops, sums, outs = near(0, w_own)
+    early_own = (q, tops, sums, outs)
+    q, *kv_pair, tops, sums, outs, p_all = near(1, w_pair, p_pair, p_half)
+    early_pair = (q, tops, sums, outs)
+
+    half = prow // 2
+    n_far0 = norm(x_far, 0, half, early_own[1], p_all)
+    n_farpair0 = swap(n_far0, 1)
+    n_far1 = norm(x_far, half, half, n_far0)
+    n_farpair1 = swap(n_far1, 1)
     tall = shape((both, 2 * prow))
-    shared = (w_own, w_pair, p_own, p_pair, qcol, cos, sin)
+    shared = (w_own, w_pair, p_all, qcol, cos, sin)
+    part_shape = shape((prow, width), jnp.float32)
     part0, send0, k_far, v_far = call(
-        functools.partial(far_kernel, hdim), part_shape + (tall, tall), 8 * MIB, 6 * mul
-    )(n_far, n_farpair, *shared, *early_own, *early_pair)
+        functools.partial(far_kernel, hdim), (part_shape, shape((prow, width)), tall, tall), 8 * MIB, 6 * mul
+    )(n_far0, n_far1, n_farpair0, n_farpair1, *shared, *early_own, *early_pair)
     got1 = swap(send0, 2)
-    part1, send1 = call(
-        functools.partial(late_kernel, hdim), part_shape, 8 * MIB, 6 * mul
-    )(n_far, *shared, *kv_own, *kv_pair, k_far, v_far)
-    got0 = swap(send1, 2)
+    halves = (shape((half, width)), shape((half, width)))
+    part1, send1a, send1b = call(
+        functools.partial(late_kernel, hdim), (part_shape,) + halves, 8 * MIB, 6 * mul
+    )(n_far0, n_far1, *shared, *kv_own, *kv_pair, k_far, v_far)
+    got0a = swap(send1a, 2)
+    got0b = swap(send1b, 2)
     late_rows = call(copy_kernel, shape(rows.shape, rows.dtype), MIB, 1000)(rows)
 
-    blocks_shape = shape((prow // 4, 4 * width))
-
-    def merge(x, part, got, outs, *after):
+    def merge(keep, start, x, part, got, late_rows, *after):
+        count = got.shape[0]
+        outs = (shape((count, width)),) * keep + (shape((count // 4, 4 * width)),)
         return pl.pallas_call(
-            functools.partial(merge_kernel, len(outs) == 2),
+            functools.partial(merge_kernel, keep, start),
             out_shape=outs,
             in_specs=[VMEM] * 4 + [ANY] * len(after),
-            scratch_shapes=[pltpu.VMEM((width // 128, prow, 128), jnp.float32)],
+            scratch_shapes=[pltpu.VMEM((width // 128, count, 128), jnp.float32)],
             compiler_params=pltpu.CompilerParams(vmem_limit_bytes=4 * MIB),
             cost_estimate=pl.CostEstimate(flops=mul // 4, bytes_accessed=1 << 20, transcendentals=0),
         )(x, part, got, late_rows, *after)
 
     fc1 = pltpu.with_memory_space_constraint(fc1_weight, pltpu.VMEM)
-    (blocks1,) = merge(x_far, part1, got1, (blocks_shape,))
+    (blocks1,) = merge(0, 0, x_far, part1, got1, late_rows)
     pair1 = swap(blocks1, 1)
     flops = prow * 4 * width * hidden
     early = call(hidden_kernel, shape((prow // 2, hidden)), 4 * MIB, flops)(blocks1, pair1, fc1, rows)
-    vit, blocks0 = merge(x_own, part0, got0, (shape((prow, width)), blocks_shape), early)
-    pair0 = swap(blocks0, 1)
+    vit_a, blocks_a = merge(1, 0, x_own, part0, got0a, late_rows, early)
+    pair_a = swap(blocks_a, 1)
+    late_rows = call(copy_kernel, shape(rows.shape, rows.dtype), MIB, 1000)(late_rows)
+    vit_b, blocks_b = merge(1, half, x_own, part0, got0b, late_rows)
+    pair_b = swap(blocks_b, 1)
     parts = hidden // 256
     merged, vit_out = pl.pallas_call(
         last_kernel,
@@ -382,12 +411,12 @@
         out_specs=[HBM] * 2,
         scratch_shapes=[
             pltpu.VMEM((parts, prow // 2, 256), jnp.bfloat16),
-            pltpu.SemaphoreType.DMA((2 + 2 * parts,)),
+            pltpu.SemaphoreType.DMA((3 + 2 * parts,)),
         ],
         compiler_params=pltpu.CompilerParams(vmem_limit_bytes=4 * MIB),
         cost_estimate=pl.CostEstimate(flops=flops, bytes_accessed=1 << 24, transcendentals=0),
         name="hidden0",
-    )(blocks0, pair0, fc1, rows, vit, early)
+    )(blocks_a, blocks_b, pair_a, pair_b, fc1, rows, vit_a, vit_b, early)
     return vit_out, merged
 
 

time: 44.2 us -> 42.8 us (0.968)
  Pallas kernels: 19 us -> 17.6 us
  waiting for transfers between devices: 16.7 us -> 15.7 us
  starting transfers between devices: 7.45 us -> 8.3 us
    ppermute x9 -> x12, waiting for transfers between devices: 16.7 us -> 15.7 us  [swap(): return lax.ppermute(value, 'sp', [(i, i ^ bit) for i in range(4)])]
    ppermute x9 -> x12, starting transfers between devices: 7.45 us -> 8.3 us  [swap(): return lax.ppermute(value, 'sp', [(i, i ^ bit) for i in range(4)])]
    pallas_call x1, Pallas kernels: 3.18 us -> 2.69 us  [two_chips(): pl.pallas_call(last_kernel, out_shape=(shape((prow, hidden)), shape((prow...]
    pallas_call x1, Pallas kernels: 2.43 us -> 1.95 us  [two_chips(): call(hidden_kernel, shape((prow // 2, hidden)), 4 * MIB, flops)]
    pallas_call x8 -> x11, Pallas kernels: 11.1 us -> 10.7 us  [the longest x2 3.35 us: near(): pl.pallas_call(functools.partial(near_kernel, hdim, side), out_shape=near...]
  transfers between devices with their start and end apart: 9 -> 12, of which waited for: 5 -> 8; matrix products, arithmetic and copies ran while one was open for 0% -> 0% of each run, Pallas kernels for 26% -> 27%
where the time goes in v5:
time: 42.8 us; the launch traced here: 42.6 us
  Pallas kernels  17.6 us (41%)
  waiting for transfers between devices  15.7 us (37%)
  starting transfers between devices  8.3 us (19%)
  between operations  1 us (2%)
    ppermute x12, waiting for transfers between devices, swap(): return lax.ppermute(value, 'sp', [(i, i ^ bit) for i in range(4)])  15.7 us
    ppermute x12, starting transfers between devices, swap(): return lax.ppermute(value, 'sp', [(i, i ^ bit) for i in range(4)])  8.3 us
    pallas_call x2, Pallas kernels, near(): pl.pallas_call(functools.partial(near_kernel, hdim, side), out_shape=near...  3.35 us
    pallas_call x1, Pallas kernels, two_chips(): call(functools.partial(late_kernel, hdim), (part_shape,) + halves, 8 * MI...  3.07 us
    pallas_call x1, Pallas kernels, two_chips(): pl.pallas_call(last_kernel, out_shape=(shape((prow, hidden)), shape((prow...  2.69 us
    pallas_call x1, Pallas kernels, two_chips(): call(functools.partial(far_kernel, hdim), (part_shape, shape((prow, width...  2.46 us
    pallas_call x1, Pallas kernels, two_chips(): pl.pallas_call(functools.partial(setup_kernel, hdim, len(sources)), out_s...  2.27 us
    pallas_call x1, Pallas kernels, two_chips(): call(hidden_kernel, shape((prow // 2, hidden)), 4 * MIB, flops)  1.95 us
  transfers between devices with their start and end apart: 12, of which 8 were waited for; matrix products, arithmetic and copies ran while one was open for 0% of the time, Pallas kernels for 27%

profile of v5, /device:TPU:0, one launch (start us, length us, event | category | flops | bytes accessed | tf_op | source)
XLA Modules:
  0.0 42.6 jit_solution(13721547094831999269)
XLA Ops:
  0.6 0.6 %collective-permute-start.2 = (bf16[960,1280]{1,0:T(8,128)(2,1)}, bf16[960,1280]{1,0:T(8,128)(2,1)S(1)}, u32[]{:S(2)}, u32[]{:S(2)}) collective-permute-start(bf16[960,1280]{1,0:T(8,128)(2,1)} %bitcast.5), channel_id=1, source_target_pairs={{0,1},{1,0},{2,3},{3,2},{4,5},{5,4},{6,7},{7,6},{8,9},{9,8},{10,11... | collective-permute-start | bytes 7372808 | tf_op jit(solution)/shard_map/ppermute | solution.py:302
  1.2 0.1 collective-permute-start.3
  1.3 0.4 %collective-permute-start.1 = (bf16[128,1280]{1,0:T(8,128)(2,1)}, bf16[128,1280]{1,0:T(8,128)(2,1)S(1)}, u32[]{:S(2)}, u32[]{:S(2)}) collective-permute-start(bf16[128,1280]{1,0:T(8,128)(2,1)} %refs_0_.1), channel_id=1, source_target_pairs={{0,1},{1,0},{2,3},{3,2},{4,5},{5,4},{6,7},{7,6},{8,9},{9,8},{10,11... | collective-permute-start | bytes 983048 | tf_op jit(solution)/shard_map/ppermute | solution.py:302
  1.7 2.6 %collective-permute-start = (bf16[128,1280]{1,0:T(8,128)(2,1)}, bf16[128,1280]{1,0:T(8,128)(2,1)S(1)}, u32[]{:S(2)}, u32[]{:S(2)}) collective-permute-start(bf16[128,1280]{1,0:T(8,128)(2,1)} %refs_0_.1), channel_id=1, source_target_pairs={{0,2},{1,3},{2,0},{3,1},{4,6},{5,7},{6,4},{7,5},{8,10},{9,11},{10,... | collective-permute-start | bytes 983048 | tf_op jit(solution)/shard_map/ppermute | solution.py:302
  4.3 2.3 %setup.1 = (bf16[128,1280]{1,0:T(8,128)(2,1)S(1)}, bf16[960,1280]{1,0:T(8,128)(2,1)S(1)}, bf16[640,1280]{1,0:T(8,128)(2,1)S(1)}, bf16[128,1280]{1,0:T(8,128)(2,1...) custom-call(bf16[128,1280]{1,0:T(8,128)(2,1)} %refs_0_.1, ...), custom_call_target="tpu_custom_call" | custom-call | flops 209715200 | bytes 4194304 | tf_op jit(solution)/shard_map/setup/pallas_call | solution.py:317
  6.5 0.8 %collective-permute-done.1.x = bf16[128,1280]{1,0:T(8,128)(2,1)S(1)} collective-permute-done((bf16[128,1280]{1,0:T(8,128)(2,1)}, bf16[128,1280]{1,0:T(8,128)(2,1)S(1)}, u32[]{:S(2)}, u32[]{:S(2)}) %collective-permute-start.1) | collective-permute-done | bytes 327712 | tf_op jit(solution)/shard_map/ppermute | solution.py:302
  7.3 0.3 shard_map.131.xb
  7.6 1.5 %shard_map.132 = (bf16[320,256]{1,0:T(8,128)(2,1)S(1)}, bf16[320,256]{1,0:T(8,128)(2,1)S(1)}, bf16[320,256]{1,0:T(8,128)(2,1)S(1)}, f32[2,256]{1,0:T(2,128)S(1)}...) custom-call(bf16[128,1280]{1,0:T(8,128)(2,1)S(1)} %get-tuple-element.38.xa, bf16[128,1280]{1,0:T(8,128)(2,1)S(1)} %shard_map.131.xb, ...), custom_call_target="tpu_custom_call" | custom-call | flops 838860800 | bytes 4194304 | tf_op jit(solution)/shard_map/pallas_call | solution.py:351
  9.2 0.0 collective-permute-done.3.rest_0_
  9.2 0.0 collective-permute-done.2.weight.wpair
  9.2 0.0 slice-start
  9.2 1.8 %shard_map.133 = (bf16[320,256]{1,0:T(8,128)(2,1)S(1)}, bf16[320,256]{1,0:T(8,128)(2,1)S(1)}, bf16[320,256]{1,0:T(8,128)(2,1)S(1)}, f32[2,256]{1,0:T(2,128)S(1)}...) custom-call(bf16[128,1280]{1,0:T(8,128)(2,1)S(1)} %get-tuple-element, ...), custom_call_target="tpu_custom_call", output_to_operand_aliasing={{6}: (7, {})} | custom-call | flops 838860800 | bytes 4194304 | tf_op jit(solution)/shard_map/pallas_call | solution.py:351
  11.0 1.7 %collective-permute-done.x = bf16[128,1280]{1,0:T(8,128)(2,1)S(1)} collective-permute-done((bf16[128,1280]{1,0:T(8,128)(2,1)}, bf16[128,1280]{1,0:T(8,128)(2,1)S(1)}, u32[]{:S(2)}, u32[]{:S(2)}) %collective-permute-start) | collective-permute-done | bytes 327712 | tf_op jit(solution)/shard_map/ppermute | solution.py:302
  12.8 0.0 slice-start.1
  12.8 0.2 shard_map.134.rest_0_.xa
  13.0 0.2 shard_map.135.xb
  13.3 0.1 collective-permute-start.5
  13.3 0.5 %collective-permute-start.4 = (bf16[64,1280]{1,0:T(8,128)(2,1)S(1)}, bf16[64,1280]{1,0:T(8,128)(2,1)S(1)}, u32[]{:S(2)}, u32[]{:S(2)}) collective-permute-start(bf16[64,1280]{1,0:T(8,128)(2,1)S(1)} %shard_map.134.rest_0_.xa), channel_id=1, source_target_pairs={{0,1},{1,0},{2,3},{3,2},{4,5},{5,4},{6,7},{7,6},{8,9},{9,8},{10,11... | collective-permute-start | bytes 491528 | tf_op jit(solution)/shard_map/ppermute | solution.py:302
  13.8 0.9 %collective-permute-done.5.xd = bf16[64,1280]{1,0:T(8,128)(2,1)S(1)} collective-permute-done((bf16[64,1280]{1,0:T(8,128)(2,1)S(1)}, bf16[64,1280]{1,0:T(8,128)(2,1)S(1)}, u32[]{:S(2)}, u32[]{:S(2)}) %collective-permute-start.5) | collective-permute-done | bytes 163872 | tf_op jit(solution)/shard_map/ppermute | solution.py:302
  14.7 0.2 collective-permute-done.4.xc
  14.9 0.0 slice-start.2
  15.0 2.5 %shard_map.136 = (f32[128,1280]{1,0:T(8,128)S(1)}, bf16[128,1280]{1,0:T(8,128)(2,1)S(1)}, bf16[640,256]{1,0:T(8,128)(2,1)S(1)}, bf16[640,256]{1,0:T(8,128)(2,1)S(1)}) custom-call(bf16[64,1280]{1,0:T(8,128)(2,1)S(1)} %shard_map.134.rest_0_.xa, bf16[64,1280]{1,0:T(8,128)(2,1)S(1)} %shard_map.135.xb, bf16[64,1280]{1,0:T(8,128)(2,1)S(1)} %collective-permute-done.4.xc, ...), custom_call_target="tpu_custom_call" | custom-call | flops 1258291200 | bytes 1048576 | tf_op jit(solution)/shard_map/pallas_call | solution.py:373
  17.4 1.8 %collective-permute-start.7 = (bf16[128,1280]{1,0:T(8,128)(2,1)S(1)}, bf16[128,1280]{1,0:T(8,128)(2,1)S(1)}, u32[]{:S(2)}, u32[]{:S(2)}) collective-permute-start(bf16[128,1280]{1,0:T(8,128)(2,1)S(1)} %get-tuple-element.62), channel_id=1, source_target_pairs={{0,2},{1,3},{2,0},{3,1},{4,6},{5,7},{6,4},{7,5},{8,10},{9,11},{10,... | collective-permute-start | bytes 983048 | tf_op jit(solution)/shard_map/ppermute | solution.py:302
  19.2 0.0 slice-start.3
  19.2 3.1 %shard_map.137 = (f32[128,1280]{1,0:T(8,128)S(1)}, bf16[64,1280]{1,0:T(8,128)(2,1)S(1)}, bf16[64,1280]{1,0:T(8,128)(2,1)S(1)}) custom-call(bf16[64,1280]{1,0:T(8,128)(2,1)S(1)} %shard_map.134.rest_0_.xa, bf16[64,1280]{1,0:T(8,128)(2,1)S(1)} %shard_map.135.xb, bf16[960,1280]{1,0:T(8,128)(2,1)S(1)} %get-tuple-element.39.weight.wown, ...), custom_call_target="tpu_custom_call" | custom-call | flops 1258291200 | bytes 1048576 | tf_op jit(solution)/shard_map/pallas_call | solution.py:378
  22.3 5.1 %collective-permute-done.7.got = bf16[128,1280]{1,0:T(8,128)(2,1)S(1)} collective-permute-done((bf16[128,1280]{1,0:T(8,128)(2,1)S(1)}, bf16[128,1280]{1,0:T(8,128)(2,1)S(1)}, u32[]{:S(2)}, u32[]{:S(2)}) %collective-permute-start.7) | collective-permute-done | bytes 327712 | tf_op jit(solution)/shard_map/ppermute | solution.py:302
  27.4 0.4 %shard_map.139.own = bf16[32,5120]{1,0:T(8,128)(2,1)S(1)} custom-call(bf16[128,1280]{1,0:T(8,128)(2,1)S(1)} %collective-permute-done.x, f32[128,1280]{1,0:T(8,128)S(1)} %get-tuple-element.61.part, bf16[128,1280]{1,0:T(8,128)(2,1)S(1)} %collective-permute-done.7.got, f32[8,1280]{1,0:T(8,128)S(1)} %shard_map.138.rows.x), custom_call_target="tpu_custom_call" | custom-call | flops 52428800 | bytes 1048576 | tf_op jit(solution)/shard_map/pallas_call | solution.py:388
  27.8 0.1 collective-permute-start.8
  27.9 1.8 %collective-permute-start.9 = (bf16[64,1280]{1,0:T(8,128)(2,1)S(1)}, bf16[64,1280]{1,0:T(8,128)(2,1)S(1)}, u32[]{:S(2)}, u32[]{:S(2)}) collective-permute-start(bf16[64,1280]{1,0:T(8,128)(2,1)S(1)} %get-tuple-element.64), channel_id=1, source_target_pairs={{0,2},{1,3},{2,0},{3,1},{4,6},{5,7},{6,4},{7,5},{8,10},{9,11},{10,... | collective-permute-start | bytes 491528 | tf_op jit(solution)/shard_map/ppermute | solution.py:302
  29.7 0.3 collective-permute-start.6
  30.0 5.0 %collective-permute-done.9.got = bf16[64,1280]{1,0:T(8,128)(2,1)S(1)} collective-permute-done((bf16[64,1280]{1,0:T(8,128)(2,1)S(1)}, bf16[64,1280]{1,0:T(8,128)(2,1)S(1)}, u32[]{:S(2)}, u32[]{:S(2)}) %collective-permute-start.9) | collective-permute-done | bytes 163872 | tf_op jit(solution)/shard_map/ppermute | solution.py:302
  35.0 0.3 shard_map.143
  35.3 0.1 collective-permute-start.11
  35.4 0.0 collective-permute-done.8.pair
  35.4 0.0 slice-done
  35.4 0.0 slice-done.1
  35.5 0.0 slice-done.2
  35.5 0.0 slice-done.3
  35.5 1.9 %shard_map.140.rest_0_.early = bf16[64,1280]{1,0:T(8,128)(2,1)S(1)} custom-call(bf16[32,5120]{1,0:T(8,128)(2,1)S(1)} %shard_map.139.own, bf16[32,5120]{1,0:T(8,128)(2,1)S(1)} %collective-permute-done.8.pair, bf16[5120,1280]{1,0:T(8,128)(2,1)S(1)} %bitcast.4, f32[8,1280]{1,0:T(8,128)S(1)} %get-tuple-element.37.rows.x), custom_call_target="tpu_custom_call" | custom-call | flops 838860800 | bytes 1048576 | tf_op jit(solution)/shard_map/pallas_call | solution.py:401
  37.4 0.6 %collective-permute-done.6.got = bf16[64,1280]{1,0:T(8,128)(2,1)S(1)} collective-permute-done((bf16[64,1280]{1,0:T(8,128)(2,1)S(1)}, bf16[64,1280]{1,0:T(8,128)(2,1)S(1)}, u32[]{:S(2)}, u32[]{:S(2)}) %collective-permute-start.6) | collective-permute-done | bytes 163872 | tf_op jit(solution)/shard_map/ppermute | solution.py:302
  38.0 0.3 shard_map.141
  38.3 0.1 collective-permute-start.10
  38.4 0.0 collective-permute-done.11.pair1
  38.4 1.4 %collective-permute-done.10.pair0 = bf16[16,5120]{1,0:T(8,128)(2,1)S(1)} collective-permute-done((bf16[16,5120]{1,0:T(8,128)(2,1)S(1)}, bf16[16,5120]{1,0:T(8,128)(2,1)S(1)}, u32[]{:S(2)}, u32[]{:S(2)}) %collective-permute-start.10) | collective-permute-done | bytes 163872 | tf_op jit(solution)/shard_map/ppermute | solution.py:302
  39.8 2.7 %hidden0.1 = (bf16[128,1280]{1,0:T(8,128)(2,1)}, bf16[128,1280]{1,0:T(8,128)(2,1)}) custom-call(bf16[16,5120]{1,0:T(8,128)(2,1)S(1)} %get-tuple-element.63.own0, bf16[16,5120]{1,0:T(8,128)(2,1)S(1)} %get-tuple-element.65.own1, bf16[16,5120]{1,0:T(8,128)(2,1)S(1)} %collective-permute-done.10.pair0, bf16[16,5120]{1,0:T(8,128)(2,1)S(1)} %collective-permute-done.11.pair1, ...), custom_call_target="tpu_custom_call" | custom-call | flops 838860800 | bytes 16777216 | tf_op jit(solution)/shard_map/hidden0/pallas_call | solution.py:408
  (3 shorter events, 0.0 us)
Async XLA Ops:
  0.6 8.6 %collective-permute-start.2 = (bf16[960,1280]{1,0:T(8,128)(2,1)}, bf16[960,1280]{1,0:T(8,128)(2,1)S(1)}, u32[]{:S(2)}, u32[]{:S(2)}) collective-permute-start(bf16[960,1280]{1,0:T(8,128)(2,1)} %bitcast.5), channel_id=1, source_target_pairs={{0,1},{1,0},{2,3},{3,2},{4,5},{5,4},{6,7},{7,6},{8,9},{9,8},{10,11... | collective-permute-start | bytes 7372808 | tf_op jit(solution)/shard_map/ppermute | solution.py:302
  1.2 8.0 %collective-permute-start.3 = (bf16[320,1280]{1,0:T(8,128)(2,1)}, bf16[320,1280]{1,0:T(8,128)(2,1)S(1)}, u32[]{:S(2)}, u32[]{:S(2)}) collective-permute-start(bf16[320,1280]{1,0:T(8,128)(2,1)} %refs_9_.1), channel_id=1, source_target_pairs={{0,1},{1,0},{2,3},{3,2},{4,5},{5,4},{6,7},{7,6},{8,9},{9,8},{10,11... | collective-permute-start | bytes 2457608 | tf_op jit(solution)/shard_map/ppermute | solution.py:302
  1.3 6.1 %collective-permute-start.1 = (bf16[128,1280]{1,0:T(8,128)(2,1)}, bf16[128,1280]{1,0:T(8,128)(2,1)S(1)}, u32[]{:S(2)}, u32[]{:S(2)}) collective-permute-start(bf16[128,1280]{1,0:T(8,128)(2,1)} %refs_0_.1), channel_id=1, source_target_pairs={{0,1},{1,0},{2,3},{3,2},{4,5},{5,4},{6,7},{7,6},{8,9},{9,8},{10,11... | collective-permute-start | bytes 983048 | tf_op jit(solution)/shard_map/ppermute | solution.py:302
  1.7 11.1 %collective-permute-start = (bf16[128,1280]{1,0:T(8,128)(2,1)}, bf16[128,1280]{1,0:T(8,128)(2,1)S(1)}, u32[]{:S(2)}, u32[]{:S(2)}) collective-permute-start(bf16[128,1280]{1,0:T(8,128)(2,1)} %refs_0_.1), channel_id=1, source_target_pairs={{0,2},{1,3},{2,0},{3,1},{4,6},{5,7},{6,4},{7,5},{8,10},{9,11},{10,... | collective-permute-start | bytes 983048 | tf_op jit(solution)/shard_map/ppermute | solution.py:302
  9.2 26.2 %slice-start = ((s8[13107200]{0:T(1024)(128)(4,1)}), s8[524288]{0:T(1024)(128)(4,1)S(1)}, s32[]{:S(2)}) async-start(s8[13107200]{0:T(1024)(128)(4,1)} %bitcast.3), calls=%async_computation | async-start | bytes 1048576
  12.8 22.7 %slice-start.1 = ((s8[13107200]{0:T(1024)(128)(4,1)}), s8[4194304]{0:T(1024)(128)(4,1)S(1)}, s32[]{:S(2)}) async-start(s8[13107200]{0:T(1024)(128)(4,1)} %bitcast.3), calls=%async_computation.1 | async-start | bytes 8388608
  13.3 1.5 %collective-permute-start.5 = (bf16[64,1280]{1,0:T(8,128)(2,1)S(1)}, bf16[64,1280]{1,0:T(8,128)(2,1)S(1)}, u32[]{:S(2)}, u32[]{:S(2)}) collective-permute-start(bf16[64,1280]{1,0:T(8,128)(2,1)S(1)} %shard_map.135.xb), channel_id=1, source_target_pairs={{0,1},{1,0},{2,3},{3,2},{4,5},{5,4},{6,7},{7,6},{8,9},{9,8},{10,11... | collective-permute-start | bytes 491528 | tf_op jit(solution)/shard_map/ppermute | solution.py:302
  13.3 1.6 %collective-permute-start.4 = (bf16[64,1280]{1,0:T(8,128)(2,1)S(1)}, bf16[64,1280]{1,0:T(8,128)(2,1)S(1)}, u32[]{:S(2)}, u32[]{:S(2)}) collective-permute-start(bf16[64,1280]{1,0:T(8,128)(2,1)S(1)} %shard_map.134.rest_0_.xa), channel_id=1, source_target_pairs={{0,1},{1,0},{2,3},{3,2},{4,5},{5,4},{6,7},{7,6},{8,9},{9,8},{10,11... | collective-permute-start | bytes 491528 | tf_op jit(solution)/shard_map/ppermute | solution.py:302
  14.9 20.5 %slice-start.2 = ((s8[13107200]{0:T(1024)(128)(4,1)}), s8[4194304]{0:T(1024)(128)(4,1)S(1)}, s32[]{:S(2)}) async-start(s8[13107200]{0:T(1024)(128)(4,1)} %bitcast.3), calls=%async_computation.2 | async-start | bytes 8388608
  17.4 10.0 %collective-permute-start.7 = (bf16[128,1280]{1,0:T(8,128)(2,1)S(1)}, bf16[128,1280]{1,0:T(8,128)(2,1)S(1)}, u32[]{:S(2)}, u32[]{:S(2)}) collective-permute-start(bf16[128,1280]{1,0:T(8,128)(2,1)S(1)} %get-tuple-element.62), channel_id=1, source_target_pairs={{0,2},{1,3},{2,0},{3,1},{4,6},{5,7},{6,4},{7,5},{8,10},{9,11},{10,... | collective-permute-start | bytes 983048 | tf_op jit(solution)/shard_map/ppermute | solution.py:302
  19.2 16.2 %slice-start.3 = ((s8[13107200]{0:T(1024)(128)(4,1)}), s8[4194304]{0:T(1024)(128)(4,1)S(1)}, s32[]{:S(2)}) async-start(s8[13107200]{0:T(1024)(128)(4,1)} %bitcast.3), calls=%async_computation.3 | async-start | bytes 8388608
  27.8 7.6 %collective-permute-start.8 = (bf16[32,5120]{1,0:T(8,128)(2,1)S(1)}, bf16[32,5120]{1,0:T(8,128)(2,1)S(1)}, u32[]{:S(2)}, u32[]{:S(2)}) collective-permute-start(bf16[32,5120]{1,0:T(8,128)(2,1)S(1)} %shard_map.139.own), channel_id=1, source_target_pairs={{0,1},{1,0},{2,3},{3,2},{4,5},{5,4},{6,7},{7,6},{8,9},{9,8},{10,11... | collective-permute-start | bytes 983048 | tf_op jit(solution)/shard_map/ppermute | solution.py:302
  27.9 7.1 %collective-permute-start.9 = (bf16[64,1280]{1,0:T(8,128)(2,1)S(1)}, bf16[64,1280]{1,0:T(8,128)(2,1)S(1)}, u32[]{:S(2)}, u32[]{:S(2)}) collective-permute-start(bf16[64,1280]{1,0:T(8,128)(2,1)S(1)} %get-tuple-element.64), channel_id=1, source_target_pairs={{0,2},{1,3},{2,0},{3,1},{4,6},{5,7},{6,4},{7,5},{8,10},{9,11},{10,... | collective-permute-start | bytes 491528 | tf_op jit(solution)/shard_map/ppermute | solution.py:302
  29.7 8.3 %collective-permute-start.6 = (bf16[64,1280]{1,0:T(8,128)(2,1)S(1)}, bf16[64,1280]{1,0:T(8,128)(2,1)S(1)}, u32[]{:S(2)}, u32[]{:S(2)}) collective-permute-start(bf16[64,1280]{1,0:T(8,128)(2,1)S(1)} %get-tuple-element.60), channel_id=1, source_target_pairs={{0,2},{1,3},{2,0},{3,1},{4,6},{5,7},{6,4},{7,5},{8,10},{9,11},{10,... | collective-permute-start | bytes 491528 | tf_op jit(solution)/shard_map/ppermute | solution.py:302
  35.3 3.1 %collective-permute-start.11 = (bf16[16,5120]{1,0:T(8,128)(2,1)S(1)}, bf16[16,5120]{1,0:T(8,128)(2,1)S(1)}, u32[]{:S(2)}, u32[]{:S(2)}) collective-permute-start(bf16[16,5120]{1,0:T(8,128)(2,1)S(1)} %get-tuple-element.65.own1), channel_id=1, source_target_pairs={{0,1},{1,0},{2,3},{3,2},{4,5},{5,4},{6,7},{7,6},{8,9},{9,8},{10,11... | collective-permute-start | bytes 491528 | tf_op jit(solution)/shard_map/ppermute | solution.py:302
  38.3 1.5 %collective-permute-start.10 = (bf16[16,5120]{1,0:T(8,128)(2,1)S(1)}, bf16[16,5120]{1,0:T(8,128)(2,1)S(1)}, u32[]{:S(2)}, u32[]{:S(2)}) collective-permute-start(bf16[16,5120]{1,0:T(8,128)(2,1)S(1)} %get-tuple-element.63.own0), channel_id=1, source_target_pairs={{0,1},{1,0},{2,3},{3,2},{4,5},{5,4},{6,7},{7,6},{8,9},{9,8},{10,11... | collective-permute-start | bytes 491528 | tf_op jit(solution)/shard_map/ppermute | solution.py:302

commit v6 on v5

--- a/solution.py
+++ b/solution.py
@@ -142,53 +142,67 @@
         copy.wait()
 
 
-def far_kernel(hdim, xa, xb, xc, xd, wown, wpair, pall, qcol, cosine, sine, *refs):
+def far_kernel(hdim, xa, xb, wown, wpair, pall, qcol, cosine, sine, *refs):
     scale = math.log2(math.e) / math.sqrt(hdim)
-    near, (part, send, kout, vout) = (refs[:4], refs[4:8]), refs[8:]
+    near, (part, send, kout, vout, raw, expos, attended) = (refs[:4], refs[4:8]), refs[8:]
     local = wown.shape[0] // 3
-    rows = 2 * xa.shape[0]
+    rows = xa.shape[0]
     me = lax.axis_index("sp")
-    normed = jnp.concatenate([x[...] for x in (xa, xb, xc, xd)], axis=0)
+    normed = jnp.concatenate([xa[...], xb[...]], axis=0)
     cos, sin = cosine[:, 2 * rows :], sine[:, 2 * rows :]
-    for side, weight in enumerate((wown, wpair)):
-        owner = me ^ side
-        base = slice(side * local, (side + 1) * local)
-        keyval = dot(weight[local:, :], normed, NT)
-        kout[base, :] = rotated(keyval[:local] + column(qcol, owner, local, 1), cos, sin, hdim)
-        vout[base, :] = (keyval[local:] + column(qcol, owner, local, 2)).astype(jnp.bfloat16)
-    pieces = []
+    pairs = local // (2 * hdim)
+    tops, shrinks, invs = {}, {}, {}
+
+    def place(side, p):
+        f = slice(2 * p * hdim, 2 * (p + 1) * hdim)
+        return f, slice(side * local + f.start, side * local + f.stop)
+
+    def project(side, c):
+        weight = (wown, wpair)[side][c * local : (c + 1) * local, :]
+        return dot(weight, normed, NT) + column(qcol, me ^ side, local, c)
+
     for side in range(2):
-        q, tops, sums, outs = near[side]
-        for p in range(local // (2 * hdim)):
-            f = slice(2 * p * hdim, 2 * (p + 1) * hdim)
-            g = slice(side * local + f.start, side * local + f.stop)
-            scores = dot(kout[g, :], q[f, :], TN)
-            old = tops[p : p + 1, :]
-            top = jnp.maximum(old, jnp.max(scores, axis=0, keepdims=True))
-            expo = jnp.exp2((scores - top) * scale)
-            shrink = jnp.exp2((old - top) * scale)
-            inv = 1.0 / (sums[p : p + 1, :] * shrink + jnp.sum(expo, axis=0, keepdims=True))
-            late = dot(vout[g, :], expo.astype(jnp.bfloat16), NN)
+        kout[side * local : (side + 1) * local, :] = rotated(project(side, 1), cos, sin, hdim)
+    for side in range(2):
+        for p in range(pairs):
+            f, g = place(side, p)
+            scores = dot(kout[g, :], near[side][0][f, :], TN)
+            raw[side * pairs + p] = scores
+            old = near[side][1][p : p + 1, :]
+            tops[side, p] = jnp.maximum(old, jnp.max(scores, axis=0, keepdims=True))
+    for side in range(2):
+        vout[side * local : (side + 1) * local, :] = project(side, 2).astype(jnp.bfloat16)
+        for p in range(pairs):
+            top = tops[side, p]
+            expo = jnp.exp2((raw[side * pairs + p] - top) * scale)
+            expos[side * pairs + p] = expo.astype(jnp.bfloat16)
+            shrink = jnp.exp2((near[side][1][p : p + 1, :] - top) * scale)
+            shrinks[side, p] = shrink
+            sums = near[side][2][p : p + 1, :]
+            invs[side, p] = 1.0 / (sums * shrink + jnp.sum(expo, axis=0, keepdims=True))
+    for side in range(2):
+        for p in range(pairs):
+            f, g = place(side, p)
+            late = dot(vout[g, :], expos[side * pairs + p], NN)
             for h in range(2):
                 lanes = slice(h * rows, (h + 1) * rows)
                 feats = slice(h * hdim, (h + 1) * hdim)
-                early = outs[f.start + h * hdim : f.start + (h + 1) * hdim, :]
-                mixed = (early * shrink[:, lanes] + late[feats, lanes]) * inv[:, lanes]
-                pieces.append(mixed.astype(jnp.bfloat16))
-    total = dot(jnp.concatenate(pieces, axis=0), pall[...], TN)
+                early = near[side][3][f.start + h * hdim : f.start + (h + 1) * hdim, :]
+                mixed = (early * shrinks[side, p][:, lanes] + late[feats, lanes]) * invs[side, p][:, lanes]
+                attended[g.start + h * hdim : g.start + (h + 1) * hdim, :] = mixed.astype(jnp.bfloat16)
+    total = dot(attended[...], pall[...], TN)
     part[...] = total
     send[...] = total.astype(jnp.bfloat16)
 
 
-def late_kernel(hdim, xa, xb, wown, wpair, pall, qcol, cosine, sine, kna, vna, knb, vnb, kf, vf, part, send0, send1):
+def late_kernel(hdim, x, wown, wpair, pall, qcol, cosine, sine, kna, vna, knb, vnb, kf, vf, part, send0, send1):
     scale = math.log2(math.e) / math.sqrt(hdim)
     local = wown.shape[0] // 3
-    rows = 2 * xa.shape[0]
+    rows = x.shape[0]
     me = lax.axis_index("sp")
-    normed = jnp.concatenate([xa[...], xb[...]], axis=0)
     pieces = []
     for side, weight in enumerate((wown, wpair)):
-        query = dot(weight[:local, :], normed, NT) + column(qcol, me ^ side, local, 0)
+        query = dot(weight[:local, :], x[...], NT) + column(qcol, me ^ side, local, 0)
         far = slice(2 * rows, 3 * rows)
         query = paired(rotated(query, cosine[:, far], sine[:, far], hdim), hdim)
         for at in range(0, local, 2 * hdim):
@@ -207,9 +221,9 @@
             pieces += [mixed[:hdim, :rows], mixed[hdim:, rows:]]
     total = dot(jnp.concatenate(pieces, axis=0), pall[...], TN)
     part[...] = total
-    half = rows // 2
-    send0[...] = total[:half].astype(jnp.bfloat16)
-    send1[...] = total[half:].astype(jnp.bfloat16)
+    cut = send0.shape[0]
+    send0[...] = total[:cut].astype(jnp.bfloat16)
+    send1[...] = total[cut:].astype(jnp.bfloat16)
 
 
 def merge_kernel(keep, start, x, part, got, rows, *rest):
@@ -246,13 +260,13 @@
 def last_kernel(own0, own1, pair0, pair1, weight, rows, vit0, vit1, early, out, vout, stage, sems):
     me = lax.axis_index("sp")
     chip, core = me // 2, me % 2
-    count = 2 * own0.shape[0]
-    half = vit0.shape[0]
+    count = own0.shape[0] + own1.shape[0]
+    cut, rest = vit0.shape[0], vit1.shape[0]
     at = lambda start: pl.ds(pl.multiple_of(start, count), count)
     there = out.at[pl.ds(pl.multiple_of((1 - chip) * 2 * count, count), 2 * count)]
     copies = [
-        pltpu.make_async_copy(vit0, vout.at[pl.ds(0, half)], sems.at[0]),
-        pltpu.make_async_copy(vit1, vout.at[pl.ds(half, half)], sems.at[1]),
+        pltpu.make_async_copy(vit0, vout.at[pl.ds(0, cut)], sems.at[0]),
+        pltpu.make_async_copy(vit1, vout.at[pl.ds(cut, rest)], sems.at[1]),
         pltpu.make_async_copy(early, there, sems.at[2]),
     ]
     for copy in copies:
@@ -362,22 +376,30 @@
     q, *kv_pair, tops, sums, outs, p_all = near(1, w_pair, p_pair, p_half)
     early_pair = (q, tops, sums, outs)
 
-    half = prow // 2
-    n_far0 = norm(x_far, 0, half, early_own[1], p_all)
-    n_farpair0 = swap(n_far0, 1)
-    n_far1 = norm(x_far, half, half, n_far0)
-    n_farpair1 = swap(n_far1, 1)
+    n_far = norm(x_far, 0, prow, early_own[1], p_all)
+    n_farpair = swap(n_far, 1)
     tall = shape((both, 2 * prow))
     shared = (w_own, w_pair, p_all, qcol, cos, sin)
     part_shape = shape((prow, width), jnp.float32)
-    part0, send0, k_far, v_far = call(
-        functools.partial(far_kernel, hdim), (part_shape, shape((prow, width)), tall, tall), 8 * MIB, 6 * mul
-    )(n_far0, n_far1, n_farpair0, n_farpair1, *shared, *early_own, *early_pair)
+    folds = both // (2 * hdim)
+    part0, send0, k_far, v_far = pl.pallas_call(
+        functools.partial(far_kernel, hdim),
+        out_shape=(part_shape, shape((prow, width)), tall, tall),
+        scratch_shapes=[
+            pltpu.VMEM((folds, 2 * prow, 2 * prow), jnp.float32),
+            pltpu.VMEM((folds, 2 * prow, 2 * prow), jnp.bfloat16),
+            pltpu.VMEM((both, prow), jnp.bfloat16),
+        ],
+        compiler_params=pltpu.CompilerParams(vmem_limit_bytes=8 * MIB),
+        cost_estimate=pl.CostEstimate(flops=6 * mul, bytes_accessed=1 << 22, transcendentals=0),
+        name="far",
+    )(n_far, n_farpair, *shared, *early_own, *early_pair)
     got1 = swap(send0, 2)
-    halves = (shape((half, width)), shape((half, width)))
+    cut = prow * 3 // 4
+    halves = (shape((cut, width)), shape((prow - cut, width)))
     part1, send1a, send1b = call(
         functools.partial(late_kernel, hdim), (part_shape,) + halves, 8 * MIB, 6 * mul
-    )(n_far0, n_far1, *shared, *kv_own, *kv_pair, k_far, v_far)
+    )(n_far, *shared, *kv_own, *kv_pair, k_far, v_far)
     got0a = swap(send1a, 2)
     got0b = swap(send1b, 2)
     late_rows = call(copy_kernel, shape(rows.shape, rows.dtype), MIB, 1000)(rows)
@@ -402,7 +424,7 @@
     vit_a, blocks_a = merge(1, 0, x_own, part0, got0a, late_rows, early)
     pair_a = swap(blocks_a, 1)
     late_rows = call(copy_kernel, shape(rows.shape, rows.dtype), MIB, 1000)(late_rows)
-    vit_b, blocks_b = merge(1, half, x_own, part0, got0b, late_rows)
+    vit_b, blocks_b = merge(1, cut, x_own, part0, got0b, late_rows)
     pair_b = swap(blocks_b, 1)
     parts = hidden // 256
     merged, vit_out = pl.pallas_call(

time: 42.8 us -> 45.6 us (1.065)
  waiting for transfers between devices: 15.7 us -> 17.9 us
  starting transfers between devices: 8.3 us -> 9.33 us
  Pallas kernels: 17.6 us -> 17.1 us
    ppermute x12 -> x11, waiting for transfers between devices: 15.7 us -> 17.9 us  [swap(): return lax.ppermute(value, 'sp', [(i, i ^ bit) for i in range(4)])]
    ppermute x12 -> x11, starting transfers between devices: 8.3 us -> 9.33 us  [swap(): return lax.ppermute(value, 'sp', [(i, i ^ bit) for i in range(4)])]
  transfers between devices with their start and end apart: 12 -> 11, of which waited for: 8 -> 7; matrix products, arithmetic and copies ran while one was open for 0% -> 0% of each run, Pallas kernels for 27% -> 25%
where the time goes in v6:
time: 45.6 us; the launch traced here: 45.4 us
  waiting for transfers between devices  17.9 us (39%)
  Pallas kernels  17.1 us (38%)
  starting transfers between devices  9.33 us (20%)
  between operations  0.97 us (2%)
    ppermute x11, waiting for transfers between devices, swap(): return lax.ppermute(value, 'sp', [(i, i ^ bit) for i in range(4)])  17.9 us
    ppermute x11, starting transfers between devices, swap(): return lax.ppermute(value, 'sp', [(i, i ^ bit) for i in range(4)])  9.33 us
    pallas_call x2, Pallas kernels, near(): pl.pallas_call(functools.partial(near_kernel, hdim, side), out_shape=near...  3.35 us
    pallas_call x1, Pallas kernels, two_chips(): call(functools.partial(late_kernel, hdim), (part_shape,) + halves, 8 * MI...  3.07 us
    pallas_call x1, Pallas kernels, two_chips(): pl.pallas_call(last_kernel, out_shape=(shape((prow, hidden)), shape((prow...  2.7 us
    pallas_call x1, Pallas kernels, two_chips(): pl.pallas_call(functools.partial(setup_kernel, hdim, len(sources)), out_s...  2.27 us
    pallas_call x1, Pallas kernels, two_chips(): pl.pallas_call(functools.partial(far_kernel, hdim), out_shape=(part_shape...  2.16 us
    pallas_call x1, Pallas kernels, two_chips(): call(hidden_kernel, shape((prow // 2, hidden)), 4 * MIB, flops)  1.94 us
  transfers between devices with their start and end apart: 11, of which 7 were waited for; matrix products, arithmetic and copies ran while one was open for 0% of the time, Pallas kernels for 25%

profile of v6, /device:TPU:0, one launch (start us, length us, event | category | flops | bytes accessed | tf_op | source)
XLA Modules:
  0.0 45.4 jit_solution(9197884390169207761)
XLA Ops:
  0.6 0.6 %collective-permute-start.2 = (bf16[960,1280]{1,0:T(8,128)(2,1)}, bf16[960,1280]{1,0:T(8,128)(2,1)S(1)}, u32[]{:S(2)}, u32[]{:S(2)}) collective-permute-start(bf16[960,1280]{1,0:T(8,128)(2,1)} %bitcast.5), channel_id=1, source_target_pairs={{0,1},{1,0},{2,3},{3,2},{4,5},{5,4},{6,7},{7,6},{8,9},{9,8},{10,11... | collective-permute-start | bytes 7372808 | tf_op jit(solution)/shard_map/ppermute | solution.py:316
  1.2 0.1 collective-permute-start.3
  1.3 0.4 collective-permute-start.1
  1.7 2.6 %collective-permute-start = (bf16[128,1280]{1,0:T(8,128)(2,1)}, bf16[128,1280]{1,0:T(8,128)(2,1)S(1)}, u32[]{:S(2)}, u32[]{:S(2)}) collective-permute-start(bf16[128,1280]{1,0:T(8,128)(2,1)} %refs_0_.1), channel_id=1, source_target_pairs={{0,2},{1,3},{2,0},{3,1},{4,6},{5,7},{6,4},{7,5},{8,10},{9,11},{10,... | collective-permute-start | bytes 983048 | tf_op jit(solution)/shard_map/ppermute | solution.py:316
  4.3 2.3 %setup.1 = (bf16[128,1280]{1,0:T(8,128)(2,1)S(1)}, bf16[960,1280]{1,0:T(8,128)(2,1)S(1)}, bf16[640,1280]{1,0:T(8,128)(2,1)S(1)}, bf16[128,1280]{1,0:T(8,128)(2,1...) custom-call(bf16[128,1280]{1,0:T(8,128)(2,1)} %refs_0_.1, ...), custom_call_target="tpu_custom_call" | custom-call | flops 209715200 | bytes 4194304 | tf_op jit(solution)/shard_map/setup/pallas_call | solution.py:331
  6.5 0.8 %collective-permute-done.1.x = bf16[128,1280]{1,0:T(8,128)(2,1)S(1)} collective-permute-done((bf16[128,1280]{1,0:T(8,128)(2,1)}, bf16[128,1280]{1,0:T(8,128)(2,1)S(1)}, u32[]{:S(2)}, u32[]{:S(2)}) %collective-permute-start.1) | collective-permute-done | bytes 327712 | tf_op jit(solution)/shard_map/ppermute | solution.py:316
  7.3 0.3 shard_map.131.xb
  7.6 0.0 slice-start
  7.7 1.5 %shard_map.132 = (bf16[320,256]{1,0:T(8,128)(2,1)S(1)}, bf16[320,256]{1,0:T(8,128)(2,1)S(1)}, bf16[320,256]{1,0:T(8,128)(2,1)S(1)}, f32[2,256]{1,0:T(2,128)S(1)}...) custom-call(bf16[128,1280]{1,0:T(8,128)(2,1)S(1)} %get-tuple-element.38.xa, bf16[128,1280]{1,0:T(8,128)(2,1)S(1)} %shard_map.131.xb, ...), custom_call_target="tpu_custom_call" | custom-call | flops 838860800 | bytes 4194304 | tf_op jit(solution)/shard_map/pallas_call | solution.py:365
  9.2 0.0 collective-permute-done.3.rest_0_
  9.2 0.0 collective-permute-done.2.weight.wpair
  9.2 0.0 slice-start.1
  9.2 1.8 %shard_map.133 = (bf16[320,256]{1,0:T(8,128)(2,1)S(1)}, bf16[320,256]{1,0:T(8,128)(2,1)S(1)}, bf16[320,256]{1,0:T(8,128)(2,1)S(1)}, f32[2,256]{1,0:T(2,128)S(1)}...) custom-call(bf16[128,1280]{1,0:T(8,128)(2,1)S(1)} %get-tuple-element, ...), custom_call_target="tpu_custom_call", output_to_operand_aliasing={{6}: (7, {})} | custom-call | flops 838860800 | bytes 4194304 | tf_op jit(solution)/shard_map/pallas_call | solution.py:365
  11.1 1.7 %collective-permute-done.x = bf16[128,1280]{1,0:T(8,128)(2,1)S(1)} collective-permute-done((bf16[128,1280]{1,0:T(8,128)(2,1)}, bf16[128,1280]{1,0:T(8,128)(2,1)S(1)}, u32[]{:S(2)}, u32[]{:S(2)}) %collective-permute-start) | collective-permute-done | bytes 327712 | tf_op jit(solution)/shard_map/ppermute | solution.py:316
  12.8 0.3 shard_map.134.xa.x
  13.1 0.1 collective-permute-start.4
  13.2 1.6 %collective-permute-done.4.xb = bf16[128,1280]{1,0:T(8,128)(2,1)S(1)} collective-permute-done((bf16[128,1280]{1,0:T(8,128)(2,1)S(1)}, bf16[128,1280]{1,0:T(8,128)(2,1)S(1)}, u32[]{:S(2)}, u32[]{:S(2)}) %collective-permute-start.4) | collective-permute-done | bytes 327712 | tf_op jit(solution)/shard_map/ppermute | solution.py:316
  14.8 0.0 slice-start.2
  14.8 2.2 %far.1 = (f32[128,1280]{1,0:T(8,128)S(1)}, bf16[128,1280]{1,0:T(8,128)(2,1)S(1)}, bf16[640,256]{1,0:T(8,128)(2,1)S(1)}, bf16[640,256]{1,0:T(8,128)(2,1)S(1)}) custom-call(bf16[128,1280]{1,0:T(8,128)(2,1)S(1)} %shard_map.134.xa.x, bf16[128,1280]{1,0:T(8,128)(2,1)S(1)} %collective-permute-done.4.xb, bf16[960,1280]{1,0:T(8,128)(2,1)S(1)} %get-tuple-element.39.weight.wown, ...), custom_call_target="tpu_custom_call" | custom-call | flops 1258291200 | bytes 4194304 | tf_op jit(solution)/shard_map/far/pallas_call | solution.py:385
  16.9 1.8 %collective-permute-start.6 = (bf16[128,1280]{1,0:T(8,128)(2,1)S(1)}, bf16[128,1280]{1,0:T(8,128)(2,1)S(1)}, u32[]{:S(2)}, u32[]{:S(2)}) collective-permute-start(bf16[128,1280]{1,0:T(8,128)(2,1)S(1)} %get-tuple-element.62), channel_id=1, source_target_pairs={{0,2},{1,3},{2,0},{3,1},{4,6},{5,7},{6,4},{7,5},{8,10},{9,11},{10,... | collective-permute-start | bytes 983048 | tf_op jit(solution)/shard_map/ppermute | solution.py:316
  18.8 0.0 slice-start.3
  18.8 3.1 %shard_map.135 = (f32[128,1280]{1,0:T(8,128)S(1)}, bf16[96,1280]{1,0:T(8,128)(2,1)S(1)}, bf16[32,1280]{1,0:T(8,128)(2,1)S(1)}) custom-call(bf16[128,1280]{1,0:T(8,128)(2,1)S(1)} %shard_map.134.xa.x, bf16[960,1280]{1,0:T(8,128)(2,1)S(1)} %get-tuple-element.39.weight.wown, bf16[960,1280]{1,0:T(8,128)(2,1)S(1)} %collective-permute-done.2.weight.wpair, ...), custom_call_target="tpu_custom_call" | custom-call | flops 1258291200 | bytes 1048576 | tf_op jit(solution)/shard_map/pallas_call | solution.py:400
  21.8 4.9 %collective-permute-done.6.got = bf16[128,1280]{1,0:T(8,128)(2,1)S(1)} collective-permute-done((bf16[128,1280]{1,0:T(8,128)(2,1)S(1)}, bf16[128,1280]{1,0:T(8,128)(2,1)S(1)}, u32[]{:S(2)}, u32[]{:S(2)}) %collective-permute-start.6) | collective-permute-done | bytes 327712 | tf_op jit(solution)/shard_map/ppermute | solution.py:316
  26.8 0.4 shard_map.137.own
  27.2 0.1 collective-permute-start.7
  27.3 1.8 %collective-permute-start.5 = (bf16[96,1280]{1,0:T(8,128)(2,1)S(1)}, bf16[96,1280]{1,0:T(8,128)(2,1)S(1)}, u32[]{:S(2)}, u32[]{:S(2)}) collective-permute-start(bf16[96,1280]{1,0:T(8,128)(2,1)S(1)} %get-tuple-element.60), channel_id=1, source_target_pairs={{0,2},{1,3},{2,0},{3,1},{4,6},{5,7},{6,4},{7,5},{8,10},{9,11},{10,... | collective-permute-start | bytes 737288 | tf_op jit(solution)/shard_map/ppermute | solution.py:316
  29.1 0.0 collective-permute-done.7.pair
  29.1 0.0 slice-done
  29.1 0.0 slice-done.1
  29.1 0.0 slice-done.2
  29.1 0.0 slice-done.3
  29.1 1.9 %shard_map.138.rest_0_.early = bf16[64,1280]{1,0:T(8,128)(2,1)S(1)} custom-call(bf16[32,5120]{1,0:T(8,128)(2,1)S(1)} %shard_map.137.own, bf16[32,5120]{1,0:T(8,128)(2,1)S(1)} %collective-permute-done.7.pair, bf16[5120,1280]{1,0:T(8,128)(2,1)S(1)} %bitcast.4, f32[8,1280]{1,0:T(8,128)S(1)} %get-tuple-element.37.rows.x), custom_call_target="tpu_custom_call" | custom-call | flops 838860800 | bytes 1048576 | tf_op jit(solution)/shard_map/pallas_call | solution.py:423
  31.1 4.6 %collective-permute-done.5.got = bf16[96,1280]{1,0:T(8,128)(2,1)S(1)} collective-permute-done((bf16[96,1280]{1,0:T(8,128)(2,1)S(1)}, bf16[96,1280]{1,0:T(8,128)(2,1)S(1)}, u32[]{:S(2)}, u32[]{:S(2)}) %collective-permute-start.5) | collective-permute-done | bytes 245792 | tf_op jit(solution)/shard_map/ppermute | solution.py:316
  35.7 0.4 shard_map.139
  36.0 0.1 collective-permute-start.9
  36.1 1.8 %collective-permute-start.8 = (bf16[32,1280]{1,0:T(8,128)(2,1)S(1)}, bf16[32,1280]{1,0:T(8,128)(2,1)S(1)}, u32[]{:S(2)}, u32[]{:S(2)}) collective-permute-start(bf16[32,1280]{1,0:T(8,128)(2,1)S(1)} %get-tuple-element.64), channel_id=1, source_target_pairs={{0,2},{1,3},{2,0},{3,1},{4,6},{5,7},{6,4},{7,5},{8,10},{9,11},{10,... | collective-permute-start | bytes 245768 | tf_op jit(solution)/shard_map/ppermute | solution.py:316
  37.9 3.0 %collective-permute-done.8.got = bf16[32,1280]{1,0:T(8,128)(2,1)S(1)} collective-permute-done((bf16[32,1280]{1,0:T(8,128)(2,1)S(1)}, bf16[32,1280]{1,0:T(8,128)(2,1)S(1)}, u32[]{:S(2)}, u32[]{:S(2)}) %collective-permute-start.8) | collective-permute-done | bytes 81952 | tf_op jit(solution)/shard_map/ppermute | solution.py:316
  40.9 0.3 shard_map.141
  41.2 0.1 collective-permute-start.10
  41.3 1.3 %collective-permute-done.10.pair1 = bf16[8,5120]{1,0:T(8,128)(2,1)S(1)} collective-permute-done((bf16[8,5120]{1,0:T(8,128)(2,1)S(1)}, bf16[8,5120]{1,0:T(8,128)(2,1)S(1)}, u32[]{:S(2)}, u32[]{:S(2)}) %collective-permute-start.10) | collective-permute-done | bytes 81952 | tf_op jit(solution)/shard_map/ppermute | solution.py:316
  42.5 0.0 collective-permute-done.9.pair0
  42.6 2.7 %hidden0.1 = (bf16[128,1280]{1,0:T(8,128)(2,1)}, bf16[128,1280]{1,0:T(8,128)(2,1)}) custom-call(bf16[24,5120]{1,0:T(8,128)(2,1)S(1)} %get-tuple-element.63.own0, bf16[8,5120]{1,0:T(8,128)(2,1)S(1)} %get-tuple-element.65.own1, bf16[24,5120]{1,0:T(8,128)(2,1)S(1)} %collective-permute-done.9.pair0, bf16[8,5120]{1,0:T(8,128)(2,1)S(1)} %collective-permute-done.10.pair1, ...), custom_call_target="tpu_custom_call" | custom-call | flops 838860800 | bytes 16777216 | tf_op jit(solution)/shard_map/hidden0/pallas_call | solution.py:430
  (3 shorter events, 0.0 us)
Async XLA Ops:
  0.6 8.6 %collective-permute-start.2 = (bf16[960,1280]{1,0:T(8,128)(2,1)}, bf16[960,1280]{1,0:T(8,128)(2,1)S(1)}, u32[]{:S(2)}, u32[]{:S(2)}) collective-permute-start(bf16[960,1280]{1,0:T(8,128)(2,1)} %bitcast.5), channel_id=1, source_target_pairs={{0,1},{1,0},{2,3},{3,2},{4,5},{5,4},{6,7},{7,6},{8,9},{9,8},{10,11... | collective-permute-start | bytes 7372808 | tf_op jit(solution)/shard_map/ppermute | solution.py:316
  1.2 8.0 %collective-permute-start.3 = (bf16[320,1280]{1,0:T(8,128)(2,1)}, bf16[320,1280]{1,0:T(8,128)(2,1)S(1)}, u32[]{:S(2)}, u32[]{:S(2)}) collective-permute-start(bf16[320,1280]{1,0:T(8,128)(2,1)} %refs_9_.1), channel_id=1, source_target_pairs={{0,1},{1,0},{2,3},{3,2},{4,5},{5,4},{6,7},{7,6},{8,9},{9,8},{10,11... | collective-permute-start | bytes 2457608 | tf_op jit(solution)/shard_map/ppermute | solution.py:316
  1.3 6.1 %collective-permute-start.1 = (bf16[128,1280]{1,0:T(8,128)(2,1)}, bf16[128,1280]{1,0:T(8,128)(2,1)S(1)}, u32[]{:S(2)}, u32[]{:S(2)}) collective-permute-start(bf16[128,1280]{1,0:T(8,128)(2,1)} %refs_0_.1), channel_id=1, source_target_pairs={{0,1},{1,0},{2,3},{3,2},{4,5},{5,4},{6,7},{7,6},{8,9},{9,8},{10,11... | collective-permute-start | bytes 983048 | tf_op jit(solution)/shard_map/ppermute | solution.py:316
  1.7 11.1 %collective-permute-start = (bf16[128,1280]{1,0:T(8,128)(2,1)}, bf16[128,1280]{1,0:T(8,128)(2,1)S(1)}, u32[]{:S(2)}, u32[]{:S(2)}) collective-permute-start(bf16[128,1280]{1,0:T(8,128)(2,1)} %refs_0_.1), channel_id=1, source_target_pairs={{0,2},{1,3},{2,0},{3,1},{4,6},{5,7},{6,4},{7,5},{8,10},{9,11},{10,... | collective-permute-start | bytes 983048 | tf_op jit(solution)/shard_map/ppermute | solution.py:316
  7.6 21.5 %slice-start = ((s8[13107200]{0:T(1024)(128)(4,1)}), s8[524288]{0:T(1024)(128)(4,1)S(1)}, s32[]{:S(2)}) async-start(s8[13107200]{0:T(1024)(128)(4,1)} %bitcast.3), calls=%async_computation | async-start | bytes 1048576
  9.2 19.9 %slice-start.1 = ((s8[13107200]{0:T(1024)(128)(4,1)}), s8[4194304]{0:T(1024)(128)(4,1)S(1)}, s32[]{:S(2)}) async-start(s8[13107200]{0:T(1024)(128)(4,1)} %bitcast.3), calls=%async_computation.1 | async-start | bytes 8388608
  13.1 1.7 %collective-permute-start.4 = (bf16[128,1280]{1,0:T(8,128)(2,1)S(1)}, bf16[128,1280]{1,0:T(8,128)(2,1)S(1)}, u32[]{:S(2)}, u32[]{:S(2)}) collective-permute-start(bf16[128,1280]{1,0:T(8,128)(2,1)S(1)} %shard_map.134.xa.x), channel_id=1, source_target_pairs={{0,1},{1,0},{2,3},{3,2},{4,5},{5,4},{6,7},{7,6},{8,9},{9,8},{10,11... | collective-permute-start | bytes 983048 | tf_op jit(solution)/shard_map/ppermute | solution.py:316
  14.8 14.3 %slice-start.2 = ((s8[13107200]{0:T(1024)(128)(4,1)}), s8[4194304]{0:T(1024)(128)(4,1)S(1)}, s32[]{:S(2)}) async-start(s8[13107200]{0:T(1024)(128)(4,1)} %bitcast.3), calls=%async_computation.2 | async-start | bytes 8388608
  16.9 9.8 %collective-permute-start.6 = (bf16[128,1280]{1,0:T(8,128)(2,1)S(1)}, bf16[128,1280]{1,0:T(8,128)(2,1)S(1)}, u32[]{:S(2)}, u32[]{:S(2)}) collective-permute-start(bf16[128,1280]{1,0:T(8,128)(2,1)S(1)} %get-tuple-element.62), channel_id=1, source_target_pairs={{0,2},{1,3},{2,0},{3,1},{4,6},{5,7},{6,4},{7,5},{8,10},{9,11},{10,... | collective-permute-start | bytes 983048 | tf_op jit(solution)/shard_map/ppermute | solution.py:316
  18.8 10.4 %slice-start.3 = ((s8[13107200]{0:T(1024)(128)(4,1)}), s8[4194304]{0:T(1024)(128)(4,1)S(1)}, s32[]{:S(2)}) async-start(s8[13107200]{0:T(1024)(128)(4,1)} %bitcast.3), calls=%async_computation.3 | async-start | bytes 8388608
  27.2 1.9 %collective-permute-start.7 = (bf16[32,5120]{1,0:T(8,128)(2,1)S(1)}, bf16[32,5120]{1,0:T(8,128)(2,1)S(1)}, u32[]{:S(2)}, u32[]{:S(2)}) collective-permute-start(bf16[32,5120]{1,0:T(8,128)(2,1)S(1)} %shard_map.137.own), channel_id=1, source_target_pairs={{0,1},{1,0},{2,3},{3,2},{4,5},{5,4},{6,7},{7,6},{8,9},{9,8},{10,11... | collective-permute-start | bytes 983048 | tf_op jit(solution)/shard_map/ppermute | solution.py:316
  27.3 8.4 %collective-permute-start.5 = (bf16[96,1280]{1,0:T(8,128)(2,1)S(1)}, bf16[96,1280]{1,0:T(8,128)(2,1)S(1)}, u32[]{:S(2)}, u32[]{:S(2)}) collective-permute-start(bf16[96,1280]{1,0:T(8,128)(2,1)S(1)} %get-tuple-element.60), channel_id=1, source_target_pairs={{0,2},{1,3},{2,0},{3,1},{4,6},{5,7},{6,4},{7,5},{8,10},{9,11},{10,... | collective-permute-start | bytes 737288 | tf_op jit(solution)/shard_map/ppermute | solution.py:316
  36.0 6.5 %collective-permute-start.9 = (bf16[24,5120]{1,0:T(8,128)(2,1)S(1)}, bf16[24,5120]{1,0:T(8,128)(2,1)S(1)}, u32[]{:S(2)}, u32[]{:S(2)}) collective-permute-start(bf16[24,5120]{1,0:T(8,128)(2,1)S(1)} %get-tuple-element.63.own0), channel_id=1, source_target_pairs={{0,1},{1,0},{2,3},{3,2},{4,5},{5,4},{6,7},{7,6},{8,9},{9,8},{10,11... | collective-permute-start | bytes 737288 | tf_op jit(solution)/shard_map/ppermute | solution.py:316
  36.1 4.8 %collective-permute-start.8 = (bf16[32,1280]{1,0:T(8,128)(2,1)S(1)}, bf16[32,1280]{1,0:T(8,128)(2,1)S(1)}, u32[]{:S(2)}, u32[]{:S(2)}) collective-permute-start(bf16[32,1280]{1,0:T(8,128)(2,1)S(1)} %get-tuple-element.64), channel_id=1, source_target_pairs={{0,2},{1,3},{2,0},{3,1},{4,6},{5,7},{6,4},{7,5},{8,10},{9,11},{10,... | collective-permute-start | bytes 245768 | tf_op jit(solution)/shard_map/ppermute | solution.py:316
  41.2 1.3 %collective-permute-start.10 = (bf16[8,5120]{1,0:T(8,128)(2,1)S(1)}, bf16[8,5120]{1,0:T(8,128)(2,1)S(1)}, u32[]{:S(2)}, u32[]{:S(2)}) collective-permute-start(bf16[8,5120]{1,0:T(8,128)(2,1)S(1)} %get-tuple-element.65.own1), channel_id=1, source_target_pairs={{0,1},{1,0},{2,3},{3,2},{4,5},{5,4},{6,7},{7,6},{8,9},{9,8},{10,11... | collective-permute-start | bytes 245768 | tf_op jit(solution)/shard_map/ppermute | solution.py:316

commit v7 on v6

--- a/solution.py
+++ b/solution.py
@@ -107,13 +107,7 @@
 
 
 def near_kernel(hdim, side, xa, xb, weight, qcol, cosine, sine, *rest):
-    if side:
-        ppair, _, qout, kout, vout, tops, sums, outs, pall, sem = rest
-        count = ppair.shape[0]
-        copy = pltpu.make_async_copy(ppair, pall.at[pl.ds(count, count)], sem)
-        copy.start()
-    else:
-        qout, kout, vout, tops, sums, outs = rest
+    qout, kout, vout, tops, sums, outs = rest
     scale = math.log2(math.e) / math.sqrt(hdim)
     local = weight.shape[0] // 3
     rows = xa.shape[0]
@@ -138,8 +132,14 @@
         total = dot(value[f], expo.astype(jnp.bfloat16), NN)
         outs[f.start : f.start + hdim, :] = total[:hdim, :rows]
         outs[f.start + hdim : f.stop, :] = total[hdim:, rows:]
-    if side:
-        copy.wait()
+
+
+def gather_kernel(ppair, half, after, pall, sem):
+    del half, after
+    count = ppair.shape[0]
+    copy = pltpu.make_async_copy(ppair, pall.at[pl.ds(count, count)], sem)
+    copy.start()
+    copy.wait()
 
 
 def far_kernel(hdim, xa, xb, wown, wpair, pall, qcol, cosine, sine, *refs):
@@ -164,6 +164,8 @@
     for side in range(2):
         kout[side * local : (side + 1) * local, :] = rotated(project(side, 1), cos, sin, hdim)
     for side in range(2):
+        vout[side * local : (side + 1) * local, :] = project(side, 2).astype(jnp.bfloat16)
+    for side in range(2):
         for p in range(pairs):
             f, g = place(side, p)
             scores = dot(kout[g, :], near[side][0][f, :], TN)
@@ -171,7 +173,6 @@
             old = near[side][1][p : p + 1, :]
             tops[side, p] = jnp.maximum(old, jnp.max(scores, axis=0, keepdims=True))
     for side in range(2):
-        vout[side * local : (side + 1) * local, :] = project(side, 2).astype(jnp.bfloat16)
         for p in range(pairs):
             top = tops[side, p]
             expo = jnp.exp2((raw[side * pairs + p] - top) * scale)
@@ -361,23 +362,28 @@
     state = shape((local // (2 * hdim), 2 * prow), jnp.float32)
     near_shape = (flat, flat, flat, state, state, shape((local, prow), jnp.float32))
 
-    def near(side, weight, *more):
-        return pl.pallas_call(
-            functools.partial(near_kernel, hdim, side),
-            out_shape=near_shape + (pltpu.VMEM((both, width), proj_weight.dtype),) * side,
-            input_output_aliases={7: 6} if side else {},
-            scratch_shapes=[pltpu.SemaphoreType.DMA] * side,
-            compiler_params=pltpu.CompilerParams(vmem_limit_bytes=8 * MIB),
-            cost_estimate=pl.CostEstimate(flops=4 * mul, bytes_accessed=1 << 22, transcendentals=0),
-        )(n_own, n_pair, weight, qcol, cos, sin, *more)
+    def near(side, weight):
+        return call(
+            functools.partial(near_kernel, hdim, side), near_shape, 8 * MIB, 4 * mul
+        )(n_own, n_pair, weight, qcol, cos, sin)
 
     q, *kv_own, tops, sums, outs = near(0, w_own)
     early_own = (q, tops, sums, outs)
-    q, *kv_pair, tops, sums, outs, p_all = near(1, w_pair, p_pair, p_half)
+    q, *kv_pair, tops, sums, outs = near(1, w_pair)
     early_pair = (q, tops, sums, outs)
 
-    n_far = norm(x_far, 0, prow, early_own[1], p_all)
+    n_far = norm(x_far, 0, prow, early_own[1], early_pair[1])
     n_farpair = swap(n_far, 1)
+    p_all = pl.pallas_call(
+        gather_kernel,
+        out_shape=pltpu.VMEM((both, width), proj_weight.dtype),
+        in_specs=[VMEM, VMEM, ANY],
+        input_output_aliases={1: 0},
+        scratch_shapes=[pltpu.SemaphoreType.DMA],
+        compiler_params=pltpu.CompilerParams(vmem_limit_bytes=2 * MIB),
+        cost_estimate=pl.CostEstimate(flops=mul // 4, bytes_accessed=1 << 20, transcendentals=0),
+        name="gather_proj",
+    )(p_pair, p_half, n_far)
     tall = shape((both, 2 * prow))
     shared = (w_own, w_pair, p_all, qcol, cos, sin)
     part_shape = shape((prow, width), jnp.float32)

time: 45.6 us -> 45.5 us (level)
    pallas_call x2 -> x3, Pallas kernels: 3.35 us -> 3.34 us  [the longest x2 3.05 us: near(): call(functools.partial(near_kernel, hdim, side), near_shape, 8 * MIB, 4 *...]
where the time goes in v7:
time: 45.5 us; the launch traced here: 45.3 us
  waiting for transfers between devices  18 us (40%)
  Pallas kernels  17 us (37%)
  starting transfers between devices  9.3 us (20%)
  between operations  0.98 us (2%)
    ppermute x11, waiting for transfers between devices, swap(): return lax.ppermute(value, 'sp', [(i, i ^ bit) for i in range(4)])  18 us
    ppermute x11, starting transfers between devices, swap(): return lax.ppermute(value, 'sp', [(i, i ^ bit) for i in range(4)])  9.3 us
    pallas_call x1, Pallas kernels, two_chips(): call(functools.partial(late_kernel, hdim), (part_shape,) + halves, 8 * MI...  3.07 us
    pallas_call x2, Pallas kernels, near(): call(functools.partial(near_kernel, hdim, side), near_shape, 8 * MIB, 4 *...  3.05 us
    pallas_call x1, Pallas kernels, two_chips(): pl.pallas_call(last_kernel, out_shape=(shape((prow, hidden)), shape((prow...  2.7 us
    pallas_call x1, Pallas kernels, two_chips(): pl.pallas_call(functools.partial(setup_kernel, hdim, len(sources)), out_s...  2.27 us
    pallas_call x1, Pallas kernels, two_chips(): pl.pallas_call(functools.partial(far_kernel, hdim), out_shape=(part_shape...  2.04 us
    pallas_call x1, Pallas kernels, two_chips(): call(hidden_kernel, shape((prow // 2, hidden)), 4 * MIB, flops)  1.95 us
  transfers between devices with their start and end apart: 11, of which 7 were waited for; matrix products, arithmetic and copies ran while one was open for 0% of the time, Pallas kernels for 25%

profile of v7, /device:TPU:0, one launch (start us, length us, event | category | flops | bytes accessed | tf_op | source)
XLA Modules:
  0.0 45.3 jit_solution(9245666838343625784)
XLA Ops:
  0.6 0.6 %collective-permute-start.2 = (bf16[960,1280]{1,0:T(8,128)(2,1)}, bf16[960,1280]{1,0:T(8,128)(2,1)S(1)}, u32[]{:S(2)}, u32[]{:S(2)}) collective-permute-start(bf16[960,1280]{1,0:T(8,128)(2,1)} %bitcast.5), channel_id=1, source_target_pairs={{0,1},{1,0},{2,3},{3,2},{4,5},{5,4},{6,7},{7,6},{8,9},{9,8},{10,11... | collective-permute-start | bytes 7372808 | tf_op jit(solution)/shard_map/ppermute | solution.py:317
  1.2 0.1 collective-permute-start.4
  1.3 0.4 collective-permute-start.1
  1.7 2.6 %collective-permute-start = (bf16[128,1280]{1,0:T(8,128)(2,1)}, bf16[128,1280]{1,0:T(8,128)(2,1)S(1)}, u32[]{:S(2)}, u32[]{:S(2)}) collective-permute-start(bf16[128,1280]{1,0:T(8,128)(2,1)} %refs_0_.1), channel_id=1, source_target_pairs={{0,2},{1,3},{2,0},{3,1},{4,6},{5,7},{6,4},{7,5},{8,10},{9,11},{10,... | collective-permute-start | bytes 983048 | tf_op jit(solution)/shard_map/ppermute | solution.py:317
  4.3 2.3 %setup.1 = (bf16[128,1280]{1,0:T(8,128)(2,1)S(1)}, bf16[960,1280]{1,0:T(8,128)(2,1)S(1)}, bf16[640,1280]{1,0:T(8,128)(2,1)S(1)}, bf16[128,1280]{1,0:T(8,128)(2,1...) custom-call(bf16[128,1280]{1,0:T(8,128)(2,1)} %refs_0_.1, ...), custom_call_target="tpu_custom_call" | custom-call | flops 209715200 | bytes 4194304 | tf_op jit(solution)/shard_map/setup/pallas_call | solution.py:332
  6.5 0.8 %collective-permute-done.1.x = bf16[128,1280]{1,0:T(8,128)(2,1)S(1)} collective-permute-done((bf16[128,1280]{1,0:T(8,128)(2,1)}, bf16[128,1280]{1,0:T(8,128)(2,1)S(1)}, u32[]{:S(2)}, u32[]{:S(2)}) %collective-permute-start.1) | collective-permute-done | bytes 327712 | tf_op jit(solution)/shard_map/ppermute | solution.py:317
  7.3 0.3 shard_map.131.xb
  7.6 1.5 %shard_map.132 = (bf16[320,256]{1,0:T(8,128)(2,1)S(1)}, bf16[320,256]{1,0:T(8,128)(2,1)S(1)}, bf16[320,256]{1,0:T(8,128)(2,1)S(1)}, f32[2,256]{1,0:T(2,128)S(1)}...) custom-call(bf16[128,1280]{1,0:T(8,128)(2,1)S(1)} %get-tuple-element.37.xa, bf16[128,1280]{1,0:T(8,128)(2,1)S(1)} %shard_map.131.xb, ...), custom_call_target="tpu_custom_call" | custom-call | flops 838860800 | bytes 1048576 | tf_op jit(solution)/shard_map/pallas_call | solution.py:366
  9.2 0.0 collective-permute-done.2.weight.wpair
  9.2 0.0 slice-start
  9.2 1.5 %shard_map.133 = (bf16[320,256]{1,0:T(8,128)(2,1)S(1)}, bf16[320,256]{1,0:T(8,128)(2,1)S(1)}, bf16[320,256]{1,0:T(8,128)(2,1)S(1)}, f32[2,256]{1,0:T(2,128)S(1)}...) custom-call(bf16[128,1280]{1,0:T(8,128)(2,1)S(1)} %get-tuple-element.37.xa, bf16[128,1280]{1,0:T(8,128)(2,1)S(1)} %shard_map.131.xb, ...), custom_call_target="tpu_custom_call" | custom-call | flops 838860800 | bytes 1048576 | tf_op jit(solution)/shard_map/pallas_call | solution.py:366
  10.7 2.0 %collective-permute-done.x = bf16[128,1280]{1,0:T(8,128)(2,1)S(1)} collective-permute-done((bf16[128,1280]{1,0:T(8,128)(2,1)}, bf16[128,1280]{1,0:T(8,128)(2,1)S(1)}, u32[]{:S(2)}, u32[]{:S(2)}) %collective-permute-start) | collective-permute-done | bytes 327712 | tf_op jit(solution)/shard_map/ppermute | solution.py:317
  12.8 0.3 shard_map.134.after.xa.x
  13.1 0.1 collective-permute-start.3
  13.2 0.0 collective-permute-done.4.ppair
  13.2 0.0 slice-start.1
  13.2 0.3 gather_proj.1.pall
  13.5 1.3 %collective-permute-done.3.xb = bf16[128,1280]{1,0:T(8,128)(2,1)S(1)} collective-permute-done((bf16[128,1280]{1,0:T(8,128)(2,1)S(1)}, bf16[128,1280]{1,0:T(8,128)(2,1)S(1)}, u32[]{:S(2)}, u32[]{:S(2)}) %collective-permute-start.3) | collective-permute-done | bytes 327712 | tf_op jit(solution)/shard_map/ppermute | solution.py:317
  14.8 0.0 slice-start.2
  14.8 2.0 %far.1 = (f32[128,1280]{1,0:T(8,128)S(1)}, bf16[128,1280]{1,0:T(8,128)(2,1)S(1)}, bf16[640,256]{1,0:T(8,128)(2,1)S(1)}, bf16[640,256]{1,0:T(8,128)(2,1)S(1)}) custom-call(bf16[128,1280]{1,0:T(8,128)(2,1)S(1)} %shard_map.134.after.xa.x, bf16[128,1280]{1,0:T(8,128)(2,1)S(1)} %collective-permute-done.3.xb, bf16[960,1280]{1,0:T(8,128)(2,1)S(1)} %get-tuple-element.38.weight.wown, ...), custom_call_target="tpu_custom_call" | custom-call | flops 1258291200 | bytes 4194304 | tf_op jit(solution)/shard_map/far/pallas_call | solution.py:391
  16.8 1.8 %collective-permute-start.6 = (bf16[128,1280]{1,0:T(8,128)(2,1)S(1)}, bf16[128,1280]{1,0:T(8,128)(2,1)S(1)}, u32[]{:S(2)}, u32[]{:S(2)}) collective-permute-start(bf16[128,1280]{1,0:T(8,128)(2,1)S(1)} %get-tuple-element.60), channel_id=1, source_target_pairs={{0,2},{1,3},{2,0},{3,1},{4,6},{5,7},{6,4},{7,5},{8,10},{9,11},{10,... | collective-permute-start | bytes 983048 | tf_op jit(solution)/shard_map/ppermute | solution.py:317
  18.6 0.0 slice-start.3
  18.6 3.1 %shard_map.135 = (f32[128,1280]{1,0:T(8,128)S(1)}, bf16[96,1280]{1,0:T(8,128)(2,1)S(1)}, bf16[32,1280]{1,0:T(8,128)(2,1)S(1)}) custom-call(bf16[128,1280]{1,0:T(8,128)(2,1)S(1)} %shard_map.134.after.xa.x, bf16[960,1280]{1,0:T(8,128)(2,1)S(1)} %get-tuple-element.38.weight.wown, bf16[960,1280]{1,0:T(8,128)(2,1)S(1)} %collective-permute-done.2.weight.wpair, ...), custom_call_target="tpu_custom_call" | custom-call | flops 1258291200 | bytes 1048576 | tf_op jit(solution)/shard_map/pallas_call | solution.py:406
  21.7 4.9 %collective-permute-done.6.got = bf16[128,1280]{1,0:T(8,128)(2,1)S(1)} collective-permute-done((bf16[128,1280]{1,0:T(8,128)(2,1)S(1)}, bf16[128,1280]{1,0:T(8,128)(2,1)S(1)}, u32[]{:S(2)}, u32[]{:S(2)}) %collective-permute-start.6) | collective-permute-done | bytes 327712 | tf_op jit(solution)/shard_map/ppermute | solution.py:317
  26.7 0.4 shard_map.137.own
  27.1 0.1 collective-permute-start.7
  27.2 1.8 %collective-permute-start.5 = (bf16[96,1280]{1,0:T(8,128)(2,1)S(1)}, bf16[96,1280]{1,0:T(8,128)(2,1)S(1)}, u32[]{:S(2)}, u32[]{:S(2)}) collective-permute-start(bf16[96,1280]{1,0:T(8,128)(2,1)S(1)} %get-tuple-element.58), channel_id=1, source_target_pairs={{0,2},{1,3},{2,0},{3,1},{4,6},{5,7},{6,4},{7,5},{8,10},{9,11},{10,... | collective-permute-start | bytes 737288 | tf_op jit(solution)/shard_map/ppermute | solution.py:317
  29.0 0.0 collective-permute-done.7.pair
  29.0 0.0 slice-done
  29.0 0.0 slice-done.1
  29.0 0.0 slice-done.2
  29.0 0.0 slice-done.3
  29.0 2.0 %shard_map.138.rest_0_.early = bf16[64,1280]{1,0:T(8,128)(2,1)S(1)} custom-call(bf16[32,5120]{1,0:T(8,128)(2,1)S(1)} %shard_map.137.own, bf16[32,5120]{1,0:T(8,128)(2,1)S(1)} %collective-permute-done.7.pair, bf16[5120,1280]{1,0:T(8,128)(2,1)S(1)} %bitcast.4, f32[8,1280]{1,0:T(8,128)S(1)} %get-tuple-element.36.rows.x), custom_call_target="tpu_custom_call" | custom-call | flops 838860800 | bytes 1048576 | tf_op jit(solution)/shard_map/pallas_call | solution.py:429
  31.0 4.6 %collective-permute-done.5.got = bf16[96,1280]{1,0:T(8,128)(2,1)S(1)} collective-permute-done((bf16[96,1280]{1,0:T(8,128)(2,1)S(1)}, bf16[96,1280]{1,0:T(8,128)(2,1)S(1)}, u32[]{:S(2)}, u32[]{:S(2)}) %collective-permute-start.5) | collective-permute-done | bytes 245792 | tf_op jit(solution)/shard_map/ppermute | solution.py:317
  35.5 0.4 shard_map.139
  35.9 0.1 collective-permute-start.9
  36.0 1.8 %collective-permute-start.8 = (bf16[32,1280]{1,0:T(8,128)(2,1)S(1)}, bf16[32,1280]{1,0:T(8,128)(2,1)S(1)}, u32[]{:S(2)}, u32[]{:S(2)}) collective-permute-start(bf16[32,1280]{1,0:T(8,128)(2,1)S(1)} %get-tuple-element.62), channel_id=1, source_target_pairs={{0,2},{1,3},{2,0},{3,1},{4,6},{5,7},{6,4},{7,5},{8,10},{9,11},{10,... | collective-permute-start | bytes 245768 | tf_op jit(solution)/shard_map/ppermute | solution.py:317
  37.8 3.1 %collective-permute-done.8.got = bf16[32,1280]{1,0:T(8,128)(2,1)S(1)} collective-permute-done((bf16[32,1280]{1,0:T(8,128)(2,1)S(1)}, bf16[32,1280]{1,0:T(8,128)(2,1)S(1)}, u32[]{:S(2)}, u32[]{:S(2)}) %collective-permute-start.8) | collective-permute-done | bytes 81952 | tf_op jit(solution)/shard_map/ppermute | solution.py:317
  40.8 0.3 shard_map.141
  41.1 0.1 collective-permute-start.10
  41.2 1.3 %collective-permute-done.10.pair1 = bf16[8,5120]{1,0:T(8,128)(2,1)S(1)} collective-permute-done((bf16[8,5120]{1,0:T(8,128)(2,1)S(1)}, bf16[8,5120]{1,0:T(8,128)(2,1)S(1)}, u32[]{:S(2)}, u32[]{:S(2)}) %collective-permute-start.10) | collective-permute-done | bytes 81952 | tf_op jit(solution)/shard_map/ppermute | solution.py:317
  42.4 0.0 collective-permute-done.9.pair0
  42.4 2.7 %hidden0.1 = (bf16[128,1280]{1,0:T(8,128)(2,1)}, bf16[128,1280]{1,0:T(8,128)(2,1)}) custom-call(bf16[24,5120]{1,0:T(8,128)(2,1)S(1)} %get-tuple-element.61.own0, bf16[8,5120]{1,0:T(8,128)(2,1)S(1)} %get-tuple-element.63.own1, bf16[24,5120]{1,0:T(8,128)(2,1)S(1)} %collective-permute-done.9.pair0, bf16[8,5120]{1,0:T(8,128)(2,1)S(1)} %collective-permute-done.10.pair1, ...), custom_call_target="tpu_custom_call" | custom-call | flops 838860800 | bytes 16777216 | tf_op jit(solution)/shard_map/hidden0/pallas_call | solution.py:436
  (3 shorter events, 0.0 us)
Async XLA Ops:
  0.6 8.5 %collective-permute-start.2 = (bf16[960,1280]{1,0:T(8,128)(2,1)}, bf16[960,1280]{1,0:T(8,128)(2,1)S(1)}, u32[]{:S(2)}, u32[]{:S(2)}) collective-permute-start(bf16[960,1280]{1,0:T(8,128)(2,1)} %bitcast.5), channel_id=1, source_target_pairs={{0,1},{1,0},{2,3},{3,2},{4,5},{5,4},{6,7},{7,6},{8,9},{9,8},{10,11... | collective-permute-start | bytes 7372808 | tf_op jit(solution)/shard_map/ppermute | solution.py:317
  1.2 12.0 %collective-permute-start.4 = (bf16[320,1280]{1,0:T(8,128)(2,1)}, bf16[320,1280]{1,0:T(8,128)(2,1)S(1)}, u32[]{:S(2)}, u32[]{:S(2)}) collective-permute-start(bf16[320,1280]{1,0:T(8,128)(2,1)} %refs_9_.1), channel_id=1, source_target_pairs={{0,1},{1,0},{2,3},{3,2},{4,5},{5,4},{6,7},{7,6},{8,9},{9,8},{10,11... | collective-permute-start | bytes 2457608 | tf_op jit(solution)/shard_map/ppermute | solution.py:317
  1.3 6.1 %collective-permute-start.1 = (bf16[128,1280]{1,0:T(8,128)(2,1)}, bf16[128,1280]{1,0:T(8,128)(2,1)S(1)}, u32[]{:S(2)}, u32[]{:S(2)}) collective-permute-start(bf16[128,1280]{1,0:T(8,128)(2,1)} %refs_0_.1), channel_id=1, source_target_pairs={{0,1},{1,0},{2,3},{3,2},{4,5},{5,4},{6,7},{7,6},{8,9},{9,8},{10,11... | collective-permute-start | bytes 983048 | tf_op jit(solution)/shard_map/ppermute | solution.py:317
  1.7 11.1 %collective-permute-start = (bf16[128,1280]{1,0:T(8,128)(2,1)}, bf16[128,1280]{1,0:T(8,128)(2,1)S(1)}, u32[]{:S(2)}, u32[]{:S(2)}) collective-permute-start(bf16[128,1280]{1,0:T(8,128)(2,1)} %refs_0_.1), channel_id=1, source_target_pairs={{0,2},{1,3},{2,0},{3,1},{4,6},{5,7},{6,4},{7,5},{8,10},{9,11},{10,... | collective-permute-start | bytes 983048 | tf_op jit(solution)/shard_map/ppermute | solution.py:317
  9.2 19.8 %slice-start = ((s8[13107200]{0:T(1024)(128)(4,1)}), s8[524288]{0:T(1024)(128)(4,1)S(1)}, s32[]{:S(2)}) async-start(s8[13107200]{0:T(1024)(128)(4,1)} %bitcast.3), calls=%async_computation | async-start | bytes 1048576
  13.1 1.7 %collective-permute-start.3 = (bf16[128,1280]{1,0:T(8,128)(2,1)S(1)}, bf16[128,1280]{1,0:T(8,128)(2,1)S(1)}, u32[]{:S(2)}, u32[]{:S(2)}) collective-permute-start(bf16[128,1280]{1,0:T(8,128)(2,1)S(1)} %shard_map.134.after.xa.x), channel_id=1, source_target_pairs={{0,1},{1,0},{2,3},{3,2},{4,5},{5,4},{6,7},{7,6},{8,9},{9,8},{10,11... | collective-permute-start | bytes 983048 | tf_op jit(solution)/shard_map/ppermute | solution.py:317
  13.2 15.8 %slice-start.1 = ((s8[13107200]{0:T(1024)(128)(4,1)}), s8[4194304]{0:T(1024)(128)(4,1)S(1)}, s32[]{:S(2)}) async-start(s8[13107200]{0:T(1024)(128)(4,1)} %bitcast.3), calls=%async_computation.1 | async-start | bytes 8388608
  14.8 14.2 %slice-start.2 = ((s8[13107200]{0:T(1024)(128)(4,1)}), s8[4194304]{0:T(1024)(128)(4,1)S(1)}, s32[]{:S(2)}) async-start(s8[13107200]{0:T(1024)(128)(4,1)} %bitcast.3), calls=%async_computation.2 | async-start | bytes 8388608
  16.8 9.8 %collective-permute-start.6 = (bf16[128,1280]{1,0:T(8,128)(2,1)S(1)}, bf16[128,1280]{1,0:T(8,128)(2,1)S(1)}, u32[]{:S(2)}, u32[]{:S(2)}) collective-permute-start(bf16[128,1280]{1,0:T(8,128)(2,1)S(1)} %get-tuple-element.60), channel_id=1, source_target_pairs={{0,2},{1,3},{2,0},{3,1},{4,6},{5,7},{6,4},{7,5},{8,10},{9,11},{10,... | collective-permute-start | bytes 983048 | tf_op jit(solution)/shard_map/ppermute | solution.py:317
  18.6 10.4 %slice-start.3 = ((s8[13107200]{0:T(1024)(128)(4,1)}), s8[4194304]{0:T(1024)(128)(4,1)S(1)}, s32[]{:S(2)}) async-start(s8[13107200]{0:T(1024)(128)(4,1)} %bitcast.3), calls=%async_computation.3 | async-start | bytes 8388608
  27.1 1.9 %collective-permute-start.7 = (bf16[32,5120]{1,0:T(8,128)(2,1)S(1)}, bf16[32,5120]{1,0:T(8,128)(2,1)S(1)}, u32[]{:S(2)}, u32[]{:S(2)}) collective-permute-start(bf16[32,5120]{1,0:T(8,128)(2,1)S(1)} %shard_map.137.own), channel_id=1, source_target_pairs={{0,1},{1,0},{2,3},{3,2},{4,5},{5,4},{6,7},{7,6},{8,9},{9,8},{10,11... | collective-permute-start | bytes 983048 | tf_op jit(solution)/shard_map/ppermute | solution.py:317
  27.2 8.4 %collective-permute-start.5 = (bf16[96,1280]{1,0:T(8,128)(2,1)S(1)}, bf16[96,1280]{1,0:T(8,128)(2,1)S(1)}, u32[]{:S(2)}, u32[]{:S(2)}) collective-permute-start(bf16[96,1280]{1,0:T(8,128)(2,1)S(1)} %get-tuple-element.58), channel_id=1, source_target_pairs={{0,2},{1,3},{2,0},{3,1},{4,6},{5,7},{6,4},{7,5},{8,10},{9,11},{10,... | collective-permute-start | bytes 737288 | tf_op jit(solution)/shard_map/ppermute | solution.py:317
  35.9 6.5 %collective-permute-start.9 = (bf16[24,5120]{1,0:T(8,128)(2,1)S(1)}, bf16[24,5120]{1,0:T(8,128)(2,1)S(1)}, u32[]{:S(2)}, u32[]{:S(2)}) collective-permute-start(bf16[24,5120]{1,0:T(8,128)(2,1)S(1)} %get-tuple-element.61.own0), channel_id=1, source_target_pairs={{0,1},{1,0},{2,3},{3,2},{4,5},{5,4},{6,7},{7,6},{8,9},{9,8},{10,11... | collective-permute-start | bytes 737288 | tf_op jit(solution)/shard_map/ppermute | solution.py:317
  36.0 4.8 %collective-permute-start.8 = (bf16[32,1280]{1,0:T(8,128)(2,1)S(1)}, bf16[32,1280]{1,0:T(8,128)(2,1)S(1)}, u32[]{:S(2)}, u32[]{:S(2)}) collective-permute-start(bf16[32,1280]{1,0:T(8,128)(2,1)S(1)} %get-tuple-element.62), channel_id=1, source_target_pairs={{0,2},{1,3},{2,0},{3,1},{4,6},{5,7},{6,4},{7,5},{8,10},{9,11},{10,... | collective-permute-start | bytes 245768 | tf_op jit(solution)/shard_map/ppermute | solution.py:317
  41.1 1.3 %collective-permute-start.10 = (bf16[8,5120]{1,0:T(8,128)(2,1)S(1)}, bf16[8,5120]{1,0:T(8,128)(2,1)S(1)}, u32[]{:S(2)}, u32[]{:S(2)}) collective-permute-start(bf16[8,5120]{1,0:T(8,128)(2,1)S(1)} %get-tuple-element.63.own1), channel_id=1, source_target_pairs={{0,1},{1,0},{2,3},{3,2},{4,5},{5,4},{6,7},{7,6},{8,9},{9,8},{10,11... | collective-permute-start | bytes 245768 | tf_op jit(solution)/shard_map/ppermute | solution.py:317

commit v8 on v7

--- a/solution.py
+++ b/solution.py
@@ -204,7 +204,7 @@
     pieces = []
     for side, weight in enumerate((wown, wpair)):
         query = dot(weight[:local, :], x[...], NT) + column(qcol, me ^ side, local, 0)
-        far = slice(2 * rows, 3 * rows)
+        far = slice(3 * rows, 4 * rows)
         query = paired(rotated(query, cosine[:, far], sine[:, far], hdim), hdim)
         for at in range(0, local, 2 * hdim):
             f = slice(side * local + at, side * local + at + 2 * hdim)
@@ -254,7 +254,7 @@
     count = own.shape[0]
     both = jnp.concatenate([own[...], pair[...]] * 2, axis=0)
     hid = gelu(dot(both, weight[...], NN)[: 2 * count] + rows[5:6, :]).astype(jnp.bfloat16)
-    for half, place in enumerate((core, 1 - core)):
+    for half, place in enumerate((1 - core, core)):
         out[pl.ds(pl.multiple_of(place * count, count), count), :] = hid[half * count : (half + 1) * count]
 
 
@@ -374,6 +374,7 @@
 
     n_far = norm(x_far, 0, prow, early_own[1], early_pair[1])
     n_farpair = swap(n_far, 1)
+    x_cross = swap(x_far, 1)
     p_all = pl.pallas_call(
         gather_kernel,
         out_shape=pltpu.VMEM((both, width), proj_weight.dtype),
@@ -400,14 +401,14 @@
         cost_estimate=pl.CostEstimate(flops=6 * mul, bytes_accessed=1 << 22, transcendentals=0),
         name="far",
     )(n_far, n_farpair, *shared, *early_own, *early_pair)
-    got1 = swap(send0, 2)
+    got1 = swap(send0, 3)
     cut = prow * 3 // 4
     halves = (shape((cut, width)), shape((prow - cut, width)))
     part1, send1a, send1b = call(
         functools.partial(late_kernel, hdim), (part_shape,) + halves, 8 * MIB, 6 * mul
-    )(n_far, *shared, *kv_own, *kv_pair, k_far, v_far)
-    got0a = swap(send1a, 2)
-    got0b = swap(send1b, 2)
+    )(n_farpair, *shared, *kv_own, *kv_pair, k_far, v_far)
+    got0a = swap(send1a, 3)
+    got0b = swap(send1b, 3)
     late_rows = call(copy_kernel, shape(rows.shape, rows.dtype), MIB, 1000)(rows)
 
     def merge(keep, start, x, part, got, late_rows, *after):
@@ -423,7 +424,7 @@
         )(x, part, got, late_rows, *after)
 
     fc1 = pltpu.with_memory_space_constraint(fc1_weight, pltpu.VMEM)
-    (blocks1,) = merge(0, 0, x_far, part1, got1, late_rows)
+    (blocks1,) = merge(0, 0, x_cross, part1, got1, late_rows)
     pair1 = swap(blocks1, 1)
     flops = prow * 4 * width * hidden
     early = call(hidden_kernel, shape((prow // 2, hidden)), 4 * MIB, flops)(blocks1, pair1, fc1, rows)

time: 45.5 us -> 44.8 us (0.985)
  waiting for transfers between devices: 18 us -> 17 us
  starting transfers between devices: 9.3 us -> 9.77 us
    ppermute x11 -> x12, waiting for transfers between devices: 18 us -> 17 us  [swap(): return lax.ppermute(value, 'sp', [(i, i ^ bit) for i in range(4)])]
    ppermute x11 -> x12, starting transfers between devices: 9.3 us -> 9.77 us  [swap(): return lax.ppermute(value, 'sp', [(i, i ^ bit) for i in range(4)])]
  transfers between devices with their start and end apart: 11 -> 12, of which waited for: 7 -> 7; matrix products, arithmetic and copies ran while one was open for 0% -> 0% of each run, Pallas kernels for 25% -> 30%
where the time goes in v8:
time: 44.8 us; the launch traced here: 44.6 us
  waiting for transfers between devices  17 us (38%)
  Pallas kernels  16.9 us (38%)
  starting transfers between devices  9.77 us (22%)
  between operations  0.95 us (2%)
    ppermute x12, waiting for transfers between devices, swap(): return lax.ppermute(value, 'sp', [(i, i ^ bit) for i in range(4)])  17 us
    ppermute x12, starting transfers between devices, swap(): return lax.ppermute(value, 'sp', [(i, i ^ bit) for i in range(4)])  9.77 us
    pallas_call x1, Pallas kernels, two_chips(): call(functools.partial(late_kernel, hdim), (part_shape,) + halves, 8 * MI...  3.07 us
    pallas_call x2, Pallas kernels, near(): call(functools.partial(near_kernel, hdim, side), near_shape, 8 * MIB, 4 *...  3.05 us
    pallas_call x1, Pallas kernels, two_chips(): pl.pallas_call(last_kernel, out_shape=(shape((prow, hidden)), shape((prow...  2.7 us
    pallas_call x1, Pallas kernels, two_chips(): pl.pallas_call(functools.partial(setup_kernel, hdim, len(sources)), out_s...  2.27 us
    pallas_call x1, Pallas kernels, two_chips(): pl.pallas_call(functools.partial(far_kernel, hdim), out_shape=(part_shape...  2.05 us
    pallas_call x1, Pallas kernels, two_chips(): call(hidden_kernel, shape((prow // 2, hidden)), 4 * MIB, flops)  1.96 us
  transfers between devices with their start and end apart: 12, of which 7 were waited for; matrix products, arithmetic and copies ran while one was open for 0% of the time, Pallas kernels for 30%

profile of v8, /device:TPU:0, one launch (start us, length us, event | category | flops | bytes accessed | tf_op | source)
XLA Modules:
  0.0 44.6 jit_solution(16037581560093135275)
XLA Ops:
  0.6 0.6 %collective-permute-start.2 = (bf16[960,1280]{1,0:T(8,128)(2,1)}, bf16[960,1280]{1,0:T(8,128)(2,1)S(1)}, u32[]{:S(2)}, u32[]{:S(2)}) collective-permute-start(bf16[960,1280]{1,0:T(8,128)(2,1)} %bitcast.5), channel_id=1, source_target_pairs={{0,1},{1,0},{2,3},{3,2},{4,5},{5,4},{6,7},{7,6},{8,9},{9,8},{10,11... | collective-permute-start | bytes 7372808 | tf_op jit(solution)/shard_map/ppermute | solution.py:317
  1.2 0.1 collective-permute-start.4
  1.3 0.4 collective-permute-start.1
  1.7 2.6 %collective-permute-start = (bf16[128,1280]{1,0:T(8,128)(2,1)}, bf16[128,1280]{1,0:T(8,128)(2,1)S(1)}, u32[]{:S(2)}, u32[]{:S(2)}) collective-permute-start(bf16[128,1280]{1,0:T(8,128)(2,1)} %refs_0_.1), channel_id=1, source_target_pairs={{0,2},{1,3},{2,0},{3,1},{4,6},{5,7},{6,4},{7,5},{8,10},{9,11},{10,... | collective-permute-start | bytes 983048 | tf_op jit(solution)/shard_map/ppermute | solution.py:317
  4.3 2.3 %setup.1 = (bf16[128,1280]{1,0:T(8,128)(2,1)S(1)}, bf16[960,1280]{1,0:T(8,128)(2,1)S(1)}, bf16[640,1280]{1,0:T(8,128)(2,1)S(1)}, bf16[128,1280]{1,0:T(8,128)(2,1...) custom-call(bf16[128,1280]{1,0:T(8,128)(2,1)} %refs_0_.1, ...), custom_call_target="tpu_custom_call" | custom-call | flops 209715200 | bytes 4194304 | tf_op jit(solution)/shard_map/setup/pallas_call | solution.py:332
  6.5 0.8 %collective-permute-done.1.x = bf16[128,1280]{1,0:T(8,128)(2,1)S(1)} collective-permute-done((bf16[128,1280]{1,0:T(8,128)(2,1)}, bf16[128,1280]{1,0:T(8,128)(2,1)S(1)}, u32[]{:S(2)}, u32[]{:S(2)}) %collective-permute-start.1) | collective-permute-done | bytes 327712 | tf_op jit(solution)/shard_map/ppermute | solution.py:317
  7.3 0.3 shard_map.131.xb
  7.6 1.5 %shard_map.132 = (bf16[320,256]{1,0:T(8,128)(2,1)S(1)}, bf16[320,256]{1,0:T(8,128)(2,1)S(1)}, bf16[320,256]{1,0:T(8,128)(2,1)S(1)}, f32[2,256]{1,0:T(2,128)S(1)}...) custom-call(bf16[128,1280]{1,0:T(8,128)(2,1)S(1)} %get-tuple-element.37.xa, bf16[128,1280]{1,0:T(8,128)(2,1)S(1)} %shard_map.131.xb, ...), custom_call_target="tpu_custom_call" | custom-call | flops 838860800 | bytes 1048576 | tf_op jit(solution)/shard_map/pallas_call | solution.py:366
  9.2 0.0 collective-permute-done.2.weight.wpair
  9.2 0.0 slice-start
  9.2 1.5 %shard_map.133 = (bf16[320,256]{1,0:T(8,128)(2,1)S(1)}, bf16[320,256]{1,0:T(8,128)(2,1)S(1)}, bf16[320,256]{1,0:T(8,128)(2,1)S(1)}, f32[2,256]{1,0:T(2,128)S(1)}...) custom-call(bf16[128,1280]{1,0:T(8,128)(2,1)S(1)} %get-tuple-element.37.xa, bf16[128,1280]{1,0:T(8,128)(2,1)S(1)} %shard_map.131.xb, ...), custom_call_target="tpu_custom_call" | custom-call | flops 838860800 | bytes 1048576 | tf_op jit(solution)/shard_map/pallas_call | solution.py:366
  10.7 2.0 %collective-permute-done.x = bf16[128,1280]{1,0:T(8,128)(2,1)S(1)} collective-permute-done((bf16[128,1280]{1,0:T(8,128)(2,1)}, bf16[128,1280]{1,0:T(8,128)(2,1)S(1)}, u32[]{:S(2)}, u32[]{:S(2)}) %collective-permute-start) | collective-permute-done | bytes 327712 | tf_op jit(solution)/shard_map/ppermute | solution.py:317
  12.8 0.3 shard_map.134.after.xa
  13.1 0.1 collective-permute-start.3
  13.2 0.5 %collective-permute-start.6 = (bf16[128,1280]{1,0:T(8,128)(2,1)S(1)}, bf16[128,1280]{1,0:T(8,128)(2,1)S(1)}, u32[]{:S(2)}, u32[]{:S(2)}) collective-permute-start(bf16[128,1280]{1,0:T(8,128)(2,1)S(1)} %collective-permute-done.x), channel_id=1, source_target_pairs={{0,1},{1,0},{2,3},{3,2},{4,5},{5,4},{6,7},{7,6},{8,9},{9,8},{10,11... | collective-permute-start | bytes 983048 | tf_op jit(solution)/shard_map/ppermute | solution.py:317
  13.6 0.0 collective-permute-done.4.ppair
  13.7 0.0 slice-start.1
  13.7 0.1 gather_proj.1.pall
  13.8 1.0 %collective-permute-done.3.xb.x = bf16[128,1280]{1,0:T(8,128)(2,1)S(1)} collective-permute-done((bf16[128,1280]{1,0:T(8,128)(2,1)S(1)}, bf16[128,1280]{1,0:T(8,128)(2,1)S(1)}, u32[]{:S(2)}, u32[]{:S(2)}) %collective-permute-start.3) | collective-permute-done | bytes 327712 | tf_op jit(solution)/shard_map/ppermute | solution.py:317
  14.8 0.0 slice-start.2
  14.8 2.1 %far.1 = (f32[128,1280]{1,0:T(8,128)S(1)}, bf16[128,1280]{1,0:T(8,128)(2,1)S(1)}, bf16[640,256]{1,0:T(8,128)(2,1)S(1)}, bf16[640,256]{1,0:T(8,128)(2,1)S(1)}) custom-call(bf16[128,1280]{1,0:T(8,128)(2,1)S(1)} %shard_map.134.after.xa, bf16[128,1280]{1,0:T(8,128)(2,1)S(1)} %collective-permute-done.3.xb.x, bf16[960,1280]{1,0:T(8,128)(2,1)S(1)} %get-tuple-element.38.weight.wown, ...), custom_call_target="tpu_custom_call" | custom-call | flops 1258291200 | bytes 4194304 | tf_op jit(solution)/shard_map/far/pallas_call | solution.py:392
  16.8 1.5 %collective-permute-start.7 = (bf16[128,1280]{1,0:T(8,128)(2,1)S(1)}, bf16[128,1280]{1,0:T(8,128)(2,1)S(1)}, u32[]{:S(2)}, u32[]{:S(2)}) collective-permute-start(bf16[128,1280]{1,0:T(8,128)(2,1)S(1)} %get-tuple-element.60), channel_id=1, source_target_pairs={{0,3},{1,2},{2,1},{3,0},{4,7},{5,6},{6,5},{7,4},{8,11},{9,10},{10,... | collective-permute-start | bytes 983048 | tf_op jit(solution)/shard_map/ppermute | solution.py:317
  18.4 0.0 slice-start.3
  18.4 3.1 %shard_map.135 = (f32[128,1280]{1,0:T(8,128)S(1)}, bf16[96,1280]{1,0:T(8,128)(2,1)S(1)}, bf16[32,1280]{1,0:T(8,128)(2,1)S(1)}) custom-call(bf16[128,1280]{1,0:T(8,128)(2,1)S(1)} %collective-permute-done.3.xb.x, bf16[960,1280]{1,0:T(8,128)(2,1)S(1)} %get-tuple-element.38.weight.wown, bf16[960,1280]{1,0:T(8,128)(2,1)S(1)} %collective-permute-done.2.weight.wpair, ...), custom_call_target="tpu_custom_call" | custom-call | flops 1258291200 | bytes 1048576 | tf_op jit(solution)/shard_map/pallas_call | solution.py:407
  21.5 0.0 collective-permute-done.6.x
  21.5 5.1 %collective-permute-done.7.got = bf16[128,1280]{1,0:T(8,128)(2,1)S(1)} collective-permute-done((bf16[128,1280]{1,0:T(8,128)(2,1)S(1)}, bf16[128,1280]{1,0:T(8,128)(2,1)S(1)}, u32[]{:S(2)}, u32[]{:S(2)}) %collective-permute-start.7) | collective-permute-done | bytes 327712 | tf_op jit(solution)/shard_map/ppermute | solution.py:317
  26.6 0.4 shard_map.137.own
  27.0 0.2 collective-permute-start.8
  27.2 1.7 %collective-permute-start.5 = (bf16[96,1280]{1,0:T(8,128)(2,1)S(1)}, bf16[96,1280]{1,0:T(8,128)(2,1)S(1)}, u32[]{:S(2)}, u32[]{:S(2)}) collective-permute-start(bf16[96,1280]{1,0:T(8,128)(2,1)S(1)} %get-tuple-element.58), channel_id=1, source_target_pairs={{0,3},{1,2},{2,1},{3,0},{4,7},{5,6},{6,5},{7,4},{8,11},{9,10},{10,... | collective-permute-start | bytes 737288 | tf_op jit(solution)/shard_map/ppermute | solution.py:317
  28.9 0.0 collective-permute-done.8.pair
  28.9 0.0 slice-done
  28.9 0.0 slice-done.1
  28.9 0.0 slice-done.2
  28.9 0.0 slice-done.3
  29.0 2.0 %shard_map.138.rest_0_.early = bf16[64,1280]{1,0:T(8,128)(2,1)S(1)} custom-call(bf16[32,5120]{1,0:T(8,128)(2,1)S(1)} %shard_map.137.own, bf16[32,5120]{1,0:T(8,128)(2,1)S(1)} %collective-permute-done.8.pair, bf16[5120,1280]{1,0:T(8,128)(2,1)S(1)} %bitcast.4, f32[8,1280]{1,0:T(8,128)S(1)} %get-tuple-element.36.rows.x), custom_call_target="tpu_custom_call" | custom-call | flops 838860800 | bytes 1048576 | tf_op jit(solution)/shard_map/pallas_call | solution.py:430
  30.9 4.0 %collective-permute-done.5.got = bf16[96,1280]{1,0:T(8,128)(2,1)S(1)} collective-permute-done((bf16[96,1280]{1,0:T(8,128)(2,1)S(1)}, bf16[96,1280]{1,0:T(8,128)(2,1)S(1)}, u32[]{:S(2)}, u32[]{:S(2)}) %collective-permute-start.5) | collective-permute-done | bytes 245792 | tf_op jit(solution)/shard_map/ppermute | solution.py:317
  34.9 0.4 shard_map.139
  35.3 0.4 collective-permute-start.10
  35.7 1.5 %collective-permute-start.9 = (bf16[32,1280]{1,0:T(8,128)(2,1)S(1)}, bf16[32,1280]{1,0:T(8,128)(2,1)S(1)}, u32[]{:S(2)}, u32[]{:S(2)}) collective-permute-start(bf16[32,1280]{1,0:T(8,128)(2,1)S(1)} %get-tuple-element.62), channel_id=1, source_target_pairs={{0,3},{1,2},{2,1},{3,0},{4,7},{5,6},{6,5},{7,4},{8,11},{9,10},{10,... | collective-permute-start | bytes 245768 | tf_op jit(solution)/shard_map/ppermute | solution.py:317
  37.2 2.9 %collective-permute-done.9.got = bf16[32,1280]{1,0:T(8,128)(2,1)S(1)} collective-permute-done((bf16[32,1280]{1,0:T(8,128)(2,1)S(1)}, bf16[32,1280]{1,0:T(8,128)(2,1)S(1)}, u32[]{:S(2)}, u32[]{:S(2)}) %collective-permute-start.9) | collective-permute-done | bytes 81952 | tf_op jit(solution)/shard_map/ppermute | solution.py:317
  40.2 0.3 shard_map.141
  40.4 0.2 collective-permute-start.11
  40.6 1.1 %collective-permute-done.11.pair1 = bf16[8,5120]{1,0:T(8,128)(2,1)S(1)} collective-permute-done((bf16[8,5120]{1,0:T(8,128)(2,1)S(1)}, bf16[8,5120]{1,0:T(8,128)(2,1)S(1)}, u32[]{:S(2)}, u32[]{:S(2)}) %collective-permute-start.11) | collective-permute-done | bytes 81952 | tf_op jit(solution)/shard_map/ppermute | solution.py:317
  41.8 0.0 collective-permute-done.10.pair0
  41.8 2.7 %hidden0.1 = (bf16[128,1280]{1,0:T(8,128)(2,1)}, bf16[128,1280]{1,0:T(8,128)(2,1)}) custom-call(bf16[24,5120]{1,0:T(8,128)(2,1)S(1)} %get-tuple-element.61.own0, bf16[8,5120]{1,0:T(8,128)(2,1)S(1)} %get-tuple-element.63.own1, bf16[24,5120]{1,0:T(8,128)(2,1)S(1)} %collective-permute-done.10.pair0, bf16[8,5120]{1,0:T(8,128)(2,1)S(1)} %collective-permute-done.11.pair1, ...), custom_call_target="tpu_custom_call" | custom-call | flops 838860800 | bytes 16777216 | tf_op jit(solution)/shard_map/hidden0/pallas_call | solution.py:437
  (3 shorter events, 0.0 us)
Async XLA Ops:
  0.6 8.5 %collective-permute-start.2 = (bf16[960,1280]{1,0:T(8,128)(2,1)}, bf16[960,1280]{1,0:T(8,128)(2,1)S(1)}, u32[]{:S(2)}, u32[]{:S(2)}) collective-permute-start(bf16[960,1280]{1,0:T(8,128)(2,1)} %bitcast.5), channel_id=1, source_target_pairs={{0,1},{1,0},{2,3},{3,2},{4,5},{5,4},{6,7},{7,6},{8,9},{9,8},{10,11... | collective-permute-start | bytes 7372808 | tf_op jit(solution)/shard_map/ppermute | solution.py:317
  1.2 12.5 %collective-permute-start.4 = (bf16[320,1280]{1,0:T(8,128)(2,1)}, bf16[320,1280]{1,0:T(8,128)(2,1)S(1)}, u32[]{:S(2)}, u32[]{:S(2)}) collective-permute-start(bf16[320,1280]{1,0:T(8,128)(2,1)} %refs_9_.1), channel_id=1, source_target_pairs={{0,1},{1,0},{2,3},{3,2},{4,5},{5,4},{6,7},{7,6},{8,9},{9,8},{10,11... | collective-permute-start | bytes 2457608 | tf_op jit(solution)/shard_map/ppermute | solution.py:317
  1.3 6.1 %collective-permute-start.1 = (bf16[128,1280]{1,0:T(8,128)(2,1)}, bf16[128,1280]{1,0:T(8,128)(2,1)S(1)}, u32[]{:S(2)}, u32[]{:S(2)}) collective-permute-start(bf16[128,1280]{1,0:T(8,128)(2,1)} %refs_0_.1), channel_id=1, source_target_pairs={{0,1},{1,0},{2,3},{3,2},{4,5},{5,4},{6,7},{7,6},{8,9},{9,8},{10,11... | collective-permute-start | bytes 983048 | tf_op jit(solution)/shard_map/ppermute | solution.py:317
  1.7 11.1 %collective-permute-start = (bf16[128,1280]{1,0:T(8,128)(2,1)}, bf16[128,1280]{1,0:T(8,128)(2,1)S(1)}, u32[]{:S(2)}, u32[]{:S(2)}) collective-permute-start(bf16[128,1280]{1,0:T(8,128)(2,1)} %refs_0_.1), channel_id=1, source_target_pairs={{0,2},{1,3},{2,0},{3,1},{4,6},{5,7},{6,4},{7,5},{8,10},{9,11},{10,... | collective-permute-start | bytes 983048 | tf_op jit(solution)/shard_map/ppermute | solution.py:317
  9.2 19.7 %slice-start = ((s8[13107200]{0:T(1024)(128)(4,1)}), s8[524288]{0:T(1024)(128)(4,1)S(1)}, s32[]{:S(2)}) async-start(s8[13107200]{0:T(1024)(128)(4,1)} %bitcast.3), calls=%async_computation | async-start | bytes 1048576
  13.1 1.7 %collective-permute-start.3 = (bf16[128,1280]{1,0:T(8,128)(2,1)S(1)}, bf16[128,1280]{1,0:T(8,128)(2,1)S(1)}, u32[]{:S(2)}, u32[]{:S(2)}) collective-permute-start(bf16[128,1280]{1,0:T(8,128)(2,1)S(1)} %shard_map.134.after.xa), channel_id=1, source_target_pairs={{0,1},{1,0},{2,3},{3,2},{4,5},{5,4},{6,7},{7,6},{8,9},{9,8},{10,11... | collective-permute-start | bytes 983048 | tf_op jit(solution)/shard_map/ppermute | solution.py:317
  13.2 8.3 %collective-permute-start.6 = (bf16[128,1280]{1,0:T(8,128)(2,1)S(1)}, bf16[128,1280]{1,0:T(8,128)(2,1)S(1)}, u32[]{:S(2)}, u32[]{:S(2)}) collective-permute-start(bf16[128,1280]{1,0:T(8,128)(2,1)S(1)} %collective-permute-done.x), channel_id=1, source_target_pairs={{0,1},{1,0},{2,3},{3,2},{4,5},{5,4},{6,7},{7,6},{8,9},{9,8},{10,11... | collective-permute-start | bytes 983048 | tf_op jit(solution)/shard_map/ppermute | solution.py:317
  13.7 15.3 %slice-start.1 = ((s8[13107200]{0:T(1024)(128)(4,1)}), s8[4194304]{0:T(1024)(128)(4,1)S(1)}, s32[]{:S(2)}) async-start(s8[13107200]{0:T(1024)(128)(4,1)} %bitcast.3), calls=%async_computation.1 | async-start | bytes 8388608
  14.8 14.2 %slice-start.2 = ((s8[13107200]{0:T(1024)(128)(4,1)}), s8[4194304]{0:T(1024)(128)(4,1)S(1)}, s32[]{:S(2)}) async-start(s8[13107200]{0:T(1024)(128)(4,1)} %bitcast.3), calls=%async_computation.2 | async-start | bytes 8388608
  16.8 9.7 %collective-permute-start.7 = (bf16[128,1280]{1,0:T(8,128)(2,1)S(1)}, bf16[128,1280]{1,0:T(8,128)(2,1)S(1)}, u32[]{:S(2)}, u32[]{:S(2)}) collective-permute-start(bf16[128,1280]{1,0:T(8,128)(2,1)S(1)} %get-tuple-element.60), channel_id=1, source_target_pairs={{0,3},{1,2},{2,1},{3,0},{4,7},{5,6},{6,5},{7,4},{8,11},{9,10},{10,... | collective-permute-start | bytes 983048 | tf_op jit(solution)/shard_map/ppermute | solution.py:317
  18.4 10.6 %slice-start.3 = ((s8[13107200]{0:T(1024)(128)(4,1)}), s8[4194304]{0:T(1024)(128)(4,1)S(1)}, s32[]{:S(2)}) async-start(s8[13107200]{0:T(1024)(128)(4,1)} %bitcast.3), calls=%async_computation.3 | async-start | bytes 8388608
  27.0 1.9 %collective-permute-start.8 = (bf16[32,5120]{1,0:T(8,128)(2,1)S(1)}, bf16[32,5120]{1,0:T(8,128)(2,1)S(1)}, u32[]{:S(2)}, u32[]{:S(2)}) collective-permute-start(bf16[32,5120]{1,0:T(8,128)(2,1)S(1)} %shard_map.137.own), channel_id=1, source_target_pairs={{0,1},{1,0},{2,3},{3,2},{4,5},{5,4},{6,7},{7,6},{8,9},{9,8},{10,11... | collective-permute-start | bytes 983048 | tf_op jit(solution)/shard_map/ppermute | solution.py:317
  27.2 7.7 %collective-permute-start.5 = (bf16[96,1280]{1,0:T(8,128)(2,1)S(1)}, bf16[96,1280]{1,0:T(8,128)(2,1)S(1)}, u32[]{:S(2)}, u32[]{:S(2)}) collective-permute-start(bf16[96,1280]{1,0:T(8,128)(2,1)S(1)} %get-tuple-element.58), channel_id=1, source_target_pairs={{0,3},{1,2},{2,1},{3,0},{4,7},{5,6},{6,5},{7,4},{8,11},{9,10},{10,... | collective-permute-start | bytes 737288 | tf_op jit(solution)/shard_map/ppermute | solution.py:317
  35.3 6.5 %collective-permute-start.10 = (bf16[24,5120]{1,0:T(8,128)(2,1)S(1)}, bf16[24,5120]{1,0:T(8,128)(2,1)S(1)}, u32[]{:S(2)}, u32[]{:S(2)}) collective-permute-start(bf16[24,5120]{1,0:T(8,128)(2,1)S(1)} %get-tuple-element.61.own0), channel_id=1, source_target_pairs={{0,1},{1,0},{2,3},{3,2},{4,5},{5,4},{6,7},{7,6},{8,9},{9,8},{10,11... | collective-permute-start | bytes 737288 | tf_op jit(solution)/shard_map/ppermute | solution.py:317
  35.7 4.4 %collective-permute-start.9 = (bf16[32,1280]{1,0:T(8,128)(2,1)S(1)}, bf16[32,1280]{1,0:T(8,128)(2,1)S(1)}, u32[]{:S(2)}, u32[]{:S(2)}) collective-permute-start(bf16[32,1280]{1,0:T(8,128)(2,1)S(1)} %get-tuple-element.62), channel_id=1, source_target_pairs={{0,3},{1,2},{2,1},{3,0},{4,7},{5,6},{6,5},{7,4},{8,11},{9,10},{10,... | collective-permute-start | bytes 245768 | tf_op jit(solution)/shard_map/ppermute | solution.py:317
  40.4 1.3 %collective-permute-start.11 = (bf16[8,5120]{1,0:T(8,128)(2,1)S(1)}, bf16[8,5120]{1,0:T(8,128)(2,1)S(1)}, u32[]{:S(2)}, u32[]{:S(2)}) collective-permute-start(bf16[8,5120]{1,0:T(8,128)(2,1)S(1)} %get-tuple-element.63.own1), channel_id=1, source_target_pairs={{0,1},{1,0},{2,3},{3,2},{4,5},{5,4},{6,7},{7,6},{8,9},{9,8},{10,11... | collective-permute-start | bytes 245768 | tf_op jit(solution)/shard_map/ppermute | solution.py:317
